TPU v7x, 32 devices: a 4x4x1 block of a 4x4x8 slice. The times are simulated.
32 devices in a mesh: dp: 1 (over z), ep: 32 (over y, x, core).
Axes of the slice: x: 4, y: 4, z: 1, core: 2. Of those that a mesh axis runs over, the one named last changes fastest.
The devices are a block of a 4x4x8 slice.
Arguments:
- h0: bfloat16 [32, 1024, 2048], P(('dp', 'ep'))
- idx: int32 [32, 1024, 6], P(('dp', 'ep'))
- slot: int32 [32, 1024, 6], P(('dp', 'ep'))
- ln_attn: bfloat16 [2048], replicated
- wq: bfloat16 [2048, 2048], replicated
- wk: bfloat16 [2048, 2048], replicated
- wv: bfloat16 [2048, 2048], replicated
- wo: bfloat16 [2048, 2048], replicated
- ln_ffn: bfloat16 [2048], replicated
- ws1: bfloat16 [2048, 2816], replicated
- ws3: bfloat16 [2048, 2816], replicated
- ws2: bfloat16 [2816, 2048], replicated
- ln_moe: bfloat16 [2048], replicated
- wr: bfloat16 [2048, 64], replicated
- ue1: bfloat16 [64, 2048, 1408], P('ep')
- ue3: bfloat16 [64, 2048, 1408], P('ep')
- ue2: bfloat16 [64, 1408, 2048], P('ep')
Outputs:
- output: bfloat16 [32, 1024, 2048], P(('dp', 'ep'))
All inputs are finite; a program needn't handle non-finite values.
Results may differ from a plain program's by a relative error of at most 0.0102654.
Values are sent between devices in bfloat16 or wider.
A program may use at most 768 MiB of HBM per device.

v0:
```python
import jax
import jax.numpy as jnp
from jax import lax
from jax.sharding import PartitionSpec as P

HEAD = 128
EPS = 1e-6
CAP_FACTOR = 2


def _mm(form, a, b):
    return jnp.einsum(form, a, b, preferred_element_type=jnp.float32)


def _rms(x, w):
    xf = x.astype(jnp.float32)
    r = lax.rsqrt(jnp.mean(xf * xf, axis=-1, keepdims=True) + EPS)
    return (xf * r * w.astype(jnp.float32)).astype(jnp.bfloat16)


def _rope(x):
    s, half = x.shape[1], x.shape[-1] // 2
    freq = 10000.0 ** (-jnp.arange(half, dtype=jnp.float32) / half)
    ang = jnp.arange(s, dtype=jnp.float32)[:, None] * freq[None, :]
    c = jnp.cos(ang)[None, :, None, :]
    sn = jnp.sin(ang)[None, :, None, :]
    x1, x2 = x[..., :half], x[..., half:]
    return jnp.concatenate([x1 * c - x2 * sn, x2 * c + x1 * sn], axis=-1)


def _dense(h0, ln_attn, wq, wk, wv, wo, ln_ffn, ws1, ws3, ws2):
    b, s, _ = h0.shape
    nh = wq.shape[1] // HEAD
    x1 = _rms(h0, ln_attn)
    q = _rope(_mm('bsd,de->bse', x1, wq).reshape(b, s, nh, HEAD)).astype(jnp.bfloat16)
    k = _rope(_mm('bsd,de->bse', x1, wk).reshape(b, s, nh, HEAD)).astype(jnp.bfloat16)
    v = _mm('bsd,de->bse', x1, wv).astype(jnp.bfloat16).reshape(b, s, nh, HEAD)
    sc = _mm('bqhe,bkhe->bhqk', q, k) * HEAD ** -0.5
    causal = jnp.arange(s)[:, None] >= jnp.arange(s)[None, :]
    p = jax.nn.softmax(jnp.where(causal, sc, -1e30), axis=-1).astype(jnp.bfloat16)
    o = _mm('bhqk,bkhe->bqhe', p, v).astype(jnp.bfloat16).reshape(b, s, nh * HEAD)
    a = (h0.astype(jnp.float32) + _mm('bse,ed->bsd', o, wo)).astype(jnp.bfloat16)
    x2 = _rms(a, ln_ffn)
    hs = (jax.nn.silu(_mm('bsd,df->bsf', x2, ws1)) * _mm('bsd,df->bsf', x2, ws3)).astype(jnp.bfloat16)
    return a, _mm('bsf,fd->bsd', hs, ws2)


def _experts(x, ue1, ue3, ue2):
    he = (jax.nn.silu(_mm('gecd,edf->egcf', x, ue1)) * _mm('gecd,edf->egcf', x, ue3)).astype(jnp.bfloat16)
    return _mm('egcf,efd->gecd', he, ue2).astype(jnp.bfloat16)


def _gate(u, wr, gi):
    lg = _mm('td,de->te', u, wr)
    hit = gi[..., None] == jnp.arange(wr.shape[1], dtype=gi.dtype)
    return jax.nn.softmax(jnp.sum(jnp.where(hit, lg[:, None, :], 0.0), axis=-1), axis=-1)


def _route(q, gate, n):
    hit = q[..., None] == jnp.arange(n, dtype=q.dtype)
    disp = jnp.any(hit, axis=-2).astype(jnp.bfloat16)
    comb = jnp.sum(jnp.where(hit, gate[..., None], 0.0), axis=-2)
    return disp, comb


def _parts(c):
    hi = c.astype(jnp.bfloat16)
    r = c - hi.astype(jnp.float32)
    mid = r.astype(jnp.bfloat16)
    lo = (r - mid.astype(jnp.float32)).astype(jnp.bfloat16)
    return hi, mid, lo


def solution(mesh):
    g_ = mesh.shape['ep']
    rows = P(('dp', 'ep'))
    rep = P()

    def local(h0, idx, slot, ln_attn, wq, wk, wv, wo, ln_ffn, ws1, ws3, ws2, ln_moe, wr, ue1, ue3, ue2):
        b, s, d = h0.shape
        top = idx.shape[-1]
        el = ue1.shape[0]
        ne = el * g_
        t = b * s
        cap = CAP_FACTOR * t * top // ne
        a, fo = _dense(h0, ln_attn, wq, wk, wv, wo, ln_ffn, ws1, ws3, ws2)
        u = _rms(h0, ln_moe).reshape(t, d)
        gi = idx.reshape(t, top)
        sl = slot.reshape(t, top)
        gate = _gate(u, wr, gi)
        disp, comb = _route(gi * cap + sl, gate, ne * cap)
        send = _mm('tr,td->rd', disp, u).astype(jnp.bfloat16).reshape(g_, el, cap, d)
        recv = lax.all_to_all(send, 'ep', 0, 0, tiled=True)
        y = _experts(recv, ue1, ue3, ue2)
        back = lax.all_to_all(y, 'ep', 0, 0, tiled=True).reshape(ne * cap, d)
        m = sum(_mm('tr,rd->td', p, back) for p in _parts(comb))
        out = a.astype(jnp.float32) + fo + m.reshape(b, s, d)
        return out.astype(jnp.bfloat16)

    specs = (rows, rows, rows) + (rep,) * 11 + (P('ep'), P('ep'), P('ep'))
    return jax.shard_map(local, mesh=mesh, in_specs=specs, out_specs=rows, check_vma=False)
```

profile of v0, /device:TPU:123, one launch (start us, length us, event | category | flops | bytes accessed | tf_op | source)
XLA Modules:
  0.0 2003.8 jit_solution(9395621477713068811)
XLA Ops:
  0.0 3.1 fusion.23
  3.2 0.8 bitcast_add_fusion
  4.5 64.1 %fusion.1 = pred[1024,12288]{1,0:T(32,128)(4,1)} fusion(s32[1024,6]{0,1:T(8,128)S(1)} %bitcast_add_fusion), kind=kLoop, calls=%fused_computation.3 | loop fusion | flops 138412032 | bytes 12607488 | tf_op jit(solution)/shard_map/reduce_or | solution.py:61
  68.7 62.1 %convolution_convert_fusion = bf16[12288,2048]{1,0:T(8,128)(2,1)} fusion(pred[1024,12288]{1,0:T(32,128)(4,1)} %fusion.1, bf16[1,1024,2048]{2,1,0:T(8,128)(2,1)} %param.17, f32[2048]{0:T(1024)S(1)} %convert_element_type.103, f32[1024]{0:T(1024)S(1)} %add_rsqrt_fusion.1), kind=kOutput, calls=%fused_computation.12 | convolution fusion | flops 51573161984 | bytes 67121152 | tf_op jit(solution)/shard_map/tr,td->rd/dot_general | solution.py:12
  130.8 604.6 %all_to_all.10 = bf16[32,2,192,2048]{3,2,1,0:T(8,128)(2,1)} all-to-all(bf16[32,2,192,2048]{3,2,1,0:T(8,128)(2,1)} %bitcast.105), channel_id=1, replica_groups=mesh['dp'=1,'ep'=32] {'ep'}, dimensions={0} | all-to-all | bytes 100663296 | tf_op jit(solution)/shard_map/all_to_all | solution.py:93
  735.4 87.8 %fusion.3 = f32[2,32,192,1408]{3,2,1,0:T(8,128)} fusion(bf16[32,2,192,2048]{3,2,1,0:T(8,128)(2,1)} %all_to_all.10, bf16[2,2048,1408]{2,1,0:T(8,128)(2,1)} %param.32), kind=kOutput, calls=%fused_computation.13 | convolution fusion | flops 70866960384 | bytes 131072000 | tf_op jit(solution)/shard_map/gecd,edf->egcf/dot_general | solution.py:12
  823.2 99.3 %multiply_convert_fusion.clone.4 = bf16[2,32,192,1408]{3,2,1,0:T(8,128)(2,1)} fusion(f32[2,32,192,1408]{3,2,1,0:T(8,128)} %fusion.3, bf16[32,2,192,2048]{3,2,1,0:T(8,128)(2,1)} %all_to_all.10, bf16[2,2048,1408]{2,1,0:T(8,128)(2,1)} %param.31), kind=kOutput, calls=%fused_computation.4.clone.clone.clone.1 | convolution fusion | flops 70970769408 | bytes 165675008 | tf_op jit(solution)/shard_map/gecd,edf->egcf/dot_general | solution.py:12
  922.5 95.7 %convert_bitcast_fusion = bf16[32,2,192,2048]{3,2,0,1:T(8,128)(2,1)} fusion(bf16[2,1408,2048]{2,1,0:T(8,128)(2,1)} %param.33, bf16[2,32,192,1408]{3,2,1,0:T(8,128)(2,1)} %multiply_convert_fusion.clone.4), kind=kOutput, calls=%fused_computation.11 | convolution fusion | flops 70892126208 | bytes 96468992 | tf_op jit(solution)/shard_map/egcf,efd->gecd/dot_general | solution.py:12
  1018.3 33.4 %copy.59 = bf16[32,2,192,2048]{3,2,1,0:T(8,128)(2,1)} copy(bf16[32,2,192,2048]{3,2,0,1:T(8,128)(2,1)} %convert_bitcast_fusion) | data formatting | bytes 100663296 | tf_op jit(solution)/shard_map/convert_element_type | solution.py:50
  1051.7 59.6 %all-to-all-start.1 = ((bf16[32,2,192,2048]{3,2,1,0:T(8,128)(2,1)}), bf16[32,2,192,2048]{3,2,1,0:T(8,128)(2,1)}, u32[]{:S(2)}, u32[]{:S(2)}) async-start(bf16[32,2,192,2048]{3,2,1,0:T(8,128)(2,1)} %copy.59), calls=%async_computation.1 | async-start | bytes 100663296 | tf_op jit(solution)/shard_map/all_to_all | solution.py:95
  1111.4 13.9 fusion.40
  1125.3 6.4 copy.66
  1131.7 12.4 copy.67
  1144.1 12.3 copy.68
  1156.9 3.6 fusion.59
  1161.5 1.3 iota_compare_fusion.1
  1162.8 1.0 fusion.62
  1163.8 12.9 fusion.43
  1176.7 16.1 fusion.46
  1192.7 4.7 fusion.51
  1197.4 37.2 %fusion.79 = (f32[16,1024]{1,0:T(8,128)S(1)}, f32[16,1024,1024]{1,2,0:T(8,128)}) fusion(pred[1024,1024]{0,1:T(8,128)(4,1)} %iota_compare_fusion.1, bf16[1024,16,64]{0,2,1:T(8,128)(2,1)} %get-tuple-element.9, bf16[1024,16,64]{0,2,1:T(8,128)(2,1)} %get-tuple-element.10, bf16[1024,16,64]{0,2,1:T(8,128)(2,1)} %get-tuple-element.6, ...), kind=kOutput, calls=%fused_computation.91 | convolution fusion | flops 4378854400 | bytes 76611584 | tf_op jit(solution)/shard_map/sub | solution.py:40
  1234.6 25.1 %fusion.50 = bf16[16,128,1024]{2,1,0:T(8,128)(2,1)} fusion(bf16[1024,16,128]{0,2,1:T(8,128)(2,1)} %bitcast.112, f32[16,1024,1024]{1,2,0:T(8,128)} %get-tuple-element.14, f32[16,1024]{1,0:T(8,128)S(1)} %get-tuple-element.13), kind=kOutput, calls=%fused_computation.66 | convolution fusion | flops 4330618880 | bytes 75563008 | tf_op jit(solution)/shard_map/bhqk,bkhe->bqhe/dot_general | solution.py:12
  1259.8 14.1 fusion.25
  1274.0 1.9 copy-done.18
  1276.0 17.9 fusion.56
  1293.9 17.6 multiply_convert_fusion.1
  1311.6 58.1 %select_reduce_fusion = f32[1024,12288]{1,0:T(8,128)} fusion(f32[1024,6]{0,1:T(8,128)S(1)} %fusion.67, s32[1024,6]{0,1:T(8,128)S(1)} %copy-done.5), kind=kLoop, calls=%fused_computation.1 | loop fusion | flops 213909504 | bytes 50380800 | tf_op jit(solution)/shard_map/reduce_sum | solution.py:62
  1369.6 421.4 %all-to-all-done.1 = bf16[32,2,192,2048]{3,2,1,0:T(8,128)(2,1)} async-done(((bf16[32,2,192,2048]{3,2,1,0:T(8,128)(2,1)}), bf16[32,2,192,2048]{3,2,1,0:T(8,128)(2,1)}, u32[]{:S(2)}, u32[]{:S(2)}) %all-to-all-start.1) | async-done | bytes 50331680 | tf_op jit(solution)/shard_map/all_to_all | solution.py:95
  1791.1 63.1 %fusion.15 = f32[1024,2048]{1,0:T(8,128)} fusion(bf16[12288,2048]{1,0:T(8,128)(2,1)} %bitcast.28, f32[1024,12288]{1,0:T(8,128)} %select_reduce_fusion), kind=kOutput, calls=%fused_computation.24 | convolution fusion | flops 51627687936 | bytes 109051904 | tf_op jit(solution)/shard_map/tr,rd->td/dot_general | solution.py:12
  1854.2 61.6 %fusion.7 = f32[1024,2048]{1,0:T(8,128)} fusion(bf16[12288,2048]{1,0:T(8,128)(2,1)} %bitcast.28, f32[1024,12288]{1,0:T(8,128)} %select_reduce_fusion), kind=kOutput, calls=%fused_computation.17 | convolution fusion | flops 51552190464 | bytes 109051904 | tf_op jit(solution)/shard_map/tr,rd->td/dot_general | solution.py:12
  1915.7 63.2 %fusion.9 = f32[1024,2048]{1,0:T(8,128)} fusion(bf16[12288,2048]{1,0:T(8,128)(2,1)} %bitcast.28, f32[1024,12288]{1,0:T(8,128)} %select_reduce_fusion), kind=kOutput, calls=%fused_computation.19 | convolution fusion | flops 51589939200 | bytes 109051904 | tf_op jit(solution)/shard_map/tr,rd->td/dot_general | solution.py:12
  1979.0 24.4 %fusion.29 = bf16[1,1024,2048]{2,1,0:T(8,128)(2,1)} fusion(bf16[1,1024,2048]{2,1,0:T(8,128)(2,1)} %copy-done.18, f32[1024,2048]{1,0:T(8,128)} %fusion.15, f32[1024,2048]{1,0:T(8,128)} %fusion.7, f32[1024,2048]{1,0:T(8,128)} %fusion.9, bf16[1024,2816]{1,0:T(8,128)(2,1)} %multiply_convert_fusion.1, bf16[2816,2048]{1,0:T(8,128)(2,1)} %param.28), kind=kOutput, calls=%fused_computation.45 | convolution fusion | flops 11823742976 | bytes 50855936 | tf_op jit(solution)/shard_map/bsf,fd->bsd/dot_general | solution.py:12
  (60 shorter events, 2.2 us)
Async XLA Ops:
  0.0 1156.9 %copy-start = (bf16[2048,64]{0,1:T(8,128)(2,1)S(1)}, bf16[2048,64]{0,1:T(8,128)(2,1)}, u32[]{:S(2)}) copy-start(bf16[2048,64]{0,1:T(8,128)(2,1)} %param.30) | copy-start | bytes 786436
  0.0 68.7 %copy-start.13 = (bf16[2048]{0:T(1024)(128)(2,1)S(1)}, bf16[2048]{0:T(1024)(128)(2,1)}, u32[]{:S(2)}) copy-start(bf16[2048]{0:T(1024)(128)(2,1)} %param.29) | copy-start | bytes 12292
  3.1 127.7 %copy-start.16 = (f32[1024]{0:T(1024)}, f32[1024]{0:T(1024)S(1)}, u32[]{:S(2)}) copy-start(f32[1024]{0:T(1024)S(1)} %add_rsqrt_fusion.1) | copy-start | bytes 12292
  3.9 0.6 copy-start.4
  68.7 62.1 %copy-start.11 = (f32[2048]{0:T(1024)}, f32[2048]{0:T(1024)S(1)}, u32[]{:S(2)}) copy-start(f32[2048]{0:T(1024)S(1)} %convert_element_type.103) | copy-start | bytes 24580
  1051.7 59.6 %copy-start.6 = (s32[1,1024,6]{1,0,2:T(1,128)S(1)}, s32[1,1024,6]{1,0,2:T(1,128)}, u32[]{:S(2)}) copy-start(s32[1,1024,6]{1,0,2:T(1,128)} %param.18) | copy-start | bytes 73732
  1051.7 59.7 %copy-start.14 = (bf16[2048]{0:T(1024)(128)(2,1)S(1)}, bf16[2048]{0:T(1024)(128)(2,1)}, u32[]{:S(2)}) copy-start(bf16[2048]{0:T(1024)(128)(2,1)} %param.20) | copy-start | bytes 12292
  1051.7 59.7 %copy-start.17 = (f32[1024]{0:T(1024)S(1)}, f32[1024]{0:T(1024)}, u32[]{:S(2)}) copy-start(f32[1024]{0:T(1024)} %copy-done.16) | copy-start | bytes 12292
  1051.7 739.3 %all-to-all-start.1 = ((bf16[32,2,192,2048]{3,2,1,0:T(8,128)(2,1)}), bf16[32,2,192,2048]{3,2,1,0:T(8,128)(2,1)}, u32[]{:S(2)}, u32[]{:S(2)}) async-start(bf16[32,2,192,2048]{3,2,1,0:T(8,128)(2,1)} %copy.59), calls=%async_computation.1 | async-start | bytes 100663296 | tf_op jit(solution)/shard_map/all_to_all | solution.py:95
  1144.1 12.3 copy-start.15
  1144.1 12.9 copy-start.12
  1160.8 0.7 copy-start.2
  1160.8 0.6 copy-start.7
  1161.5 15.2 slice-start
  1163.7 12.9 slice-start.1
  1259.8 14.2 copy-start.3
  1259.8 14.2 copy-start.8
  1259.8 14.2 copy-start.9
  1259.8 16.2 copy-start.10
  1259.8 34.1 %slice-start.2 = ((s8[11534336]{0:T(1024)(128)(4,1)}), s8[4194304]{0:T(1024)(128)(4,1)S(1)}, s32[]{:S(2)}) async-start(s8[11534336]{0:T(1024)(128)(4,1)} %bitcast.114), calls=%async_computation.4 | async-start | bytes 8388608
  1259.8 34.1 %slice-start.3 = ((s8[11534336]{0:T(1024)(128)(4,1)}), s8[4194304]{0:T(1024)(128)(4,1)S(1)}, s32[]{:S(2)}) async-start(s8[11534336]{0:T(1024)(128)(4,1)} %bitcast.114), calls=%async_computation.5 | async-start | bytes 8388608
  1273.9 2.0 copy-start.18
  1276.0 18.0 slice-start.4
  1293.9 17.7 copy-start.5
  1979.0 24.4 %copy-start.1 = (bf16[2048,64]{0,1:T(8,128)(2,1)S(1)}, bf16[2048,64]{0,1:T(8,128)(2,1)}, u32[]{:S(2)}) copy-start(bf16[2048,64]{0,1:T(8,128)(2,1)} %param.30) | copy-start | bytes 786436
where the time goes:
time: 2010 us; the launch traced here: 2000 us
  matrix products  716 us (36%)
  blocking collectives  605 us (30%)
  waiting for transfers between devices  421 us (21%)
  other arithmetic  135 us (7%)
  local copies, waits for them, and re-layouts  67.1 us (3%)
  starting transfers between devices  59.6 us (3%)
    dot_general x16, matrix products, _mm(): return jnp.einsum(form, a, b, preferred_element_type=jnp.float32)  679 us
    all_to_all x1, blocking collectives, local(): recv = lax.all_to_all(send, 'ep', 0, 0, tiled=True)  605 us
    all_to_all x1, waiting for transfers between devices, local(): back = lax.all_to_all(y, 'ep', 0, 0, tiled=True).reshape(ne * cap, d)  421 us
    reduce_or x1, other arithmetic, _route(): disp = jnp.any(hit, axis=-2).astype(jnp.bfloat16)  64.1 us
    all_to_all x1, starting transfers between devices, local(): back = lax.all_to_all(y, 'ep', 0, 0, tiled=True).reshape(ne * cap, d)  59.6 us
    reduce_sum x1, other arithmetic, _route(): comb = jnp.sum(jnp.where(hit, gate[..., None], 0.0), axis=-2)  58.1 us
  transfers between devices with their start and end apart: 1, of which 1 were waited for; matrix products, arithmetic and copies ran while one was open for 13% of the time, Pallas kernels for 0%

commit v1 on v0

v1 whole, which is shorter than its diff:
```python
import functools
import math

import jax
import jax.numpy as jnp
from jax import lax
from jax.experimental import pallas as pl
from jax.experimental.pallas import tpu as pltpu
from jax.sharding import PartitionSpec as P

HEAD = 128
EPS = 1e-6
CAP_FACTOR = 2
CORES = 2
EXTRA = 16
F32 = jnp.float32
BF16 = jnp.bfloat16
MESH = pl.DeviceIdType.MESH


def _mm(form, a, b):
    return jnp.einsum(form, a, b, preferred_element_type=jnp.float32)


def _rms(x, w):
    xf = x.astype(jnp.float32)
    r = lax.rsqrt(jnp.mean(xf * xf, axis=-1, keepdims=True) + EPS)
    return (xf * r * w.astype(jnp.float32)).astype(jnp.bfloat16)


def _rope(x):
    s, half = x.shape[1], x.shape[-1] // 2
    freq = 10000.0 ** (-jnp.arange(half, dtype=jnp.float32) / half)
    ang = jnp.arange(s, dtype=jnp.float32)[:, None] * freq[None, :]
    c = jnp.cos(ang)[None, :, None, :]
    sn = jnp.sin(ang)[None, :, None, :]
    x1, x2 = x[..., :half], x[..., half:]
    return jnp.concatenate([x1 * c - x2 * sn, x2 * c + x1 * sn], axis=-1)


def _dense(h0, ln_attn, wq, wk, wv, wo, ln_ffn, ws1, ws3, ws2):
    b, s, _ = h0.shape
    nh = wq.shape[1] // HEAD
    x1 = _rms(h0, ln_attn)
    q = _rope(_mm('bsd,de->bse', x1, wq).reshape(b, s, nh, HEAD)).astype(jnp.bfloat16)
    k = _rope(_mm('bsd,de->bse', x1, wk).reshape(b, s, nh, HEAD)).astype(jnp.bfloat16)
    v = _mm('bsd,de->bse', x1, wv).astype(jnp.bfloat16).reshape(b, s, nh, HEAD)
    sc = _mm('bqhe,bkhe->bhqk', q, k) * HEAD ** -0.5
    causal = jnp.arange(s)[:, None] >= jnp.arange(s)[None, :]
    p = jax.nn.softmax(jnp.where(causal, sc, -1e30), axis=-1).astype(jnp.bfloat16)
    o = _mm('bhqk,bkhe->bqhe', p, v).astype(jnp.bfloat16).reshape(b, s, nh * HEAD)
    a = (h0.astype(jnp.float32) + _mm('bse,ed->bsd', o, wo)).astype(jnp.bfloat16)
    x2 = _rms(a, ln_ffn)
    hs = (jax.nn.silu(_mm('bsd,df->bsf', x2, ws1)) * _mm('bsd,df->bsf', x2, ws3)).astype(jnp.bfloat16)
    return a, _mm('bsf,fd->bsd', hs, ws2)


def _gate(u, wr, gi):
    lg = _mm('td,de->te', u, wr)
    hit = gi[..., None] == jnp.arange(wr.shape[1], dtype=gi.dtype)
    return jax.nn.softmax(jnp.sum(jnp.where(hit, lg[:, None, :], 0.0), axis=-1), axis=-1)


def _parts(c):
    hi = c.astype(jnp.bfloat16)
    r = c - hi.astype(jnp.float32)
    mid = r.astype(jnp.bfloat16)
    lo = (r - mid.astype(jnp.float32)).astype(jnp.bfloat16)
    return hi, mid, lo


def _place(n):
    side = math.isqrt(n // CORES)
    me = lax.axis_index('ep')
    return side, me, (me // CORES) % side, me // (CORES * side), me % CORES


def _order(k, side):
    i, b = k % side, k // side
    return side - 1 - (i + b + 1) % side, side - 1 - i


def _k1(n, cap, slots, ug, qr, ue1, ue3, ue2, r_out, w13, w2, u, pm, xs, h, ys, wsem, w2sem, usem, ssem, rsem):
    side, me, x, y, c = _place(n)
    t, d = u.shape[1], u.shape[2]
    f = h.shape[1]
    dh = d // 2
    steps = side * side
    total = steps * 2

    def chip(k):
        dx, dy = _order(k, side)
        return (x + dx) % side, (y + dy) % side

    def u_copy(k):
        cx, cy = chip(k)
        return pltpu.make_async_copy(ug.at[pl.ds((cy * side + cx) * CORES, CORES), pl.ds(0, t)], u, usem)

    u_copy(0).start()
    for el in range(2):
        for j in range(f // 128):
            pltpu.make_async_copy(ue1.at[el, :, pl.ds(128 * j, 128)], w13.at[el, :, pl.ds(256 * j, 128)], wsem.at[el]).start()
            pltpu.make_async_copy(ue3.at[el, :, pl.ds(128 * j, 128)], w13.at[el, :, pl.ds(256 * j + 128, 128)], wsem.at[el]).start()
        pltpu.make_async_copy(ue2.at[el], w2.at[el], w2sem.at[el]).start()

    barrier = pltpu.get_barrier_semaphore()
    peers = 0
    for off in range(side):
        for dc in range(CORES):
            if off or dc:
                cc = (c + dc) % CORES
                pl.semaphore_signal(barrier, inc=1, device_id={'ep': (((y + off) % side) * side + x) * CORES + cc}, device_id_type=MESH)
                peers += 1
                if off:
                    pl.semaphore_signal(barrier, inc=1, device_id={'ep': (y * side + (x + off) % side) * CORES + cc}, device_id_type=MESH)
                    peers += 1
    pl.semaphore_wait(barrier, peers)

    def send(it):
        k, el = it // 2, it % 2
        s = it % slots
        dx, dy = _order(k, side)
        cx, cy = chip(k)
        for cc in range(CORES):
            for half, off, line, mine, dest in (
                (0, dy, cx, y, (cy * side + x) * CORES + cc),
                (1, dx, cy, x, (y * side + cx) * CORES + cc),
            ):
                src = ys.at[s, pl.ds(cc * cap, cap), pl.ds(half * dh, dh)]
                dst = r_out.at[half, line, pl.ds((mine * CORES + c) * (2 * cap) + el * cap, cap)]
                own = (off == 0) & (c == cc)

                @pl.when(own)
                def _():
                    pltpu.make_async_copy(src, dst, ssem.at[s]).start()

                @pl.when(jnp.logical_not(own))
                def _():
                    pltpu.make_async_remote_copy(src, dst, ssem.at[s], rsem, device_id={'ep': dest}, device_id_type=MESH).start()

    def wait_sent(s):
        pltpu.make_async_copy(ys.at[s], ys.at[s], ssem.at[s]).wait()

    @pl.loop(0, steps)
    def _(k):
        cx, cy = chip(k)
        u_copy(k).wait()

        @pl.loop(0, CORES)
        def _(cc):
            q = qr[(cy * side + cx) * CORES + cc]
            slot = lax.broadcasted_iota(jnp.int32, (cap, t), 0).astype(F32)
            for el in range(2):
                pm[pl.ds(el * cap, cap)] = jnp.where(slot == q[el:el + 1], 1.0, 0.0).astype(BF16)
            wide = min(512, d)
            for m in range(d // wide):
                cols = pl.ds(m * wide, wide)
                got = jnp.dot(pm[...], u[cc, :, cols], preferred_element_type=F32).astype(BF16)
                for el in range(2):
                    xs[el, pl.ds(pl.multiple_of(cc * cap, 16), cap), cols] = got[el * cap:(el + 1) * cap]

        @pl.when(k + 1 < steps)
        def _():
            u_copy(k + 1).start()

        @pl.loop(0, 2)
        def _(el):
            it = 2 * k + el
            s = it % slots

            @pl.when(it >= 1)
            def _():
                send(it - 1)

            @pl.when(it >= slots)
            def _():
                wait_sent(s)

            @pl.when(k == 0)
            def _():
                pltpu.make_async_copy(w13.at[el], w13.at[el], wsem.at[el]).wait()
                pltpu.make_async_copy(w2.at[el], w2.at[el], w2sem.at[el]).wait()

            group = 2
            for j in range(0, f // 128, group):
                g = min(group, f // 128 - j)
                a = jnp.dot(xs[el], w13[el, :, pl.ds(256 * j, 256 * g)], preferred_element_type=F32)
                for i in range(g):
                    a1, a3 = a[:, 256 * i:256 * i + 128], a[:, 256 * i + 128:256 * i + 256]
                    h[:, pl.ds(128 * (j + i), 128)] = (jax.nn.silu(a1) * a3).astype(BF16)
            wide = min(512, d)
            for m in range(d // wide):
                cols = pl.ds(m * wide, wide)
                ys[s, :, cols] = jnp.dot(h[...], w2[el, :, cols], preferred_element_type=F32).astype(BF16)

    send(total - 1)
    for s in range(slots):
        wait_sent(s)
    got = r_out.at[:, :, pl.ds(0, (CORES * side - 1) * 2 * cap)]
    pltpu.make_async_copy(got, got, rsem).wait()


def _k2(n, cap, r, pg, z, out, rb, mr, mt, pm, sb, rx2, rxf, zb, ob, lsem, msem, ssem, r2sem, rfsem, zsem, osem):
    side, me, x, y, c = _place(n)
    t = mt.shape[0]
    kk, dh = rb.shape[1], rb.shape[2]
    nm = rx2.shape[2] * 2
    tile = rx2.shape[3]
    keep = sb.shape[0] // nm
    units = 2 * side

    def role(w):
        s = side - 1 - w // 2
        return w % 2, s + (s // 2) * (1 - 2 * (s % 2))

    def at(half, off):
        return ((y + half * off) % side * side + (x + (1 - half) * off) % side) * CORES + c

    def line(w):
        half, off = role(w)
        return half, (x * (1 - half) + y * half + off) % side

    def loads(w):
        half, at_line = line(w)
        b = w % 2
        return (
            pltpu.make_async_copy(r.at[half, at_line], rb.at[b], lsem.at[b]),
            pltpu.make_async_copy(pg.at[half, at_line], mr.at[b], msem.at[b]),
        )

    for cp in loads(0):
        cp.start()

    barrier = pltpu.get_barrier_semaphore()
    for half in range(2):
        for off in (1, side - 1):
            pl.semaphore_signal(barrier, inc=1, device_id={'ep': at(half, off)}, device_id_type=MESH)
    pl.semaphore_wait(barrier, 4)

    def z_copy(half, m):
        return pltpu.make_async_copy(z.at[pl.ds(m * tile, tile), pl.ds(half * dh, dh)], zb, zsem)

    def o_copy(half, m, b):
        return pltpu.make_async_copy(ob.at[b], out.at[pl.ds(m * tile, tile), pl.ds(half * dh, dh)], osem.at[b])

    def send(w, m):
        half, off = role(w)
        b = w % keep
        src = sb.at[b * nm + m]

        def go(dst, sem, step):
            pltpu.make_async_remote_copy(src, dst, ssem.at[b], sem, device_id={'ep': at(half, step)}, device_id_type=MESH).start()

        @pl.when((off == 2) & (m < nm // 2))
        def _():
            go(rx2.at[half, 0, m], r2sem.at[half, 0, m], 1)

        @pl.when((off == 2) & (m >= nm // 2))
        def _():
            go(rx2.at[half, 1, m - nm // 2], r2sem.at[half, 1, m - nm // 2], side - 1)

        @pl.when(off == 1)
        def _():
            go(rxf.at[half, 0, m], rfsem.at[half, 0, m], 1)

        @pl.when(off == side - 1)
        def _():
            go(rxf.at[half, 1, m], rfsem.at[half, 1, m], side - 1)

    def wait_recv(ref, sem):
        pltpu.make_async_copy(ref, ref, sem).wait()

    def wait_sent(b):
        sent = sb.at[pl.ds(b * nm, nm)]
        pltpu.make_async_copy(sent, sent, ssem.at[b]).wait()

    @pl.loop(0, units)
    def _(w):
        half, off = role(w)
        for cp in loads(w):
            cp.wait()

        @pl.when(w + 1 < units)
        def _():
            for cp in loads(w + 1):
                cp.start()

        meta = mr[w % 2]
        mt[...] = jnp.concatenate([meta, jnp.zeros((128 - meta.shape[0], t), F32)], axis=0).T

        @pl.when((w >= keep) & (w < units - 2))
        def _():
            wait_sent(w % keep)

        @pl.loop(0, nm)
        def _(m):
            it = w * nm + m

            @pl.when((it >= 1) & (it <= (units - 2) * nm))
            def _():
                send((it - 1) // nm, (it - 1) % nm)

            @pl.when(off == 0)
            def _():
                z_copy(half, m).start()

            rows = mt[pl.ds(m * tile, tile)]
            step = kk // 6
            for kc in range(0, kk, step):
                at_k = lax.broadcasted_iota(jnp.int32, (tile, step), 1).astype(F32) + float(kc)
                v = jnp.zeros((tile, step), F32)
                for j in range(6):
                    v = jnp.where(at_k == rows[:, j:j + 1], rows[:, 8 + j:9 + j], v)
                for i, part in enumerate(_parts(v)):
                    pm[pl.ds(i * tile, tile), pl.ds(kc, step)] = part

            wide = min(512, dh)
            own = w // (units - 2)
            here = (1 - own) * (w % keep * nm + m) + own * (keep * nm)
            for i in range(dh // wide):
                cols = pl.ds(i * wide, wide)
                o = jnp.dot(pm[...], rb[w % 2, :, cols], preferred_element_type=F32)
                sb[here, :, cols] = o[:tile] + o[tile:2 * tile] + o[2 * tile:]

            @pl.when((off == 1) & (m < nm // 2))
            def _():
                wait_recv(rx2.at[half, 0, m], r2sem.at[half, 0, m])
                sb[here] = sb[here] + rx2[half, 0, m]

            @pl.when((off == side - 1) & (m >= nm // 2))
            def _():
                wait_recv(rx2.at[half, 1, m - nm // 2], r2sem.at[half, 1, m - nm // 2])
                sb[here] = sb[here] + rx2[half, 1, m - nm // 2]

            @pl.when(off == 0)
            def _():
                done = half * nm + m

                @pl.when(done >= 2)
                def _():
                    o_copy((done - 2) // nm, (done - 2) % nm, m % 2).wait()

                wait_recv(rxf.at[half, 0, m], rfsem.at[half, 0, m])
                wait_recv(rxf.at[half, 1, m], rfsem.at[half, 1, m])
                z_copy(half, m).wait()
                total = zb[...] + (sb[here] + rxf[half, 0, m] + rxf[half, 1, m])
                ob[m % 2] = total.astype(BF16)
                o_copy(half, m, m % 2).start()

    for w in range(units - 2 - keep, units - 2):
        wait_sent(w % keep)
    for m in (nm - 2, nm - 1):
        o_copy(1, m, m % 2).wait()


def _experts(ug, qr, ue1, ue3, ue2, n, cap):
    t, d, f = qr.shape[-1], ug.shape[-1], ue1.shape[-1]
    side = math.isqrt(n // CORES)
    slots = 4
    any_ = pl.BlockSpec(memory_space=pl.ANY)
    flops = n * 2 * cap * (2 * t * d + 6 * d * f)
    return pl.pallas_call(
        functools.partial(_k1, n, cap, slots),
        out_shape=jax.ShapeDtypeStruct((2, side, CORES * side * 2 * cap, d // 2), BF16),
        in_specs=[any_, pl.BlockSpec(memory_space=pltpu.VMEM), any_, any_, any_],
        out_specs=any_,
        scratch_shapes=[
            pltpu.VMEM((2, d, 2 * f), BF16),
            pltpu.VMEM((2, f, d), BF16),
            pltpu.VMEM((CORES, t, d), BF16),
            pltpu.VMEM((2 * cap, t), BF16),
            pltpu.VMEM((2, CORES * cap, d), BF16),
            pltpu.VMEM((CORES * cap, f), BF16),
            pltpu.VMEM((slots, CORES * cap, d), BF16),
            pltpu.SemaphoreType.DMA((2,)),
            pltpu.SemaphoreType.DMA((2,)),
            pltpu.SemaphoreType.DMA,
            pltpu.SemaphoreType.DMA((slots,)),
            pltpu.SemaphoreType.DMA,
        ],
        cost_estimate=pl.CostEstimate(flops=flops, bytes_accessed=4 * n * t * d, transcendentals=n * 2 * cap * f),
        compiler_params=pltpu.CompilerParams(collective_id=0, has_side_effects=True, vmem_limit_bytes=67043328),
        name='experts',
    )(ug, qr, ue1, ue3, ue2)


def _combine(r, pg, z, n, cap):
    t, d = z.shape
    dh = d // 2
    side = math.isqrt(n // CORES)
    nm = 4
    tile = t // nm
    kk = r.shape[2]
    keep = 3
    any_ = pl.BlockSpec(memory_space=pl.ANY)
    return pl.pallas_call(
        functools.partial(_k2, n, cap),
        out_shape=jax.ShapeDtypeStruct((t, d), BF16),
        in_specs=[any_, any_, any_],
        out_specs=any_,
        scratch_shapes=[
            pltpu.VMEM((2, kk, dh), BF16),
            pltpu.VMEM((2, pg.shape[2], t), F32),
            pltpu.VMEM((t, 128), F32),
            pltpu.VMEM((3 * tile, kk), BF16),
            pltpu.VMEM((keep * nm + 1, tile, dh), F32),
            pltpu.VMEM((2, 2, nm // 2, tile, dh), F32),
            pltpu.VMEM((2, 2, nm, tile, dh), F32),
            pltpu.VMEM((tile, dh), F32),
            pltpu.VMEM((2, tile, dh), BF16),
            pltpu.SemaphoreType.DMA((2,)),
            pltpu.SemaphoreType.DMA((2,)),
            pltpu.SemaphoreType.DMA((keep,)),
            pltpu.SemaphoreType.DMA((2, 2, nm // 2)),
            pltpu.SemaphoreType.DMA((2, 2, nm)),
            pltpu.SemaphoreType.DMA,
            pltpu.SemaphoreType.DMA((2,)),
        ],
        cost_estimate=pl.CostEstimate(flops=2 * side * 3 * 2 * t * kk * dh, bytes_accessed=2 * r.size, transcendentals=0),
        compiler_params=pltpu.CompilerParams(collective_id=1, has_side_effects=True, vmem_limit_bytes=67043328),
        name='combine',
    )(r, pg, z)


def _encode(gi, sl, gate, t, d):
    rows = [gi.T.astype(BF16), sl.T.astype(BF16)] + [p.T for p in _parts(gate)]
    e = jnp.concatenate(rows, axis=0)
    e = jnp.pad(e, ((0, EXTRA * d // t - e.shape[0]), (0, 0)))
    return e.reshape(EXTRA, d)


def _decode(extra, top, t, n, cap):
    side = math.isqrt(n // CORES)
    me = lax.axis_index('ep')
    x, y = (me // CORES) % side, me // (CORES * side)
    e = extra.reshape(n, -1, t).astype(F32)
    ex, sl = e[:, :top].astype(jnp.int32), e[:, top:2 * top].astype(jnp.int32)
    g = e[:, 2 * top:3 * top] + e[:, 3 * top:4 * top] + e[:, 4 * top:5 * top]
    q = []
    for el in range(2):
        mine = ex == me * 2 + el
        q.append(jnp.sum(jnp.where(mine, sl + 1, 0), axis=1) - 1)
    qr = jnp.stack(q + [q[0]] * 6, axis=1).astype(F32)
    chip_x, chip_y = (ex // (2 * CORES)) % side, ex // (2 * CORES * side)
    low = (ex % (2 * CORES)) * cap + sl
    pa = jnp.where(chip_x == x, chip_y * (2 * CORES * cap) + low, -1)
    pb = jnp.where(chip_y == y, chip_x * (2 * CORES * cap) + low, -1)
    pad = jnp.zeros((n, 8 - top, t), F32)
    out = []
    for p in (pa, pb):
        out.append(jnp.concatenate([p.astype(F32), pad, g, pad], axis=1))
    grid = lambda v: v.reshape(side, side, CORES, 16, t)
    c = me % CORES
    va = lax.dynamic_slice(grid(out[0]), (y, 0, c, 0, 0), (1, side, 1, 16, t)).reshape(side, 16, t)
    vb = lax.dynamic_slice(grid(out[1]), (0, x, c, 0, 0), (side, 1, 1, 16, t)).reshape(side, 16, t)
    return qr, jnp.stack([va, vb])


def solution(mesh):
    n = mesh.shape['ep']
    rows = P(('dp', 'ep'))
    rep = P()

    def local(h0, idx, slot, ln_attn, wq, wk, wv, wo, ln_ffn, ws1, ws3, ws2, ln_moe, wr, ue1, ue3, ue2):
        b, s, d = h0.shape
        top = idx.shape[-1]
        ne = ue1.shape[0] * n
        t = b * s
        cap = CAP_FACTOR * t * top // ne
        u = _rms(h0, ln_moe).reshape(t, d)
        gi, sl = idx.reshape(t, top), slot.reshape(t, top)
        gate = _gate(u, wr, gi)
        ug = lax.all_gather(jnp.concatenate([u, _encode(gi, sl, gate, t, d)], axis=0), 'ep')
        a, fo = _dense(h0, ln_attn, wq, wk, wv, wo, ln_ffn, ws1, ws3, ws2)
        z = (a.astype(F32) + fo).reshape(t, d)
        qr, pg = _decode(ug[:, t:], top, t, n, cap)
        r = _experts(ug, qr, ue1, ue3, ue2, n, cap)
        return _combine(r, pg, z, n, cap).reshape(b, s, d)

    specs = (rows, rows, rows) + (rep,) * 11 + (P('ep'), P('ep'), P('ep'))
    return jax.shard_map(local, mesh=mesh, in_specs=specs, out_specs=rows, check_vma=False)
```

time: 2010 us -> 1140 us (0.57)
  the two profiles are of different devices: /device:TPU:123 before, /device:TPU:97 now
where the time goes in v1:
time: 1140 us
  Pallas kernels  696 us (61%)
  waiting for transfers between devices  174 us (15%)
  matrix products  168 us (15%)
  local copies, waits for them, and re-layouts  47.3 us (4%)
  other arithmetic  36.2 us (3%)
  between operations  14.1 us (1%)
    pallas_call x1, Pallas kernels, _experts(): pl.pallas_call(functools.partial(_k1, n, cap, slots), out_shape=jax.Shape...  441 us
    pallas_call x1, Pallas kernels, _combine(): pl.pallas_call(functools.partial(_k2, n, cap), out_shape=jax.ShapeDtypeSt...  255 us
    all_gather x1, waiting for transfers between devices, local(): lax.all_gather(jnp.concatenate([u, _encode(gi, sl, gate, t, d)], axis=0),...  174 us
    dot_general x8, matrix products, _mm(): return jnp.einsum(form, a, b, preferred_element_type=jnp.float32)  134 us
    sub x1, matrix products, _dense(): jax.nn.softmax(jnp.where(causal, sc, -1e+30), axis=-1).astype(jnp.bfloat16)  33.6 us
    dot_general x2, local copies, waits for them, and re-layouts, _mm(): return jnp.einsum(form, a, b, preferred_element_type=jnp.float32)  24.6 us
  transfers between devices with their start and end apart: 1, of which 1 were waited for; matrix products, arithmetic and copies ran while one was open for 18% of the time, Pallas kernels for 0%

profile of v1, /device:TPU:97, one launch (start us, length us, event | category | flops | bytes accessed | tf_op | source)
XLA Modules:
  0.0 1135.9 jit_solution(15742106933560547697)
XLA Ops:
  6.6 3.2 fusion.10
  11.3 1.0 fusion.19
  12.3 2.0 copy-done
  14.3 1.4 fusion.70
  16.5 4.9 pad_maximum_fusion
  22.1 13.9 %fusion.26 = bf16[1024,2048]{1,0:T(8,128)(2,1)} fusion(bf16[2048,2048]{1,0:T(8,128)(2,1)} %param.23, bf16[1,1024,2048]{2,1,0:T(8,128)(2,1)} %param.17, f32[2048]{0:T(1024)S(1)} %convert_element_type.141, f32[1024]{0:T(1024)S(1)} %add_rsqrt_fusion.1), kind=kOutput, calls=%fused_computation.43 | convolution fusion | flops 8600420352 | bytes 16789504 | tf_op jit(solution)/shard_map/bsd,de->bse/dot_general | solution.py:22
  36.0 6.4 copy.47
  42.4 12.3 %copy.48 = bf16[2048,2048]{1,0:T(8,128)(2,1)} copy(bf16[2048,2048]{0,1:T(8,128)(2,1)} %bitcast.93) | data formatting | bytes 16777216 | tf_op jit(solution)/shard_map/bsd,de->bse/dot_general | solution.py:22
  54.7 12.2 %copy.49 = bf16[2048,2048]{1,0:T(8,128)(2,1)} copy(bf16[2048,2048]{0,1:T(8,128)(2,1)} %bitcast.94) | data formatting | bytes 16777216 | tf_op jit(solution)/shard_map/bsd,de->bse/dot_general | solution.py:22
  67.3 1.0 fusion.53
  68.3 12.8 %fusion.29 = f32[1,1024,16,128]{1,3,2,0:T(8,128)S(1)} fusion(bf16[16,128,2048]{2,1,0:T(8,128)(2,1)} %bitcast.96, bf16[1,1024,2048]{2,1,0:T(8,128)(2,1)} %param.17, f32[2048]{0:T(1024)S(1)} %convert_element_type.141, f32[1024]{0:T(1024)S(1)} %add_rsqrt_fusion.1), kind=kOutput, calls=%fused_computation.44 | convolution fusion | flops 8598323200 | bytes 20983808 | tf_op jit(solution)/shard_map/bsd,de->bse/dot_general | solution.py:22
  81.2 11.7 %fusion.32 = f32[1,1024,16,128]{1,3,2,0:T(8,128)S(1)} fusion(bf16[16,128,2048]{2,1,0:T(8,128)(2,1)} %bitcast.95, bf16[1,1024,2048]{2,1,0:T(8,128)(2,1)S(1)} %copy-done.3, f32[2048]{0:T(1024)S(1)} %convert_element_type.141, f32[1024]{0:T(1024)S(1)} %add_rsqrt_fusion.1), kind=kOutput, calls=%fused_computation.45 | convolution fusion | flops 8598323200 | bytes 20983808 | tf_op jit(solution)/shard_map/bsd,de->bse/dot_general | solution.py:22
  92.9 4.8 fusion.37
  97.7 33.6 %fusion.69 = (f32[16,1024]{1,0:T(8,128)S(1)}, f32[16,1024,1024]{1,2,0:T(8,128)}) fusion(pred[1024,1024]{0,1:T(8,128)(4,1)S(1)} %iota_compare_fusion, bf16[1024,16,64]{0,2,1:T(8,128)(2,1)} %get-tuple-element.17, bf16[1024,16,64]{0,2,1:T(8,128)(2,1)} %get-tuple-element.18, bf16[1024,16,64]{0,2,1:T(8,128)(2,1)} %get-tuple-element.11, ...), kind=kOutput, calls=%fused_computation.116 | convolution fusion | flops 4378854400 | bytes 76611584 | tf_op jit(solution)/shard_map/sub | solution.py:50
  131.3 25.5 %fusion.36 = bf16[16,128,1024]{2,1,0:T(8,128)(2,1)} fusion(bf16[1024,16,128]{0,2,1:T(8,128)(2,1)} %bitcast.97, f32[16,1024,1024]{1,2,0:T(8,128)} %get-tuple-element.26, f32[16,1024]{1,0:T(8,128)S(1)} %get-tuple-element.25), kind=kOutput, calls=%fused_computation.51 | convolution fusion | flops 4330618880 | bytes 75563008 | tf_op jit(solution)/shard_map/bhqk,bkhe->bqhe/dot_general | solution.py:22
  156.8 14.0 %fusion.12 = (f32[1024]{0:T(1024)S(1)}, bf16[1,1024,2048]{2,1,0:T(8,128)(2,1)S(1)}) fusion(bf16[1024,2048]{0,1:T(8,128)(2,1)} %bitcast.101, bf16[2048,2048]{1,0:T(8,128)(2,1)} %param.24, bf16[1,1024,2048]{2,1,0:T(8,128)(2,1)} %param.17), kind=kOutput, calls=%fused_computation.22 | convolution fusion | flops 8602516480 | bytes 20975616 | tf_op jit(solution)/shard_map/bse,ed->bsd/dot_general | solution.py:22
  170.8 2.0 copy-done.8
  172.8 17.7 %fusion.43 = f32[1024,2816]{1,0:T(8,128)} fusion(bf16[2048,2816]{1,0:T(8,128)(2,1)} %param.26, bf16[1,1024,2048]{2,1,0:T(8,128)(2,1)S(1)} %get-tuple-element.28, f32[2048]{0:T(1024)S(1)} %copy-done.5, f32[1024]{0:T(1024)S(1)} %add_rsqrt_fusion), kind=kOutput, calls=%fused_computation.72 | convolution fusion | flops 11819548672 | bytes 27275264 | tf_op jit(solution)/shard_map/bsd,df->bsf/dot_general | solution.py:22
  190.5 37.0 %fusion.15.z = f32[1024,2048]{1,0:T(8,128)} fusion(bf16[1,1024,2048]{2,1,0:T(8,128)(2,1)} %copy-done.8, bf16[2816,2048]{1,0:T(8,128)(2,1)} %param.28, f32[1024,2816]{1,0:T(8,128)} %fusion.43, bf16[2048,2816]{1,0:T(8,128)(2,1)} %param.27, f32[2048]{0:T(1024)S(1)} %copy-done.5, f32[1024]{0:T(1024)S(1)} %add_rsqrt_fusion), kind=kOutput, calls=%fused_computation.25 | convolution fusion | flops 23652204544 | bytes 47198208 | tf_op jit(solution)/shard_map/bsf,fd->bsd/dot_general | solution.py:22
  227.5 174.4 %all-gather.3.cloned.1.call-done = bf16[33280,2048]{1,0:T(8,128)(2,1)} async-done(((bf16[1040,2048]{1,0:T(8,128)(2,1)}), bf16[33280,2048]{1,0:T(8,128)(2,1)}) %all-gather.3.cloned.1.call-update) | async-done | bytes 136314896 | tf_op jit(solution)/shard_map/all_gather | solution.py:473
  401.9 4.1 slice_convert_fusion
  406.0 5.1 reshape.244
  411.1 2.8 slice_add_fusion
  413.9 5.1 select_convert_fusion.1
  419.1 2.8 select_reduce_fusion.1
  422.2 1.6 stack.4
  423.8 1.1 convert_element_type.138.qr
  425.0 1.9 pad_maximum_fusion.4
  426.9 0.8 pad_maximum_fusion.19.pg
  427.8 441.2 %experts.1.r = bf16[2,4,3072,1024]{3,2,1,0:T(8,128)(2,1)} custom-call(bf16[32,1040,2048]{2,1,0:T(8,128)(2,1)} %bitcast.5.ug, f32[32,8,1024]{2,1,0:T(8,128)} %convert_element_type.138.qr, bf16[2,2048,1408]{2,1,0:T(8,128)(2,1)} %ue1.1, bf16[2,2048,1408]{2,1,0:T(8,128)(2,1)} %ue3.1, bf16[2,1408,2048]{2,1,0:T(8,128)(2,1)} %ue2.1), custom_call_target="tpu_custom_call" | custom-call | flops 264140488704 | bytes 268435456 | tf_op jit(solution)/shard_map/experts/pallas_call | solution.py:362
  868.9 255.0 %combine.1 = bf16[1024,2048]{1,0:T(8,128)(2,1)} custom-call(bf16[2,4,3072,1024]{3,2,1,0:T(8,128)(2,1)} %experts.1.r, f32[2,4,16,1024]{3,2,1,0:T(8,128)} %pad_maximum_fusion.19.pg, f32[1024,2048]{1,0:T(8,128)} %fusion.15.z), custom_call_target="tpu_custom_call" | custom-call | flops 154618822656 | bytes 50331648 | tf_op jit(solution)/shard_map/combine/pallas_call | solution.py:396
  1124.0 4.8 copy.58
  (41 shorter events, 3.6 us)
Async XLA Ops:
  6.5 395.3 %all-gather.3.cloned.1.call-start = ((), (), s32[]{:S(2)}) async-start(), calls=%async_computation | async-start | bytes 140574720 | tf_op jit(solution)/shard_map/all_gather | solution.py:473
  6.6 4.7 copy-start.2
  6.6 7.8 copy-start.4
  12.3 2.0 copy-start
  16.5 5.0 copy-start.6
  16.5 5.0 copy-start.7
  68.3 12.9 %copy-start.3 = (bf16[1,1024,2048]{2,1,0:T(8,128)(2,1)S(1)}, bf16[1,1024,2048]{2,1,0:T(8,128)(2,1)}, u32[]{:S(2)}) copy-start(bf16[1,1024,2048]{2,1,0:T(8,128)(2,1)} %param.17) | copy-start | bytes 12582916
  156.8 16.0 %copy-start.5 = (f32[2048]{0:T(1024)S(1)}, f32[2048]{0:T(1024)}, u32[]{:S(2)}) copy-start(f32[2048]{0:T(1024)} %convert_element_type.150) | copy-start | bytes 24580
  170.8 2.0 copy-start.8
  411.1 7.9 copy-start.1
Sparse Core Ops, SparseCore 0:
  21.6 380.2 all-gather.2

commit v2 on v1

v2 whole, which is shorter than its diff:
```python
import functools
import math

import jax
import jax.numpy as jnp
from jax import lax
from jax.experimental import pallas as pl
from jax.experimental.pallas import tpu as pltpu
from jax.sharding import PartitionSpec as P

HEAD = 128
EPS = 1e-6
CAP_FACTOR = 2
CORES = 2
EXTRA = 16
F32 = jnp.float32
BF16 = jnp.bfloat16
MESH = pl.DeviceIdType.MESH


def _mm(form, a, b):
    return jnp.einsum(form, a, b, preferred_element_type=jnp.float32)


def _rms(x, w):
    xf = x.astype(jnp.float32)
    r = lax.rsqrt(jnp.mean(xf * xf, axis=-1, keepdims=True) + EPS)
    return (xf * r * w.astype(jnp.float32)).astype(jnp.bfloat16)


def _rope(x):
    s, half = x.shape[1], x.shape[-1] // 2
    freq = 10000.0 ** (-jnp.arange(half, dtype=jnp.float32) / half)
    ang = jnp.arange(s, dtype=jnp.float32)[:, None] * freq[None, :]
    c = jnp.cos(ang)[None, :, None, :]
    sn = jnp.sin(ang)[None, :, None, :]
    x1, x2 = x[..., :half], x[..., half:]
    return jnp.concatenate([x1 * c - x2 * sn, x2 * c + x1 * sn], axis=-1)


def _dense(h0, ln_attn, wq, wk, wv, wo, ln_ffn, ws1, ws3, ws2):
    b, s, _ = h0.shape
    nh = wq.shape[1] // HEAD
    x1 = _rms(h0, ln_attn)
    q = _rope(_mm('bsd,de->bse', x1, wq).reshape(b, s, nh, HEAD)).astype(jnp.bfloat16)
    k = _rope(_mm('bsd,de->bse', x1, wk).reshape(b, s, nh, HEAD)).astype(jnp.bfloat16)
    v = _mm('bsd,de->bse', x1, wv).astype(jnp.bfloat16).reshape(b, s, nh, HEAD)
    sc = _mm('bqhe,bkhe->bhqk', q, k) * HEAD ** -0.5
    causal = jnp.arange(s)[:, None] >= jnp.arange(s)[None, :]
    p = jax.nn.softmax(jnp.where(causal, sc, -1e30), axis=-1).astype(jnp.bfloat16)
    o = _mm('bhqk,bkhe->bqhe', p, v).astype(jnp.bfloat16).reshape(b, s, nh * HEAD)
    a = (h0.astype(jnp.float32) + _mm('bse,ed->bsd', o, wo)).astype(jnp.bfloat16)
    x2 = _rms(a, ln_ffn)
    hs = (jax.nn.silu(_mm('bsd,df->bsf', x2, ws1)) * _mm('bsd,df->bsf', x2, ws3)).astype(jnp.bfloat16)
    return a, _mm('bsf,fd->bsd', hs, ws2)


def _gate(u, wr, gi):
    lg = _mm('td,de->te', u, wr)
    hit = gi[..., None] == jnp.arange(wr.shape[1], dtype=gi.dtype)
    return jax.nn.softmax(jnp.sum(jnp.where(hit, lg[:, None, :], 0.0), axis=-1), axis=-1)


def _parts(c):
    hi = c.astype(jnp.bfloat16)
    r = c - hi.astype(jnp.float32)
    mid = r.astype(jnp.bfloat16)
    lo = (r - mid.astype(jnp.float32)).astype(jnp.bfloat16)
    return hi, mid, lo


def _place(n):
    side = math.isqrt(n // CORES)
    me = lax.axis_index('ep')
    return side, me, (me // CORES) % side, me // (CORES * side), me % CORES


def _turn(i, side):
    s = side - 1 - i
    return s + (s // 2) * (1 - 2 * (s % 2))


def _order(k, side):
    i, b = k % side, k // side
    return _turn((i + b + 1) % side, side), _turn(i, side)


def _routing(rows, t):
    e = rows.astype(F32)
    left, right = e[:, :t], e[:, t:]
    lo = jnp.concatenate([left[12:16], right[12:14]], axis=0)
    return left[0:6], left[6:12], right[0:6] + right[6:12] + lo


def _k1(n, cap, slots, ug, ue1, ue3, ue2, r_out, rl, w13, w2, u, pm, xs, h, ys, wsem, w2sem, usem, ssem, rsem, relsem, fsem):
    side, me, x, y, c = _place(n)
    t, d = pm.shape[1], u.shape[2]
    f = h.shape[1]
    dh = d // 2
    steps = side * side
    total = steps * 2
    far = side // 2
    lag = 4

    def chip(k):
        dx, dy = _order(k, side)
        return (x + dx) % side, (y + dy) % side

    def u_copy(k):
        cx, cy = chip(k)
        return pltpu.make_async_copy(ug.at[pl.ds((cy * side + cx) * CORES, CORES)], u, usem)

    u_copy(0).start()
    for el in range(2):
        for j in range(f // 128):
            pltpu.make_async_copy(ue1.at[el, :, pl.ds(128 * j, 128)], w13.at[el, :, pl.ds(256 * j, 128)], wsem.at[el]).start()
            pltpu.make_async_copy(ue3.at[el, :, pl.ds(128 * j, 128)], w13.at[el, :, pl.ds(256 * j + 128, 128)], wsem.at[el]).start()
        pltpu.make_async_copy(ue2.at[el], w2.at[el], w2sem.at[el]).start()

    def device(half, off, cc):
        return ((y + (1 - half) * off) % side * side + (x + half * off) % side) * CORES + cc

    barrier = pltpu.get_barrier_semaphore()
    peers = 0
    for off in range(side):
        for dc in range(CORES):
            for half in range(2):
                if off or (dc and not half):
                    pl.semaphore_signal(barrier, inc=1, device_id={'ep': device(half, off, (c + dc) % CORES)}, device_id_type=MESH)
                    peers += 1
    pl.semaphore_wait(barrier, peers)

    def remote(src, dst, send_sem, recv_sem, dest):
        return pltpu.make_async_remote_copy(src, dst, send_sem, recv_sem, device_id={'ep': dest}, device_id_type=MESH)

    def send(it):
        k, el = it // 2, it % 2
        s = it % slots
        dx, dy = _order(k, side)
        cx, cy = chip(k)
        for cc in range(CORES):
            for half, off, line, mine in ((0, dy, cx, y), (1, dx, cy, x)):
                src = ys.at[s, pl.ds(cc * cap, cap), pl.ds(half * dh, dh)]
                dst = r_out.at[half, line, pl.ds((mine * CORES + c) * (2 * cap) + el * cap, cap)]
                own = (off == 0) & (c == cc)

                @pl.when(own)
                def _():
                    pltpu.make_async_copy(src, dst, ssem.at[s]).start()

                @pl.when(jnp.logical_not(own) & (off != far))
                def _():
                    remote(src, dst, ssem.at[s], rsem, device(half, off, cc)).start()

                @pl.when(off == far)
                def _():
                    at = (half, cc, k // side, el)
                    remote(src, rl.at[at], ssem.at[s], relsem.at[at], device(half, 1 - 2 * cc, c)).start()

    def forward(it):
        k, el = it // 2, it % 2
        dx, dy = _order(k, side)
        cx, cy = chip(k)
        for half, off, line, mine in ((0, dy, cx, y), (1, dx, cy, x)):
            @pl.when(off == far)
            def _():
                for cc in range(CORES):
                    at = (half, cc, k // side, el)
                    step = 1 - 2 * cc
                    pltpu.make_async_copy(rl.at[at], rl.at[at], relsem.at[at]).wait()
                    origin = (mine - step + side) % side
                    dst = r_out.at[half, line, pl.ds((origin * CORES + c) * (2 * cap) + el * cap, cap)]
                    remote(rl.at[at], dst, fsem, rsem, device(half, step, cc)).start()

    def wait_sent(s):
        pltpu.make_async_copy(ys.at[s], ys.at[s], ssem.at[s]).wait()

    @pl.loop(0, steps)
    def _(k):
        u_copy(k).wait()

        @pl.loop(0, CORES)
        def _(cc):
            ex, sl, _ = _routing(u[cc, t:], t)
            slot = lax.broadcasted_iota(jnp.int32, (cap, t), 0).astype(F32)
            for el in range(2):
                mine = (me * 2 + el).astype(F32)
                q = jnp.sum(jnp.where(ex == mine, sl + 1.0, 0.0), axis=0, keepdims=True) - 1.0
                pm[pl.ds(el * cap, cap)] = jnp.where(slot == q, 1.0, 0.0).astype(BF16)
            wide = min(512, d)
            for m in range(d // wide):
                cols = pl.ds(m * wide, wide)
                got = jnp.dot(pm[...], u[cc, :t, cols], preferred_element_type=F32).astype(BF16)
                for el in range(2):
                    xs[el, pl.ds(pl.multiple_of(cc * cap, 16), cap), cols] = got[el * cap:(el + 1) * cap]

        @pl.when(k + 1 < steps)
        def _():
            u_copy(k + 1).start()

        @pl.loop(0, 2)
        def _(el):
            it = 2 * k + el
            s = it % slots

            @pl.when(it >= 1)
            def _():
                send(it - 1)

            @pl.when(it >= 1 + lag)
            def _():
                forward(it - 1 - lag)

            @pl.when(it >= slots)
            def _():
                wait_sent(s)

            @pl.when(k == 0)
            def _():
                pltpu.make_async_copy(w13.at[el], w13.at[el], wsem.at[el]).wait()
                pltpu.make_async_copy(w2.at[el], w2.at[el], w2sem.at[el]).wait()

            group = 2
            for j in range(0, f // 128, group):
                g = min(group, f // 128 - j)
                a = jnp.dot(xs[el], w13[el, :, pl.ds(256 * j, 256 * g)], preferred_element_type=F32)
                for i in range(g):
                    a1, a3 = a[:, 256 * i:256 * i + 128], a[:, 256 * i + 128:256 * i + 256]
                    h[:, pl.ds(128 * (j + i), 128)] = (jax.nn.silu(a1) * a3).astype(BF16)
            wide = min(512, d)
            for m in range(d // wide):
                cols = pl.ds(m * wide, wide)
                ys[s, :, cols] = jnp.dot(h[...], w2[el, :, cols], preferred_element_type=F32).astype(BF16)

    send(total - 1)
    for s in range(slots):
        wait_sent(s)
    pltpu.make_async_copy(rl, rl, fsem).wait()
    got = r_out.at[:, :, pl.ds(0, (CORES * side - 1) * 2 * cap)]
    pltpu.make_async_copy(got, got, rsem).wait()


def _k2(n, cap, keep, ug, r, z, out, rb, mr, mt, pma, pmb, sb, rx2, rxf, zb, ob, lsem, msem, ssem, r2sem, rfsem, zsem, osem):
    side, me, x, y, c = _place(n)
    kk, dh = rb.shape[1], rb.shape[2]
    tile = zb.shape[1]
    t = 4 * tile
    experts = kk // cap
    units = 16
    sending = 12
    far = side // 2

    def role(w):
        q, half, b = w // 4, w % 4 // 2, w % 2
        first = 1 - (q + 3) // 4
        middle = (q + 1) // 2 % 2
        off = first * far + middle * (1 + (side - 2) * b)
        return half, off, b + middle * (q % 2) * (1 - 2 * b)

    def at(half, off):
        return ((y + half * off) % side * side + (x + (1 - half) * off) % side) * CORES + c

    def line(half, off):
        return (x * (1 - half) + y * half + off) % side

    def load(w):
        half, off, _ = role(w)
        return pltpu.make_async_copy(r.at[half, line(half, off)], rb.at[w % 2], lsem.at[w % 2])

    load(0).start()
    for half in range(2):
        for off in range(side):
            pltpu.make_async_copy(ug.at[at(half, off), pl.ds(t, mr.shape[2])], mr.at[half, off], msem).start()

    barrier = pltpu.get_barrier_semaphore()
    for half in range(2):
        for off in (1, side - 1):
            pl.semaphore_signal(barrier, inc=1, device_id={'ep': at(half, off)}, device_id_type=MESH)
    pl.semaphore_wait(barrier, 4)
    pltpu.make_async_copy(mr, mr, msem).wait()

    def prepare(w):
        half, off, mh = role(w)
        hf = half.astype(F32) if hasattr(half, 'astype') else float(half)
        ex, sl, g = _routing(mr[half, off], t)
        cy = jnp.floor(ex * (1.0 / (2 * CORES * side)))
        cx = jnp.floor((ex - cy * (2 * CORES * side)) * (1.0 / (2 * CORES)))
        low = ex - cy * (2 * CORES * side) - cx * (2 * CORES)
        mine = x.astype(F32) * (1.0 - hf) + y.astype(F32) * hf
        across = cx * (1.0 - hf) + cy * hf
        along = cy * (1.0 - hf) + cx * hf
        e = jnp.where(across == mine, along * (2 * CORES) + low, -1.0)
        gap = jnp.zeros((2, t), F32)
        m = jnp.concatenate([e, gap, sl, gap, g, jnp.zeros((106, t), F32)], axis=0)
        for i in range(2):
            @pl.when(mh == i)
            def _():
                mt[w % 2] = m[:, i * 2 * tile:(i + 1) * 2 * tile].T

    def build(pm, w, i):
        rows = mt[w % 2, pl.ds(i * tile, tile)]
        lane = lax.broadcasted_iota(jnp.int32, (tile, 128), 1).astype(F32)
        slot = jnp.zeros((tile, 128), F32)
        gate = jnp.zeros((tile, 128), F32)
        for j in range(6):
            hit = lane == rows[:, j:j + 1]
            slot = slot + jnp.where(hit, rows[:, 8 + j:9 + j] + 4096.0, 0.0)
            gate = gate + jnp.where(hit, rows[:, 16 + j:17 + j], 0.0)
        slot = slot - 4096.0
        for k0 in range(0, kk, 128):
            v = jnp.zeros((tile, 128), F32)
            for e in range(k0 // cap, min(experts - 1, (k0 + 127) // cap) + 1):
                s_e = slot[:, e:e + 1]
                v = jnp.where(lane + float(k0 - e * cap) == s_e, gate[:, e:e + 1], v)
            for p, part in enumerate(_parts(v)):
                pm[pl.ds(p * tile, tile), pl.ds(k0, 128)] = part

    def z_copy(half, m, i):
        return pltpu.make_async_copy(z.at[pl.ds(m * tile, tile), pl.ds(half * dh, dh)], zb.at[i], zsem.at[i])

    def o_copy(half, m, i):
        return pltpu.make_async_copy(ob.at[i], out.at[pl.ds(m * tile, tile), pl.ds(half * dh, dh)], osem.at[i])

    def send(w, i):
        half, off, mh = role(w)
        b = w % keep
        src = sb.at[b * 2 + i]

        def go(dst, sem, step):
            pltpu.make_async_remote_copy(src, dst, ssem.at[b], sem, device_id={'ep': at(half, step)}, device_id_type=MESH).start()

        @pl.when((off == far) & (mh == 0))
        def _():
            go(rx2.at[half, 0, i], r2sem.at[half, 0, i], 1)

        @pl.when((off == far) & (mh == 1))
        def _():
            go(rx2.at[half, 1, i], r2sem.at[half, 1, i], side - 1)

        @pl.when(off == 1)
        def _():
            go(rxf.at[half, 0, mh * 2 + i], rfsem.at[half, 0, mh * 2 + i], 1)

        @pl.when(off == side - 1)
        def _():
            go(rxf.at[half, 1, mh * 2 + i], rfsem.at[half, 1, mh * 2 + i], side - 1)

    def wait_recv(ref, sem):
        pltpu.make_async_copy(ref, ref, sem).wait()

    def wait_sent(b):
        sent = sb.at[pl.ds(b * 2, 2)]
        pltpu.make_async_copy(sent, sent, ssem.at[b]).wait()

    prepare(0)
    build(pma, 0, 0)

    @pl.loop(0, units)
    def _(w):
        half, off, mh = role(w)
        after = w + 1 - (w + 1) // units
        load(w).wait()

        @pl.when(w + 1 < units)
        def _():
            load(w + 1).start()

        @pl.when(w + 1 < units)
        def _():
            prepare(w + 1)

        @pl.when((w >= keep) & (w < sending))
        def _():
            wait_sent(w % keep)

        @pl.when(off == 0)
        def _():
            for i in range(2):
                z_copy(half, mh * 2 + i, i).start()

        own = w // sending
        for i, pm in ((0, pma), (1, pmb)):
            here = (1 - own) * (w % keep * 2 + i) + own * (keep * 2)
            m = mh * 2 + i
            wide = min(512, dh)
            for j in range(dh // wide):
                cols = pl.ds(j * wide, wide)
                o = jnp.dot(pm[...], rb[w % 2, :, cols], preferred_element_type=F32)
                sb[here, :, cols] = o[:tile] + o[tile:2 * tile] + o[2 * tile:]
            if i == 0:
                build(pmb, w, 1)
            else:
                build(pma, after, 0)

            @pl.when((off == 1) & (mh == 0))
            def _():
                wait_recv(rx2.at[half, 0, i], r2sem.at[half, 0, i])
                sb[here] = sb[here] + rx2[half, 0, i]

            @pl.when((off == side - 1) & (mh == 1))
            def _():
                wait_recv(rx2.at[half, 1, i], r2sem.at[half, 1, i])
                sb[here] = sb[here] + rx2[half, 1, i]

            @pl.when(off == 0)
            def _():
                @pl.when(w > sending)
                def _():
                    o_copy(0, 0, i).wait()

                for way in range(2):
                    wait_recv(rxf.at[half, way, m], rfsem.at[half, way, m])
                z_copy(half, m, i).wait()
                total = zb[i] + (sb[here] + rxf[half, 0, m] + rxf[half, 1, m])
                ob[i] = total.astype(BF16)
                o_copy(half, m, i).start()

            @pl.when(w < sending)
            def _():
                send(w, i)

    for w in range(sending - keep, sending):
        wait_sent(w % keep)
    for i in range(2):
        o_copy(0, 0, i).wait()


def _experts(ug, ue1, ue3, ue2, n, cap, t):
    d, f = ug.shape[-1], ue1.shape[-1]
    side = math.isqrt(n // CORES)
    slots = 6
    any_ = pl.BlockSpec(memory_space=pl.ANY)
    flops = n * 2 * cap * (2 * t * d + 6 * d * f)
    return pl.pallas_call(
        functools.partial(_k1, n, cap, slots),
        out_shape=(
            jax.ShapeDtypeStruct((2, side, CORES * side * 2 * cap, d // 2), BF16),
            jax.ShapeDtypeStruct((2, CORES, side, 2, cap, d // 2), BF16),
        ),
        in_specs=[any_] * 4,
        out_specs=(any_, any_),
        scratch_shapes=[
            pltpu.VMEM((2, d, 2 * f), BF16),
            pltpu.VMEM((2, f, d), BF16),
            pltpu.VMEM((CORES, ug.shape[1], d), BF16),
            pltpu.VMEM((2 * cap, t), BF16),
            pltpu.VMEM((2, CORES * cap, d), BF16),
            pltpu.VMEM((CORES * cap, f), BF16),
            pltpu.VMEM((slots, CORES * cap, d), BF16),
            pltpu.SemaphoreType.DMA((2,)),
            pltpu.SemaphoreType.DMA((2,)),
            pltpu.SemaphoreType.DMA,
            pltpu.SemaphoreType.DMA((slots,)),
            pltpu.SemaphoreType.DMA,
            pltpu.SemaphoreType.DMA((2, CORES, side, 2)),
            pltpu.SemaphoreType.DMA,
        ],
        cost_estimate=pl.CostEstimate(flops=flops, bytes_accessed=4 * n * t * d, transcendentals=n * 2 * cap * f),
        compiler_params=pltpu.CompilerParams(collective_id=0, has_side_effects=True, vmem_limit_bytes=67043328),
        name='experts',
    )(ug, ue1, ue3, ue2)[0]


def _combine(ug, r, z, n, cap):
    t, d = z.shape
    dh = d // 2
    side = math.isqrt(n // CORES)
    tile = t // 4
    kk = r.shape[2]
    keep = 4
    any_ = pl.BlockSpec(memory_space=pl.ANY)
    return pl.pallas_call(
        functools.partial(_k2, n, cap, keep),
        out_shape=jax.ShapeDtypeStruct((t, d), BF16),
        in_specs=[any_, any_, any_],
        out_specs=any_,
        scratch_shapes=[
            pltpu.VMEM((2, kk, dh), BF16),
            pltpu.VMEM((2, side, EXTRA, d), BF16),
            pltpu.VMEM((2, 2 * tile, 128), F32),
            pltpu.VMEM((3 * tile, kk), BF16),
            pltpu.VMEM((3 * tile, kk), BF16),
            pltpu.VMEM((keep * 2 + 1, tile, dh), F32),
            pltpu.VMEM((2, 2, 2, tile, dh), F32),
            pltpu.VMEM((2, 2, 4, tile, dh), F32),
            pltpu.VMEM((2, tile, dh), F32),
            pltpu.VMEM((2, tile, dh), BF16),
            pltpu.SemaphoreType.DMA((2,)),
            pltpu.SemaphoreType.DMA,
            pltpu.SemaphoreType.DMA((keep,)),
            pltpu.SemaphoreType.DMA((2, 2, 2)),
            pltpu.SemaphoreType.DMA((2, 2, 4)),
            pltpu.SemaphoreType.DMA((2,)),
            pltpu.SemaphoreType.DMA((2,)),
        ],
        cost_estimate=pl.CostEstimate(flops=2 * side * 3 * 2 * t * kk * dh, bytes_accessed=2 * r.size, transcendentals=0),
        compiler_params=pltpu.CompilerParams(collective_id=1, has_side_effects=True, vmem_limit_bytes=67043328),
        name='combine',
    )(ug, r, z)


def _encode(gi, sl, gate):
    hi, mid, lo = (p.T for p in _parts(gate))
    left = jnp.concatenate([gi.T.astype(BF16), sl.T.astype(BF16), lo[:4]], axis=0)
    right = jnp.concatenate([hi, mid, lo[4:], jnp.zeros((2, gi.shape[0]), BF16)], axis=0)
    return jnp.concatenate([left, right], axis=1)


def solution(mesh):
    n = mesh.shape['ep']
    rows = P(('dp', 'ep'))
    rep = P()

    def local(h0, idx, slot, ln_attn, wq, wk, wv, wo, ln_ffn, ws1, ws3, ws2, ln_moe, wr, ue1, ue3, ue2):
        b, s, d = h0.shape
        top = idx.shape[-1]
        ne = ue1.shape[0] * n
        t = b * s
        cap = CAP_FACTOR * t * top // ne
        u = _rms(h0, ln_moe).reshape(t, d)
        gi, sl = idx.reshape(t, top), slot.reshape(t, top)
        gate = _gate(u, wr, gi)
        ug = lax.all_gather(jnp.concatenate([u, _encode(gi, sl, gate)], axis=0), 'ep')
        a, fo = _dense(h0, ln_attn, wq, wk, wv, wo, ln_ffn, ws1, ws3, ws2)
        z = (a.astype(F32) + fo).reshape(t, d)
        r = _experts(ug, ue1, ue3, ue2, n, cap, t)
        return _combine(ug, r, z, n, cap).reshape(b, s, d)

    specs = (rows, rows, rows) + (rep,) * 11 + (P('ep'), P('ep'), P('ep'))
    return jax.shard_map(local, mesh=mesh, in_specs=specs, out_specs=rows, check_vma=False)
```

time: 1140 us -> 985 us (0.86)
  Pallas kernels: 696 us -> 560 us
  other arithmetic: 36.2 us -> 19 us
    pallas_call x2, Pallas kernels: 696 us -> 560 us  [the longest x1 361 us: _experts(): pl.pallas_call(functools.partial(_k1, n, cap, slots), out_shape=(jax.Shap...]
  transfers between devices with their start and end apart: 1 -> 1, of which waited for: 1 -> 1; matrix products, arithmetic and copies ran while one was open for 18% -> 21% of each run, Pallas kernels for 0% -> 0%
where the time goes in v2:
time: 985 us; the launch traced here: 975 us
  Pallas kernels  560 us (57%)
  waiting for transfers between devices  174 us (18%)
  matrix products  168 us (17%)
  local copies, waits for them, and re-layouts  39.9 us (4%)
  other arithmetic  19 us (2%)
  between operations  13.9 us (1%)
    pallas_call x1, Pallas kernels, _experts(): pl.pallas_call(functools.partial(_k1, n, cap, slots), out_shape=(jax.Shap...  361 us
    pallas_call x1, Pallas kernels, _combine(): pl.pallas_call(functools.partial(_k2, n, cap, keep), out_shape=jax.ShapeD...  199 us
    all_gather x1, waiting for transfers between devices, local(): lax.all_gather(jnp.concatenate([u, _encode(gi, sl, gate)], axis=0), 'ep')  174 us
    dot_general x8, matrix products, _mm(): return jnp.einsum(form, a, b, preferred_element_type=jnp.float32)  134 us
    sub x1, matrix products, _dense(): jax.nn.softmax(jnp.where(causal, sc, -1e+30), axis=-1).astype(jnp.bfloat16)  33.5 us
    dot_general x2, local copies, waits for them, and re-layouts, _mm(): return jnp.einsum(form, a, b, preferred_element_type=jnp.float32)  24.6 us
  transfers between devices with their start and end apart: 1, of which 1 were waited for; matrix products, arithmetic and copies ran while one was open for 21% of the time, Pallas kernels for 0%

profile of v2, /device:TPU:97, one launch (start us, length us, event | category | flops | bytes accessed | tf_op | source)
XLA Modules:
  0.0 974.9 jit_solution(10738284389056451800)
XLA Ops:
  6.6 0.0 all-gather.3.cloned.1.call-start
  6.6 3.1 fusion.10
  9.7 0.7 convert_element_type.99
  10.4 3.2 fusion.19
  13.6 0.0 copy-start
  13.6 2.0 copy-done
  15.6 1.4 fusion.62
  17.0 0.2 select_reduce_fusion
  17.4 5.0 maximum_maximum_fusion
  22.4 0.1 all-gather.3.cloned.1.call-update
  22.5 12.3 %copy.38 = bf16[2048,2048]{1,0:T(8,128)(2,1)} copy(bf16[2048,2048]{0,1:T(8,128)(2,1)} %bitcast.85) | data formatting | bytes 16777216 | tf_op jit(solution)/shard_map/bsd,de->bse/dot_general | solution.py:22
  34.9 12.2 %copy.39 = bf16[2048,2048]{1,0:T(8,128)(2,1)} copy(bf16[2048,2048]{0,1:T(8,128)(2,1)} %bitcast.86) | data formatting | bytes 16777216 | tf_op jit(solution)/shard_map/bsd,de->bse/dot_general | solution.py:22
  47.1 13.9 %fusion.26 = bf16[1024,2048]{1,0:T(8,128)(2,1)} fusion(bf16[2048,2048]{1,0:T(8,128)(2,1)} %param.23, bf16[1,1024,2048]{2,1,0:T(8,128)(2,1)} %param.17, f32[2048]{0:T(1024)S(1)} %convert_element_type.111, f32[1024]{0:T(1024)S(1)} %add_rsqrt_fusion.1), kind=kOutput, calls=%fused_computation.43 | convolution fusion | flops 8600420352 | bytes 16789504 | tf_op jit(solution)/shard_map/bsd,de->bse/dot_general | solution.py:22
  61.0 6.4 copy.37
  67.4 0.6 convert_element_type.120
  68.0 0.3 iota_compare_fusion
  68.4 1.0 fusion.46
  69.3 0.0 copy-start.1
  69.4 12.9 %fusion.29 = f32[1,1024,16,128]{1,3,2,0:T(8,128)S(1)} fusion(bf16[16,128,2048]{2,1,0:T(8,128)(2,1)} %bitcast.88, bf16[1,1024,2048]{2,1,0:T(8,128)(2,1)} %param.17, f32[2048]{0:T(1024)S(1)} %convert_element_type.111, f32[1024]{0:T(1024)S(1)} %add_rsqrt_fusion.1), kind=kOutput, calls=%fused_computation.44 | convolution fusion | flops 8598323200 | bytes 20983808 | tf_op jit(solution)/shard_map/bsd,de->bse/dot_general | solution.py:22
  82.2 11.7 %fusion.32 = f32[1,1024,16,128]{1,3,2,0:T(8,128)S(1)} fusion(bf16[16,128,2048]{2,1,0:T(8,128)(2,1)} %bitcast.87, bf16[1,1024,2048]{2,1,0:T(8,128)(2,1)S(1)} %copy-done.1, f32[2048]{0:T(1024)S(1)} %convert_element_type.111, f32[1024]{0:T(1024)S(1)} %add_rsqrt_fusion.1), kind=kOutput, calls=%fused_computation.45 | convolution fusion | flops 8598323200 | bytes 20983808 | tf_op jit(solution)/shard_map/bsd,de->bse/dot_general | solution.py:22
  94.0 4.8 fusion.37
  98.7 33.5 %fusion.61 = (f32[16,1024]{1,0:T(8,128)S(1)}, f32[16,1024,1024]{1,2,0:T(8,128)}) fusion(pred[1024,1024]{0,1:T(8,128)(4,1)S(1)} %iota_compare_fusion, bf16[1024,16,64]{0,2,1:T(8,128)(2,1)} %get-tuple-element.11, bf16[1024,16,64]{0,2,1:T(8,128)(2,1)} %get-tuple-element.12, bf16[1024,16,64]{0,2,1:T(8,128)(2,1)} %get-tuple-element.8, ...), kind=kOutput, calls=%fused_computation.77 | convolution fusion | flops 4378854400 | bytes 76611584 | tf_op jit(solution)/shard_map/sub | solution.py:50
  132.3 25.5 %fusion.36 = bf16[16,128,1024]{2,1,0:T(8,128)(2,1)} fusion(bf16[1024,16,128]{0,2,1:T(8,128)(2,1)} %bitcast.89, f32[16,1024,1024]{1,2,0:T(8,128)} %get-tuple-element.20, f32[16,1024]{1,0:T(8,128)S(1)} %get-tuple-element.19), kind=kOutput, calls=%fused_computation.47 | convolution fusion | flops 4330618880 | bytes 75563008 | tf_op jit(solution)/shard_map/bhqk,bkhe->bqhe/dot_general | solution.py:22
  157.8 14.0 %fusion.12 = (f32[1024]{0:T(1024)S(1)}, bf16[1,1024,2048]{2,1,0:T(8,128)(2,1)S(1)}) fusion(bf16[1024,2048]{0,1:T(8,128)(2,1)} %bitcast.91, bf16[2048,2048]{1,0:T(8,128)(2,1)} %param.24, bf16[1,1024,2048]{2,1,0:T(8,128)(2,1)} %param.17), kind=kOutput, calls=%fused_computation.22 | convolution fusion | flops 8602516480 | bytes 20975616 | tf_op jit(solution)/shard_map/bse,ed->bsd/dot_general | solution.py:22
  171.8 0.0 copy-start.8
  171.8 2.0 copy-done.8
  173.8 17.7 %fusion.43 = f32[1024,2816]{1,0:T(8,128)} fusion(bf16[2048,2816]{1,0:T(8,128)(2,1)} %param.26, bf16[1,1024,2048]{2,1,0:T(8,128)(2,1)S(1)} %get-tuple-element.22, f32[2048]{0:T(1024)S(1)} %copy-done.5, f32[1024]{0:T(1024)S(1)} %add_rsqrt_fusion), kind=kOutput, calls=%fused_computation.54 | convolution fusion | flops 11819548672 | bytes 27275264 | tf_op jit(solution)/shard_map/bsd,df->bsf/dot_general | solution.py:22
  191.5 37.0 %fusion.15.z = f32[1024,2048]{1,0:T(8,128)} fusion(bf16[1,1024,2048]{2,1,0:T(8,128)(2,1)} %copy-done.8, bf16[2816,2048]{1,0:T(8,128)(2,1)} %param.28, f32[1024,2816]{1,0:T(8,128)} %fusion.43, bf16[2048,2816]{1,0:T(8,128)(2,1)} %param.27, f32[2048]{0:T(1024)S(1)} %copy-done.5, f32[1024]{0:T(1024)S(1)} %add_rsqrt_fusion), kind=kOutput, calls=%fused_computation.25 | convolution fusion | flops 23652204544 | bytes 47198208 | tf_op jit(solution)/shard_map/bsf,fd->bsd/dot_general | solution.py:22
  228.5 174.4 %all-gather.3.cloned.1.call-done = bf16[33280,2048]{1,0:T(8,128)(2,1)} async-done(((bf16[1040,2048]{1,0:T(8,128)(2,1)}), bf16[33280,2048]{1,0:T(8,128)(2,1)}) %all-gather.3.cloned.1.call-update) | async-done | bytes 136314896 | tf_op jit(solution)/shard_map/all_gather | solution.py:523
  402.9 361.3 %experts.1 = (bf16[2,4,3072,1024]{3,2,1,0:T(8,128)(2,1)}, bf16[2,2,4,2,192,1024]{5,4,3,2,1,0:T(8,128)(2,1)}) custom-call(bf16[32,1040,2048]{2,1,0:T(8,128)(2,1)} %bitcast.5.ug, bf16[2,2048,1408]{2,1,0:T(8,128)(2,1)} %ue1.1, bf16[2,2048,1408]{2,1,0:T(8,128)(2,1)} %ue3.1, bf16[2,1408,2048]{2,1,0:T(8,128)(2,1)} %ue2.1), custom_call_target="tpu_custom_call" | custom-call | flops 264140488704 | bytes 268435456 | tf_op jit(solution)/shard_map/experts/pallas_call | solution.py:434
  764.3 198.7 %combine.1 = bf16[1024,2048]{1,0:T(8,128)(2,1)} custom-call(bf16[32,1040,2048]{2,1,0:T(8,128)(2,1)} %bitcast.5.ug, bf16[2,4,3072,1024]{3,2,1,0:T(8,128)(2,1)} %get-tuple-element.6.r, f32[1024,2048]{1,0:T(8,128)} %fusion.15.z), custom_call_target="tpu_custom_call" | custom-call | flops 154618822656 | bytes 50331648 | tf_op jit(solution)/shard_map/combine/pallas_call | solution.py:472
  963.0 4.8 copy.48
  (25 shorter events, 0.2 us)
Async XLA Ops:
  6.5 9.1 copy-start.2
  6.5 10.5 %copy-start.3 = (s32[1,1024,6]{1,0,2:T(1,128)S(1)}, s32[1,1024,6]{1,0,2:T(1,128)}, u32[]{:S(2)}) copy-start(s32[1,1024,6]{1,0,2:T(1,128)} %param.18) | copy-start | bytes 73732
  6.6 10.5 %copy-start.4 = (s32[1,1024,6]{1,0,2:T(1,128)S(1)}, s32[1,1024,6]{1,0,2:T(1,128)}, u32[]{:S(2)}) copy-start(s32[1,1024,6]{1,0,2:T(1,128)} %param.19) | copy-start | bytes 73732
  6.6 396.4 %all-gather.3.cloned.1.call-start = ((), (), s32[]{:S(2)}) async-start(), calls=%async_computation | async-start | bytes 140574720 | tf_op jit(solution)/shard_map/all_gather | solution.py:523
  13.6 2.0 copy-start
  15.6 6.9 copy-start.6
  61.0 6.4 copy-start.7
  69.3 12.9 %copy-start.1 = (bf16[1,1024,2048]{2,1,0:T(8,128)(2,1)S(1)}, bf16[1,1024,2048]{2,1,0:T(8,128)(2,1)}, u32[]{:S(2)}) copy-start(bf16[1,1024,2048]{2,1,0:T(8,128)(2,1)} %param.17) | copy-start | bytes 12582916
  157.8 16.0 %copy-start.5 = (f32[2048]{0:T(1024)S(1)}, f32[2048]{0:T(1024)}, u32[]{:S(2)}) copy-start(f32[2048]{0:T(1024)} %convert_element_type.120) | copy-start | bytes 24580
  171.8 2.0 copy-start.8
Sparse Core Ops, SparseCore 0:
  22.6 380.2 all-gather.2

commit v3 on v0

v3 whole, which is shorter than its diff:
```python
import functools
import math

import jax
import jax.numpy as jnp
from jax import lax
from jax.experimental import pallas as pl
from jax.experimental.pallas import tpu as pltpu
from jax.sharding import PartitionSpec as P

HEAD = 128
EPS = 1e-6
CAP_FACTOR = 2
CORES = 2
EXTRA = 16
F32 = jnp.float32
BF16 = jnp.bfloat16
MESH = pl.DeviceIdType.MESH


def _mm(form, a, b):
    return jnp.einsum(form, a, b, preferred_element_type=jnp.float32)


def _rms(x, w):
    xf = x.astype(jnp.float32)
    r = lax.rsqrt(jnp.mean(xf * xf, axis=-1, keepdims=True) + EPS)
    return (xf * r * w.astype(jnp.float32)).astype(jnp.bfloat16)


def _rope(x):
    s, half = x.shape[1], x.shape[-1] // 2
    freq = 10000.0 ** (-jnp.arange(half, dtype=jnp.float32) / half)
    ang = jnp.arange(s, dtype=jnp.float32)[:, None] * freq[None, :]
    c = jnp.cos(ang)[None, :, None, :]
    sn = jnp.sin(ang)[None, :, None, :]
    x1, x2 = x[..., :half], x[..., half:]
    return jnp.concatenate([x1 * c - x2 * sn, x2 * c + x1 * sn], axis=-1)


def _dense(h0, ln_attn, wq, wk, wv, wo, ln_ffn, ws1, ws3, ws2):
    b, s, _ = h0.shape
    nh = wq.shape[1] // HEAD
    x1 = _rms(h0, ln_attn)
    q = _rope(_mm('bsd,de->bse', x1, wq).reshape(b, s, nh, HEAD)).astype(jnp.bfloat16)
    k = _rope(_mm('bsd,de->bse', x1, wk).reshape(b, s, nh, HEAD)).astype(jnp.bfloat16)
    v = _mm('bsd,de->bse', x1, wv).astype(jnp.bfloat16).reshape(b, s, nh, HEAD)
    sc = _mm('bqhe,bkhe->bhqk', q, k) * HEAD ** -0.5
    causal = jnp.arange(s)[:, None] >= jnp.arange(s)[None, :]
    p = jax.nn.softmax(jnp.where(causal, sc, -1e30), axis=-1).astype(jnp.bfloat16)
    o = _mm('bhqk,bkhe->bqhe', p, v).astype(jnp.bfloat16).reshape(b, s, nh * HEAD)
    a = (h0.astype(jnp.float32) + _mm('bse,ed->bsd', o, wo)).astype(jnp.bfloat16)
    x2 = _rms(a, ln_ffn)
    hs = (jax.nn.silu(_mm('bsd,df->bsf', x2, ws1)) * _mm('bsd,df->bsf', x2, ws3)).astype(jnp.bfloat16)
    return a, _mm('bsf,fd->bsd', hs, ws2)


def _gate(u, wr, gi):
    lg = _mm('td,de->te', u, wr)
    hit = gi[..., None] == jnp.arange(wr.shape[1], dtype=gi.dtype)
    return jax.nn.softmax(jnp.sum(jnp.where(hit, lg[:, None, :], 0.0), axis=-1), axis=-1)


def _parts(c):
    hi = c.astype(jnp.bfloat16)
    r = c - hi.astype(jnp.float32)
    mid = r.astype(jnp.bfloat16)
    lo = (r - mid.astype(jnp.float32)).astype(jnp.bfloat16)
    return hi, mid, lo


def _place(n):
    side = math.isqrt(n // CORES)
    me = lax.axis_index('ep')
    return side, me, (me // CORES) % side, me // (CORES * side), me % CORES


def _pick(table, k):
    power = (1 + 3 * (k % 2)) * (1 + 15 * (k // 2 % 2)) * (1 + 255 * (k // 4))
    return table // power % 4


def _pack(values):
    return sum(v * 4 ** i for i, v in enumerate(values))


STEP_X = (_pack((2, 2, 1, 0, 1, 1, 1, 0)), _pack((2, 2, 3, 0, 3, 3, 3, 0)))
STEP_Y = (_pack((2, 1, 2, 2, 1, 3, 0, 1)), _pack((0, 3, 2, 0, 3, 1, 0, 3)))
STEPS = 8


def _order(k, i):
    return _pick(STEP_X[i], k), _pick(STEP_Y[i], k)


def _routing(rows, t):
    e = rows.astype(F32)
    left, right = e[:, :t], e[:, t:]
    lo = jnp.concatenate([left[12:16], right[12:14]], axis=0)
    return left[0:6], left[6:12], right[0:6] + right[6:12] + lo


def _ffn(n, cap, ug, ue1, ue3, ue2, y_out, w13, w2, u, pm, xs, h, ys, wsem, w2sem, usem, ysem, before):
    side, me, x, y, c = _place(n)
    t, d = pm.shape[1], u.shape[2]
    f = h.shape[1]
    dh = d // 2

    def u_copy(k, i):
        dx, dy = _order(k, i)
        return pltpu.make_async_copy(ug.at[(y + dy) % side * side + (x + dx) % side], u.at[i], usem.at[i])

    def weights(el):
        for j in range(f // 128):
            pltpu.make_async_copy(ue1.at[el, :, pl.ds(128 * j, 128)], w13.at[el, :, pl.ds(256 * j, 128)], wsem.at[el]).start()
            pltpu.make_async_copy(ue3.at[el, :, pl.ds(128 * j, 128)], w13.at[el, :, pl.ds(256 * j + 128, 128)], wsem.at[el]).start()
        pltpu.make_async_copy(ue2.at[el], w2.at[el], w2sem.at[el]).start()

    def y_copies(k, el):
        return [
            pltpu.make_async_copy(
                ys.at[el, pl.ds(i * cap, cap), pl.ds(half * dh, dh)], y_out.at[2 * k + i, half, pl.ds(el * cap, cap)], ysem.at[el])
            for i in range(2) for half in range(2)
        ]

    def wait_kept(el):
        pltpu.make_async_copy(ys.at[el], ys.at[el], ysem.at[el]).wait()

    for i in range(2):
        u_copy(0, i).start()
    for el in range(2):
        weights(el)

    @pl.loop(0, STEPS)
    def _(k):
        before(k)

        @pl.loop(0, 2)
        def _(i):
            pltpu.make_async_copy(u.at[i], u.at[i], usem.at[i]).wait()
            ex, sl, _ = _routing(u[i, t:], t)
            slot = lax.broadcasted_iota(jnp.int32, (cap, t), 0).astype(F32)
            for el in range(2):
                mine = (me * 2 + el).astype(F32)
                q = jnp.sum(jnp.where(ex == mine, sl + 1.0, 0.0), axis=0, keepdims=True) - 1.0
                pm[pl.ds(el * cap, cap)] = jnp.where(slot == q, 1.0, 0.0).astype(BF16)
            wide = min(512, d)
            for m in range(d // wide):
                cols = pl.ds(m * wide, wide)
                got = jnp.dot(pm[...], u[i, :t, cols], preferred_element_type=F32).astype(BF16)
                for el in range(2):
                    xs[el, pl.ds(pl.multiple_of(i * cap, 16), cap), cols] = got[el * cap:(el + 1) * cap]

        @pl.when(k + 1 < STEPS)
        def _():
            for i in range(2):
                u_copy(k + 1, i).start()

        @pl.loop(0, 2)
        def _(el):
            @pl.when(k == 0)
            def _():
                pltpu.make_async_copy(w13.at[el], w13.at[el], wsem.at[el]).wait()
                pltpu.make_async_copy(w2.at[el], w2.at[el], w2sem.at[el]).wait()

            group = 2
            for j in range(0, f // 128, group):
                g = min(group, f // 128 - j)
                a = jnp.dot(xs[el], w13[el, :, pl.ds(256 * j, 256 * g)], preferred_element_type=F32)
                for i in range(g):
                    a1, a3 = a[:, 256 * i:256 * i + 128], a[:, 256 * i + 128:256 * i + 256]
                    h[:, pl.ds(128 * (j + i), 128)] = (jax.nn.silu(a1) * a3).astype(BF16)

            @pl.when(k >= 1)
            def _():
                wait_kept(el)

            wide = min(512, d)
            for m in range(d // wide):
                cols = pl.ds(m * wide, wide)
                ys[el, :, cols] = jnp.dot(h[...], w2[el, :, cols], preferred_element_type=F32).astype(BF16)
            for cp in y_copies(k, el):
                cp.start()

    for el in range(2):
        wait_kept(el)


def _ffn_scratch(t, d, f, cap):
    return [
        pltpu.VMEM((2, d, 2 * f), BF16),
        pltpu.VMEM((2, f, d), BF16),
        pltpu.VMEM((2, t + EXTRA, d), BF16),
        pltpu.VMEM((2 * cap, t), BF16),
        pltpu.VMEM((2, 2 * cap, d), BF16),
        pltpu.VMEM((2 * cap, f), BF16),
        pltpu.VMEM((2, 2 * cap, d), BF16),
    ]


FFN_SEMS = [pltpu.SemaphoreType.DMA((2,))] * 4


def _k1(n, cap, ug, ue1, ue3, ue2, y_out, *refs):
    _ffn(n, cap, ug, ue1, ue3, ue2, y_out, *refs, before=lambda k: None)


def _k2(n, cap, keep, ug0, ug1, y0, ue1, ue3, ue2, rxf, y1, r, rl, rx2, mr, wsem, w2sem, usem, ysem,
        ssem, rsem, relsem, fsem, lsem, msem, bsem, r2sem, rfsem):
    side, me, x, y, c = _place(n)
    t, d = rxf.shape[1], rxf.shape[2]
    f = ue1.shape[2]
    kk, dh = r.shape[2], r.shape[3]
    tile = rx2.shape[3]
    experts = kk // cap
    far = side // 2
    units = 16
    ys = (y0, y1)

    def device(axis, off, cc):
        return ((y + axis * off) % side * side + (x + (1 - axis) * off) % side) * CORES + cc

    def remote(src, dst, send_sem, recv_sem, dest):
        return pltpu.make_async_remote_copy(src, dst, send_sem, recv_sem, device_id={'ep': dest}, device_id_type=MESH)

    for p, ug in ((0, ug0), (1, ug1)):
        axis = (c + p) % 2
        for off in range(side):
            pltpu.make_async_copy(ug.at[device(axis, off, 0) // CORES, pl.ds(t, EXTRA)], mr.at[p, off], msem).start()

    barrier = pltpu.get_barrier_semaphore()
    peers = 0
    for off in range(side):
        for dc in range(CORES):
            for axis in range(2):
                if off or (dc and not axis):
                    pl.semaphore_signal(barrier, inc=1, device_id={'ep': device(axis, off, (c + dc) % CORES)}, device_id_type=MESH)
                    peers += 1
    pl.semaphore_wait(barrier, peers)

    def send(p, k, want_far):
        for i in range(2):
            dx, dy = _order(k, i)
            for half, off, other, mine, line in ((0, dy, dx, y, (x + dx) % side), (1, dx, dy, x, (y + dy) % side)):
                cc = (p + half) % 2
                src = ys[p].at[2 * k + i, half]

                def near():
                    own = (off == 0) & (c == cc)
                    dst = r.at[p, line, pl.ds((mine * CORES + c) * (2 * cap), 2 * cap)]

                    @pl.when(own)
                    def _():
                        pltpu.make_async_copy(src, dst, rsem.at[p, line]).start()

                    @pl.when(jnp.logical_not(own) & (off != far))
                    def _():
                        remote(src, dst, ssem.at[p], rsem.at[p, line], device(1 - half, off, cc)).start()

                def relayed():
                    @pl.when(off == far)
                    def _():
                        for el in range(2):
                            at = (p, half, el, other)
                            remote(src.at[pl.ds(el * cap, cap)], rl.at[at], ssem.at[p], relsem.at[at], device(1 - half, 1 - 2 * el, c)).start()

                if want_far != 0:
                    relayed()
                if want_far != 1:
                    near()

    def forward(p, other):
        for half, mine, line in ((0, y, (x + other) % side), (1, x, (y + other) % side)):
            for el in range(2):
                at = (p, half, el, other)
                step = 1 - 2 * el
                pltpu.make_async_copy(rl.at[at], rl.at[at], relsem.at[at]).wait()
                origin = (mine - step + side) % side
                dst = r.at[p, line, pl.ds((origin * CORES + c) * (2 * cap) + el * cap, cap)]
                remote(rl.at[at], dst, fsem.at[p], rsem.at[p, line], device(1 - half, step, (p + half) % 2)).start()

    for want in (1, 0):
        @pl.loop(0, STEPS)
        def _(k):
            send(0, k, want)

    def before(k):
        @pl.when(k == 2)
        def _():
            @pl.loop(0, side)
            def _(other):
                forward(0, other)

        @pl.when((k >= 2) & (k < 6))
        def _():
            send(1, k - 2, 2)

    def experts_phase(*refs):
        _ffn(n, cap, ug1, ue1, ue3, ue2, y1, *refs, wsem, w2sem, usem, ysem, before=before)

    pl.run_scoped(experts_phase, *_ffn_scratch(t, d, f, cap))

    def role(w):
        p, q, b = w // 8, w % 8 // 2, w % 2
        first = 1 - (q + 3) // 4
        middle = (q + 1) // 2 % 2
        off = first * far + middle * (1 + (side - 2) * b)
        return p, (c + p) % 2, off, b + middle * (q % 2) * (1 - 2 * b)

    def combine_phase(rb, mt, pma, pmb, sb):
        def load(w):
            p, axis, off, _ = role(w)
            line = (x * (1 - axis) + y * axis + off) % side
            return r.at[p, line], rsem.at[p, line], pltpu.make_async_copy(r.at[p, line], rb.at[w % 2], lsem.at[w % 2])

        def start_load(w):
            rows, sem, copy = load(w)
            q, b = w % 8 // 2, w % 2

            @pl.when((q == 1) | ((b == 0) & (q != 2)))
            def _():
                pltpu.make_async_copy(rows, rows, sem).wait()

            copy.start()

        def prepare(w):
            p, axis, off, mh = role(w)
            af = axis.astype(F32)
            ex, sl, g = _routing(mr[p, off], t)
            cy = jnp.floor(ex * (1.0 / (2 * CORES * side)))
            cx = jnp.floor((ex - cy * (2 * CORES * side)) * (1.0 / (2 * CORES)))
            low = ex - cy * (2 * CORES * side) - cx * (2 * CORES)
            mine = x.astype(F32) * (1.0 - af) + y.astype(F32) * af
            across = cx * (1.0 - af) + cy * af
            along = cy * (1.0 - af) + cx * af
            e = jnp.where(across == mine, along * (2 * CORES) + low, -1.0)
            gap = jnp.zeros((2, t), F32)
            m = jnp.concatenate([e, gap, sl, gap, g, jnp.zeros((106, t), F32)], axis=0)
            for i in range(2):
                @pl.when(mh == i)
                def _():
                    mt[w % 2] = m[:, i * 2 * tile:(i + 1) * 2 * tile].T

        def build(pm, w, i):
            rows = mt[w % 2, pl.ds(i * tile, tile)]
            lane = lax.broadcasted_iota(jnp.int32, (tile, 128), 1).astype(F32)
            slot = jnp.zeros((tile, 128), F32)
            gate = jnp.zeros((tile, 128), F32)
            for j in range(6):
                hit = lane == rows[:, j:j + 1]
                slot = slot + jnp.where(hit, rows[:, 8 + j:9 + j] + 4096.0, 0.0)
                gate = gate + jnp.where(hit, rows[:, 16 + j:17 + j], 0.0)
            slot = slot - 4096.0
            for k0 in range(0, kk, 128):
                v = jnp.zeros((tile, 128), F32)
                for e in range(k0 // cap, min(experts - 1, (k0 + 127) // cap) + 1):
                    v = jnp.where(lane + float(k0 - e * cap) == slot[:, e:e + 1], gate[:, e:e + 1], v)
                for i_part, part in enumerate(_parts(v)):
                    pm[pl.ds(i_part * tile, tile), pl.ds(k0, 128)] = part

        def send_sum(w, i):
            p, axis, off, mh = role(w)
            b = w % keep
            src = sb.at[b * 2 + i]
            rows = pl.ds((mh * 2 + i) * tile, tile)
            out = [rxf.at[j, rows, pl.ds(pl.multiple_of(axis * dh, dh), dh)] for j in range(3)]

            for way in range(2):
                step = 1 - 2 * way

                @pl.when((off == far) & (mh == way))
                def _():
                    remote(src, rx2.at[p, way, i], bsem.at[b], r2sem.at[p, way, i], device(axis, step, c)).start()

                @pl.when(off == (side + step) % side)
                def _():
                    remote(src, out[way], bsem.at[b], rfsem.at[way], device(axis, step, p)).start()

            @pl.when((off == 0) & (axis == 0))
            def _():
                pltpu.make_async_copy(src, out[2], bsem.at[b]).start()

            @pl.when((off == 0) & (axis == 1))
            def _():
                remote(src, out[2], bsem.at[b], rfsem.at[2], device(axis, 0, p)).start()

        def wait_sent(b):
            sent = sb.at[pl.ds(b * 2, 2)]
            pltpu.make_async_copy(sent, sent, bsem.at[b]).wait()

        pltpu.make_async_copy(mr, mr, msem).wait()
        start_load(0)
        prepare(0)
        build(pma, 0, 0)

        @pl.loop(0, units)
        def _(w):
            p, axis, off, mh = role(w)
            after = w + 1 - (w + 1) // units
            load(w)[2].wait()

            @pl.when(w + 1 < units)
            def _():
                start_load(w + 1)
                prepare(w + 1)

            @pl.when(w == 2)
            def _():
                forward(1, far)

                @pl.loop(4, STEPS)
                def _(k):
                    send(1, k, 0)

            @pl.when(w == 4)
            def _():
                for other in range(side):
                    if other != far:
                        forward(1, other)

            @pl.when(w >= keep)
            def _():
                wait_sent(w % keep)

            for i, pm in ((0, pma), (1, pmb)):
                here = w % keep * 2 + i
                wide = min(512, dh)
                for j in range(dh // wide):
                    cols = pl.ds(j * wide, wide)
                    o = jnp.dot(pm[...], rb[w % 2, :, cols], preferred_element_type=F32)
                    sb[here, :, cols] = o[:tile] + o[tile:2 * tile] + o[2 * tile:]
                if i == 0:
                    build(pmb, w, 1)
                else:
                    build(pma, after, 0)

                for way in range(2):
                    @pl.when((off == (side + 1 - 2 * way) % side) & (mh == way))
                    def _():
                        got = rx2.at[p, way, i]
                        pltpu.make_async_copy(got, got, r2sem.at[p, way, i]).wait()
                        sb[here] = sb[here] + rx2[p, way, i]

                send_sum(w, i)

        for w in range(units - keep, units):
            wait_sent(w % keep)

    pl.run_scoped(
        combine_phase,
        pltpu.VMEM((2, kk, dh), BF16),
        pltpu.VMEM((2, 2 * tile, 128), F32),
        pltpu.VMEM((3 * tile, kk), BF16),
        pltpu.VMEM((3 * tile, kk), BF16),
        pltpu.VMEM((keep * 2, tile, dh), F32),
    )

    for p in range(2):
        blocks = ys[p].at[pl.ds(0, 2 * STEPS - 2)]
        pltpu.make_async_copy(blocks, blocks, ssem.at[p]).wait()
        pltpu.make_async_copy(rl.at[p], rl.at[p], fsem.at[p]).wait()
    for j, got in enumerate((rxf.at[0], rxf.at[1], rxf.at[2, :, pl.ds(dh, dh)])):
        pltpu.make_async_copy(got, got, rfsem.at[j]).wait()


ANY = pl.BlockSpec(memory_space=pl.ANY)


def _experts(ug, ue1, ue3, ue2, n, cap, t):
    d, f = ug.shape[-1], ue1.shape[-1]
    return pl.pallas_call(
        functools.partial(_k1, n, cap),
        out_shape=jax.ShapeDtypeStruct((2 * STEPS, 2, 2 * cap, d // 2), BF16),
        in_specs=[ANY] * 4,
        out_specs=ANY,
        scratch_shapes=_ffn_scratch(t, d, f, cap) + FFN_SEMS,
        cost_estimate=pl.CostEstimate(flops=n * cap * (2 * t * d + 6 * d * f), bytes_accessed=2 * n * t * d, transcendentals=n * cap * f),
        compiler_params=pltpu.CompilerParams(vmem_limit_bytes=67043328),
        name='experts',
    )(ug, ue1, ue3, ue2)


def _exchange(ug0, ug1, y0, ue1, ue3, ue2, n, cap, t):
    d, f = ug0.shape[-1], ue1.shape[-1]
    dh = d // 2
    side = math.isqrt(n // CORES)
    tile = t // 4
    kk = CORES * side * 2 * cap
    keep = 4
    flops = n * cap * (2 * t * d + 6 * d * f) + 2 * side * 3 * 2 * t * kk * dh
    return pl.pallas_call(
        functools.partial(_k2, n, cap, keep),
        out_shape=(
            jax.ShapeDtypeStruct((3, t, d), F32),
            jax.ShapeDtypeStruct(y0.shape, BF16),
            jax.ShapeDtypeStruct((2, side, kk, dh), BF16),
            jax.ShapeDtypeStruct((2, 2, 2, side, cap, dh), BF16),
        ),
        in_specs=[ANY] * 6,
        out_specs=(ANY,) * 4,
        scratch_shapes=[
            pltpu.VMEM((2, 2, 2, tile, dh), F32),
            pltpu.VMEM((2, side, EXTRA, d), BF16),
        ] + FFN_SEMS + [
            pltpu.SemaphoreType.DMA((2,)),
            pltpu.SemaphoreType.DMA((2, side)),
            pltpu.SemaphoreType.DMA((2, 2, 2, side)),
            pltpu.SemaphoreType.DMA((2,)),
            pltpu.SemaphoreType.DMA((2,)),
            pltpu.SemaphoreType.DMA,
            pltpu.SemaphoreType.DMA((keep,)),
            pltpu.SemaphoreType.DMA((2, 2, 2)),
            pltpu.SemaphoreType.DMA((3,)),
        ],
        cost_estimate=pl.CostEstimate(flops=flops, bytes_accessed=4 * n * t * d, transcendentals=n * cap * f),
        compiler_params=pltpu.CompilerParams(collective_id=0, has_side_effects=True, vmem_limit_bytes=67043328),
        name='exchange',
    )(ug0, ug1, y0, ue1, ue3, ue2)[0]


def _encode(gi, sl, gate):
    hi, mid, lo = (p.T for p in _parts(gate))
    left = jnp.concatenate([gi.T.astype(BF16), sl.T.astype(BF16), lo[:4]], axis=0)
    right = jnp.concatenate([hi, mid, lo[4:], jnp.zeros((2, gi.shape[0]), BF16)], axis=0)
    return jnp.concatenate([left, right], axis=1)


def solution(mesh):
    n = mesh.shape['ep']
    rows = P(('dp', 'ep'))
    rep = P()

    def local(h0, idx, slot, ln_attn, wq, wk, wv, wo, ln_ffn, ws1, ws3, ws2, ln_moe, wr, ue1, ue3, ue2):
        b, s, d = h0.shape
        top = idx.shape[-1]
        ne = ue1.shape[0] * n
        t = b * s
        cap = CAP_FACTOR * t * top // ne
        u = _rms(h0, ln_moe).reshape(t, d)
        gi, sl = idx.reshape(t, top), slot.reshape(t, top)
        gate = _gate(u, wr, gi)
        mine = jnp.concatenate([u, _encode(gi, sl, gate)], axis=0)
        part = mine.shape[0] // CORES
        c = lax.axis_index('ep') % CORES
        kept = lax.dynamic_slice_in_dim(mine, c * part, part)
        given = lax.dynamic_slice_in_dim(mine, (1 - c) * part, part)
        taken = lax.ppermute(given, 'ep', [(i, i ^ 1) for i in range(n)])
        ug0 = lax.all_gather(jnp.where(c == 0, kept, taken), 'ep').reshape(n // CORES, -1, d)
        ug1 = lax.all_gather(jnp.where(c == 0, taken, kept), 'ep').reshape(n // CORES, -1, d)
        a, fo = _dense(h0, ln_attn, wq, wk, wv, wo, ln_ffn, ws1, ws3, ws2)
        z = (a.astype(F32) + fo).reshape(t, d)
        ug0, z = lax.optimization_barrier((ug0, z))
        y0 = _experts(ug0, ue1, ue3, ue2, n, cap, t)
        r = _exchange(ug0, ug1, y0, ue1, ue3, ue2, n, cap, t)
        return (z + (r[0] + r[1] + r[2])).astype(BF16).reshape(b, s, d)

    specs = (rows, rows, rows) + (rep,) * 11 + (P('ep'), P('ep'), P('ep'))
    return jax.shard_map(local, mesh=mesh, in_specs=specs, out_specs=rows, check_vma=False)
```

time: 2010 us -> 909 us (0.45)
  the two profiles are of different devices: /device:TPU:123 before, /device:TPU:97 now
where the time goes in v3:
time: 909 us; the launch traced here: 901 us
  Pallas kernels  608 us (67%)
  matrix products  168 us (18%)
  other arithmetic  48.6 us (5%)
  local copies, waits for them, and re-layouts  38.5 us (4%)
  waiting for transfers between devices  22.1 us (2%)
  between operations  14.1 us (2%)
    pallas_call x1, Pallas kernels, _exchange(): pl.pallas_call(functools.partial(_k2, n, cap, keep), out_shape=(jax.Shape...  432 us
    pallas_call x1, Pallas kernels, _experts(): pl.pallas_call(functools.partial(_k1, n, cap), out_shape=jax.ShapeDtypeSt...  176 us
    dot_general x8, matrix products, _mm(): return jnp.einsum(form, a, b, preferred_element_type=jnp.float32)  134 us
    sub x1, matrix products, _dense(): jax.nn.softmax(jnp.where(causal, sc, -1e+30), axis=-1).astype(jnp.bfloat16)  33.5 us
    dot_general x2, local copies, waits for them, and re-layouts, _mm(): return jnp.einsum(form, a, b, preferred_element_type=jnp.float32)  24.6 us
  transfers between devices with their start and end apart: 3, of which 2 were waited for; matrix products, arithmetic and copies ran while one was open for 23% of the time, Pallas kernels for 20%

profile of v3, /device:TPU:97, one launch (start us, length us, event | category | flops | bytes accessed | tf_op | source)
XLA Modules:
  0.0 901.0 jit_solution(11511703494583095094)
XLA Ops:
  6.6 3.1 fusion.10
  9.7 0.7 convert_element_type.102
  10.4 0.8 convert_bitcast_fusion
  11.1 3.2 fusion.21
  14.4 2.0 copy-done
  16.4 1.4 fusion.64
  18.2 14.5 %maximum_maximum_fusion = bf16[1040,2048]{1,0:T(8,128)(2,1)S(1)} fusion(bf16[2,1024]{1,0:T(2,128)(2,1)S(1)} %broadcast_in_dim.22, bf16[2,1024]{1,0:T(2,128)(2,1)S(1)} %slice.37, bf16[6,1024]{1,0:T(8,128)(2,1)S(1)} %get-tuple-element.19, bf16[6,1024]{1,0:T(8,128)(2,1)S(1)} %bitcast_convert_fusion, bf16[4,1024]{1,0:T(4,128)(2,1)S(1)} %slice.36, ...), kind=kLoop, calls=%fused_computation.29 | loop fusion | flops 34078720 | bytes 8519680 | tf_op jit(solution)/shard_map/concatenate | solution.py:542
  32.7 2.0 copy-done.1
  34.7 1.5 constant_dynamic-slice_fusion
  36.1 2.0 collective-permute-start
  38.2 3.8 collective-permute-done
  42.0 4.8 broadcast_select_fusion
  47.1 0.6 all-gather.7.cloned.1.call-update
  47.7 0.6 convert_element_type.123
  48.3 13.9 %fusion.28 = bf16[1024,2048]{1,0:T(8,128)(2,1)} fusion(bf16[2048,2048]{1,0:T(8,128)(2,1)} %param.23, bf16[1,1024,2048]{2,1,0:T(8,128)(2,1)} %param.17, f32[2048]{0:T(1024)S(1)} %convert_element_type.114, f32[1024]{0:T(1024)S(1)} %add_rsqrt_fusion.1), kind=kOutput, calls=%fused_computation.46 | convolution fusion | flops 8600420352 | bytes 16789504 | tf_op jit(solution)/shard_map/bsd,de->bse/dot_general | solution.py:22
  62.2 6.4 copy.37
  68.6 12.3 %copy.38 = bf16[2048,2048]{1,0:T(8,128)(2,1)} copy(bf16[2048,2048]{0,1:T(8,128)(2,1)} %bitcast.93) | data formatting | bytes 16777216 | tf_op jit(solution)/shard_map/bsd,de->bse/dot_general | solution.py:22
  80.9 12.3 %copy.39 = bf16[2048,2048]{1,0:T(8,128)(2,1)} copy(bf16[2048,2048]{0,1:T(8,128)(2,1)} %bitcast.94) | data formatting | bytes 16777216 | tf_op jit(solution)/shard_map/bsd,de->bse/dot_general | solution.py:22
  93.6 1.0 fusion.48
  94.6 12.9 %fusion.31 = f32[1,1024,16,128]{1,3,2,0:T(8,128)S(1)} fusion(bf16[16,128,2048]{2,1,0:T(8,128)(2,1)} %bitcast.96, bf16[1,1024,2048]{2,1,0:T(8,128)(2,1)} %param.17, f32[2048]{0:T(1024)S(1)} %convert_element_type.114, f32[1024]{0:T(1024)S(1)} %add_rsqrt_fusion.1), kind=kOutput, calls=%fused_computation.47 | convolution fusion | flops 8598323200 | bytes 20983808 | tf_op jit(solution)/shard_map/bsd,de->bse/dot_general | solution.py:22
  107.4 11.5 %fusion.34 = f32[1,1024,16,128]{1,3,2,0:T(8,128)S(1)} fusion(bf16[16,128,2048]{2,1,0:T(8,128)(2,1)} %bitcast.95, bf16[1,1024,2048]{2,1,0:T(8,128)(2,1)S(1)} %copy-done.2, f32[2048]{0:T(1024)S(1)} %convert_element_type.114, f32[1024]{0:T(1024)S(1)} %add_rsqrt_fusion.1), kind=kOutput, calls=%fused_computation.48 | convolution fusion | flops 8598323200 | bytes 20983808 | tf_op jit(solution)/shard_map/bsd,de->bse/dot_general | solution.py:22
  119.0 5.0 fusion.39
  123.9 33.5 %fusion.63 = (f32[16,1024]{1,0:T(8,128)S(1)}, f32[16,1024,1024]{1,2,0:T(8,128)}) fusion(pred[1024,1024]{0,1:T(8,128)(4,1)S(1)} %iota_compare_fusion, bf16[1024,16,64]{0,2,1:T(8,128)(2,1)} %get-tuple-element.17, bf16[1024,16,64]{0,2,1:T(8,128)(2,1)} %get-tuple-element.18, bf16[1024,16,64]{0,2,1:T(8,128)(2,1)} %get-tuple-element.12, ...), kind=kOutput, calls=%fused_computation.83 | convolution fusion | flops 4378854400 | bytes 76611584 | tf_op jit(solution)/shard_map/sub | solution.py:50
  157.5 25.1 %fusion.38 = bf16[16,128,1024]{2,1,0:T(8,128)(2,1)} fusion(bf16[1024,16,128]{0,2,1:T(8,128)(2,1)} %bitcast.97, f32[16,1024,1024]{1,2,0:T(8,128)} %get-tuple-element.26, f32[16,1024]{1,0:T(8,128)S(1)} %get-tuple-element.25), kind=kOutput, calls=%fused_computation.50 | convolution fusion | flops 4330618880 | bytes 75563008 | tf_op jit(solution)/shard_map/bhqk,bkhe->bqhe/dot_general | solution.py:22
  182.6 14.2 %fusion.12 = (f32[1024]{0:T(1024)S(1)}, bf16[1,1024,2048]{2,1,0:T(8,128)(2,1)S(1)}) fusion(bf16[1024,2048]{0,1:T(8,128)(2,1)} %bitcast.98, bf16[2048,2048]{1,0:T(8,128)(2,1)} %param.24, bf16[1,1024,2048]{2,1,0:T(8,128)(2,1)} %param.17), kind=kOutput, calls=%fused_computation.22 | convolution fusion | flops 8602516480 | bytes 20975616 | tf_op jit(solution)/shard_map/bse,ed->bsd/dot_general | solution.py:22
  196.9 2.0 copy-done.7
  198.9 17.7 %fusion.45 = f32[1024,2816]{1,0:T(8,128)} fusion(bf16[2048,2816]{1,0:T(8,128)(2,1)} %param.26, bf16[1,1024,2048]{2,1,0:T(8,128)(2,1)S(1)} %get-tuple-element.28, f32[2048]{0:T(1024)S(1)} %copy-done.4, f32[1024]{0:T(1024)S(1)} %add_rsqrt_fusion), kind=kOutput, calls=%fused_computation.59 | convolution fusion | flops 11819548672 | bytes 27275264 | tf_op jit(solution)/shard_map/bsd,df->bsf/dot_general | solution.py:22
  216.6 37.3 %fusion.15 = f32[1024,2048]{1,0:T(8,128)} fusion(bf16[1,1024,2048]{2,1,0:T(8,128)(2,1)} %copy-done.7, bf16[2816,2048]{1,0:T(8,128)(2,1)} %param.28, f32[1024,2816]{1,0:T(8,128)} %fusion.45, bf16[2048,2816]{1,0:T(8,128)(2,1)} %param.27, f32[2048]{0:T(1024)S(1)} %copy-done.4, f32[1024]{0:T(1024)S(1)} %add_rsqrt_fusion), kind=kOutput, calls=%fused_computation.25 | convolution fusion | flops 23652204544 | bytes 47198208 | tf_op jit(solution)/shard_map/bsf,fd->bsd/dot_general | solution.py:22
  253.8 176.4 %experts.1.y0 = bf16[16,2,384,1024]{3,2,1,0:T(8,128)(2,1)} custom-call(bf16[16,1040,2048]{2,1,0:T(8,128)(2,1)} %bitcast.5.ug.ug0, bf16[2,2048,1408]{2,1,0:T(8,128)(2,1)} %ue1.3, bf16[2,2048,1408]{2,1,0:T(8,128)(2,1)} %ue3.3, bf16[2,1408,2048]{2,1,0:T(8,128)(2,1)} %ue2.3), custom_call_target="tpu_custom_call" | custom-call | flops 132070244352 | bytes 134217728 | tf_op jit(solution)/shard_map/experts/pallas_call | solution.py:471
  430.3 17.6 %all-gather.7.cloned.1.call-done = bf16[16640,2048]{1,0:T(8,128)(2,1)} async-done(((bf16[520,2048]{1,0:T(8,128)(2,1)}), bf16[16640,2048]{1,0:T(8,128)(2,1)}) %all-gather.7.cloned.1.call-update) | async-done | bytes 68157456 | tf_op jit(solution)/shard_map/all_gather | solution.py:549
  447.9 431.5 %exchange.1 = (f32[3,1024,2048]{2,1,0:T(8,128)}, bf16[16,2,384,1024]{3,2,1,0:T(8,128)(2,1)}, bf16[2,4,3072,1024]{3,2,1,0:T(8,128)(2,1)}, bf16[2,2,2,4,192,1024]{5,4,3,2,1,0:T(8,128)(2,1)}) custom-call(bf16[16,1040,2048]{2,1,0:T(8,128)(2,1)} %bitcast.5.ug.ug0, bf16[16,1040,2048]{2,1,0:T(8,128)(2,1)} %bitcast.26.ug1, bf16[16,2,384,1024]{3,2,1,0:T(8,128)(2,1)} %experts.1.y0, ...), custom_call_target="tpu_custom_call" | custom-call | flops 286689067008 | bytes 268435456 | tf_op jit(solution)/shard_map/exchange/pallas_call | solution.py:491
  879.4 14.3 %fusion.19 = bf16[1,1024,2048]{2,1,0:T(8,128)(2,1)} fusion(f32[1024,2048]{1,0:T(8,128)} %fusion.15, f32[3,1024,2048]{2,1,0:T(8,128)} %get-tuple-element.10), kind=kLoop, calls=%fused_computation.30 | loop fusion | flops 8388608 | bytes 37748736 | tf_op jit(solution)/shard_map/reshape | solution.py:555
  (30 shorter events, 1.0 us)
Async XLA Ops:
  6.5 9.8 %copy-start.3 = (bf16[2048,64]{0,1:T(8,128)(2,1)S(1)}, bf16[2048,64]{0,1:T(8,128)(2,1)}, u32[]{:S(2)}) copy-start(bf16[2048,64]{0,1:T(8,128)(2,1)} %param.30) | copy-start | bytes 786436
  6.5 247.3 %all-gather.5.cloned.1.call-start = ((), (), s32[]{:S(2)}) async-start(), calls=%async_computation | async-start | bytes 70287360 | tf_op jit(solution)/shard_map/all_gather | solution.py:548
  14.4 2.0 copy-start
  32.7 2.0 copy-start.1
  34.7 13.0 %copy-start.5 = (bf16[2048]{0:T(1024)(128)(2,1)S(1)}, bf16[2048]{0:T(1024)(128)(2,1)}, u32[]{:S(2)}) copy-start(bf16[2048]{0:T(1024)(128)(2,1)} %param.20) | copy-start | bytes 12292
  34.7 13.0 %copy-start.6 = (bf16[2048]{0:T(1024)(128)(2,1)S(1)}, bf16[2048]{0:T(1024)(128)(2,1)}, u32[]{:S(2)}) copy-start(bf16[2048]{0:T(1024)(128)(2,1)} %param.25) | copy-start | bytes 12292
  36.1 5.9 collective-permute-start
  46.9 401.0 %all-gather.7.cloned.1.call-start = ((), (), s32[]{:S(2)}) async-start(), calls=%async_computation.1 | async-start | bytes 70287360 | tf_op jit(solution)/shard_map/all_gather | solution.py:549
  94.6 12.9 %copy-start.2 = (bf16[1,1024,2048]{2,1,0:T(8,128)(2,1)S(1)}, bf16[1,1024,2048]{2,1,0:T(8,128)(2,1)}, u32[]{:S(2)}) copy-start(bf16[1,1024,2048]{2,1,0:T(8,128)(2,1)} %param.17) | copy-start | bytes 12582916
  182.6 16.3 %copy-start.4 = (f32[2048]{0:T(1024)S(1)}, f32[2048]{0:T(1024)}, u32[]{:S(2)}) copy-start(f32[2048]{0:T(1024)} %convert_element_type.123) | copy-start | bytes 24580
  196.9 2.0 copy-start.7
Sparse Core Ops, SparseCore 0:
  47.0 201.1 all-gather.4
  250.3 197.5 all-gather.6

commit v4 on v3

v4 whole, which is shorter than its diff:
```python
import functools
import math

import jax
import jax.numpy as jnp
from jax import lax
from jax.experimental import pallas as pl
from jax.experimental.pallas import tpu as pltpu
from jax.sharding import PartitionSpec as P

HEAD = 128
LANES = 128
EPS = 1e-6
CAP_FACTOR = 2
CORES = 2
F32 = jnp.float32
BF16 = jnp.bfloat16
MESH = pl.DeviceIdType.MESH
BOTH = (0, 1)
SEM = pltpu.SemaphoreType.DMA
SEM2, SEM4 = SEM((2,)), SEM((4,))


def _mm(form, a, b):
    return jnp.einsum(form, a, b, preferred_element_type=jnp.float32)


def _rms(x, w):
    xf = x.astype(jnp.float32)
    r = lax.rsqrt(jnp.mean(xf * xf, axis=-1, keepdims=True) + EPS)
    return (xf * r * w.astype(jnp.float32)).astype(jnp.bfloat16)


def _rope(x):
    s, half = x.shape[1], x.shape[-1] // 2
    freq = 10000.0 ** (-jnp.arange(half, dtype=jnp.float32) / half)
    ang = jnp.arange(s, dtype=jnp.float32)[:, None] * freq[None, :]
    c = jnp.cos(ang)[None, :, None, :]
    sn = jnp.sin(ang)[None, :, None, :]
    x1, x2 = x[..., :half], x[..., half:]
    return jnp.concatenate([x1 * c - x2 * sn, x2 * c + x1 * sn], axis=-1)


def _dense(h0, ln_attn, wq, wk, wv, wo, ln_ffn, ws1, ws3, ws2):
    b, s, _ = h0.shape
    nh = wq.shape[1] // HEAD
    x1 = _rms(h0, ln_attn)
    q = _rope(_mm('bsd,de->bse', x1, wq).reshape(b, s, nh, HEAD)).astype(jnp.bfloat16)
    k = _rope(_mm('bsd,de->bse', x1, wk).reshape(b, s, nh, HEAD)).astype(jnp.bfloat16)
    v = _mm('bsd,de->bse', x1, wv).astype(jnp.bfloat16).reshape(b, s, nh, HEAD)
    sc = _mm('bqhe,bkhe->bhqk', q, k) * HEAD ** -0.5
    causal = jnp.arange(s)[:, None] >= jnp.arange(s)[None, :]
    p = jax.nn.softmax(jnp.where(causal, sc, -1e30), axis=-1).astype(jnp.bfloat16)
    o = _mm('bhqk,bkhe->bqhe', p, v).astype(jnp.bfloat16).reshape(b, s, nh * HEAD)
    a = (h0.astype(jnp.float32) + _mm('bse,ed->bsd', o, wo)).astype(jnp.bfloat16)
    x2 = _rms(a, ln_ffn)
    hs = (jax.nn.silu(_mm('bsd,df->bsf', x2, ws1)) * _mm('bsd,df->bsf', x2, ws3)).astype(jnp.bfloat16)
    return a, _mm('bsf,fd->bsd', hs, ws2)


def _parts(c):
    hi = c.astype(jnp.bfloat16)
    r = c - hi.astype(jnp.float32)
    mid = r.astype(jnp.bfloat16)
    lo = (r - mid.astype(jnp.float32)).astype(jnp.bfloat16)
    return hi, mid, lo


def _place(n):
    side = math.isqrt(n // CORES)
    me = lax.axis_index('ep')
    return side, me, (me // CORES) % side, me // (CORES * side), me % CORES


def _pick(table, k):
    power = (1 + 3 * (k % 2)) * (1 + 15 * (k // 2 % 2)) * (1 + 255 * (k // 4))
    return table // power % 4


def _pack(values):
    return sum(int(v) * 4 ** i for i, v in enumerate(values))


STEP_X = (_pack('22101110'), _pack('22303330'))
STEP_Y = (_pack('21221301'), _pack('03203103'))
STEPS = 8


def _order(k, i):
    return _pick(STEP_X[i], k), _pick(STEP_Y[i], k)


def _routing(rows, t):
    e = rows.astype(F32)
    half = t // 2

    def block(q):
        return jnp.concatenate([e[i][:, q * half:(q + 1) * half] for i in BOTH], axis=1)

    b = [block(q) for q in range(4)]
    lo = jnp.concatenate([b[0][6:], b[1][6:], b[2][6:]], axis=0)
    return b[0][:6], b[1][:6], b[2][:6] + b[3][:6] + lo


def _k0(n, h0, idx, slot, ln, wr, out0, out1, hb, ub, eb, hsem, lsem, ssem, rsem):
    side, me, x, y, c = _place(n)
    t = hb.shape[0]
    half, tile, ne = t // 2, t // 4, wr.shape[0]
    order = (1 - c, c)

    def h_copy(o, i):
        rows = pl.ds(pl.multiple_of((order[o] * 2 + i) * tile, tile), tile)
        return pltpu.make_async_copy(h0.at[rows], hb.at[pl.ds((o * 2 + i) * tile, tile)], hsem.at[o * 2 + i])

    for o in BOTH:
        for i in BOTH:
            h_copy(o, i).start()

    other = me + 1 - 2 * c
    barrier = pltpu.get_barrier_semaphore()
    pl.semaphore_signal(barrier, inc=1, device_id={'ep': other}, device_id_type=MESH)
    pl.semaphore_wait(barrier, 1)

    def gives(out):
        return [
            pltpu.make_async_remote_copy(src, out.at[rows], ssem.at[j], rsem.at[j], device_id={'ep': other}, device_id_type=MESH)
            for j, (src, rows) in enumerate(((ub.at[0], pl.ds(0, half)), (eb.at[0], pl.ds(half, 8))))
        ]

    def keeps(out):
        return [
            pltpu.make_async_copy(src, out.at[rows], lsem.at[j])
            for j, (src, rows) in enumerate(((ub.at[1], pl.ds(0, half)), (eb.at[1], pl.ds(half, 8))))
        ]

    w = ln[...].astype(F32)
    expert = lax.broadcasted_iota(jnp.int32, (ne, tile), 0)
    for o in BOTH:
        for i in BOTH:
            h_copy(o, i).wait()
            xf = hb[pl.ds((o * 2 + i) * tile, tile)].astype(F32)
            u = (xf * lax.rsqrt(jnp.mean(xf * xf, axis=-1, keepdims=True) + EPS) * w).astype(BF16)
            ub[o, pl.ds(i * tile, tile)] = u
            lg = lax.dot_general(wr[...], u, (((1,), (1,)), ((), ())), preferred_element_type=F32)
            cols = pl.ds(pl.multiple_of((order[o] * 2 + i) * tile, tile), tile)
            ex, sl = idx[:, cols], slot[:, cols]
            pick = [jnp.sum(jnp.where(expert == ex[j:j + 1], lg, 0.0), axis=0, keepdims=True) for j in range(6)]
            top = functools.reduce(jnp.maximum, pick)
            e = [jnp.exp(v - top) for v in pick]
            total = functools.reduce(jnp.add, e)
            parts = [_parts(v / total) for v in e]
            hi, mid, lo = ([p[q].astype(F32) for p in parts] for q in range(3))
            exf, slf = ex.astype(F32), sl.astype(F32)
            zero = jnp.zeros((1, tile), F32)
            blocks = ([exf] + lo[:2], [slf] + lo[2:4], hi + lo[4:], mid + [zero, zero])
            for q, rows in enumerate(blocks):
                eb[o, :, pl.ds(q * half + i * tile, tile)] = jnp.concatenate(rows, axis=0).astype(BF16)
        for p, out in enumerate((out0, out1)):
            @pl.when(c == p)
            def _():
                for cp in (gives(out) if o == 0 else keeps(out)):
                    cp.start()
    for cp in gives(out0) + keeps(out0):
        cp.wait()


def _ffn(n, cap, ugs, ue1, ue3, ue2, y_out, w13, w2, u, ur, pm, xs, h, ys, wsem, w2sem, usem, ysem, before):
    side, me, x, y, c = _place(n)
    t, d = pm.shape[1], u.shape[2]
    f = h.shape[1]
    dh, th = d // 2, t // 2

    def load_u(ug, k):
        for i in BOTH:
            dx, dy = _order(k, i)
            chip = (y + dy) % side * side + (x + dx) % side
            for j in BOTH:
                pltpu.make_async_copy(ug.at[chip, j, pl.ds(0, th)], u.at[i, pl.ds(j * th, th)], usem.at[i]).start()
                pltpu.make_async_copy(ug.at[chip, j, pl.ds(th, 8)], ur.at[i, j], usem.at[2 + i]).start()

    def weights(el):
        for j in range(f // LANES):
            pltpu.make_async_copy(ue1.at[el, :, pl.ds(LANES * j, LANES)], w13.at[el, :, pl.ds(256 * j, LANES)], wsem.at[el]).start()
            pltpu.make_async_copy(ue3.at[el, :, pl.ds(LANES * j, LANES)], w13.at[el, :, pl.ds(256 * j + LANES, LANES)], wsem.at[el]).start()
        pltpu.make_async_copy(ue2.at[el], w2.at[el], w2sem.at[el]).start()

    def keep(p, k, el):
        for i in BOTH:
            for half in BOTH:
                pltpu.make_async_copy(
                    ys.at[el, pl.ds(i * cap, cap), pl.ds(half * dh, dh)],
                    y_out.at[p, 2 * k + i, half, pl.ds(el * cap, cap)], ysem.at[el]).start()

    def wait_kept(el):
        pltpu.make_async_copy(ys.at[el], ys.at[el], ysem.at[el]).wait()

    load_u(ugs[0], 0)
    for el in BOTH:
        weights(el)

    @pl.loop(0, 2 * STEPS)
    def _(step):
        p, k = step // STEPS, step % STEPS
        before(step)

        @pl.when(step == STEPS)
        def _():
            load_u(ugs[1], 0)

        @pl.loop(0, 2)
        def _(i):
            pltpu.make_async_copy(u.at[i], u.at[i], usem.at[i]).wait()
            pltpu.make_async_copy(ur.at[i], ur.at[i], usem.at[2 + i]).wait()
            ex, sl, _ = _routing(ur[i], t)
            slot = lax.broadcasted_iota(jnp.int32, (cap, t), 0).astype(F32)
            for el in BOTH:
                mine = (me * 2 + el).astype(F32)
                q = jnp.sum(jnp.where(ex == mine, sl + 1.0, 0.0), axis=0, keepdims=True) - 1.0
                pm[pl.ds(el * cap, cap)] = jnp.where(slot == q, 1.0, 0.0).astype(BF16)
            wide = min(512, d)
            for m in range(d // wide):
                cols = pl.ds(m * wide, wide)
                got = jnp.dot(pm[...], u[i, :, cols], preferred_element_type=F32).astype(BF16)
                for el in BOTH:
                    xs[el, pl.ds(pl.multiple_of(i * cap, 16), cap), cols] = got[el * cap:(el + 1) * cap]

        @pl.when(step < STEPS - 1)
        def _():
            load_u(ugs[0], k + 1)

        @pl.when((step >= STEPS) & (step < 2 * STEPS - 1))
        def _():
            load_u(ugs[1], k + 1)

        @pl.loop(0, 2)
        def _(el):
            @pl.when(step == 0)
            def _():
                pltpu.make_async_copy(w13.at[el], w13.at[el], wsem.at[el]).wait()
                pltpu.make_async_copy(w2.at[el], w2.at[el], w2sem.at[el]).wait()

            group = 2
            for j in range(0, f // LANES, group):
                g = min(group, f // LANES - j)
                a = jnp.dot(xs[el], w13[el, :, pl.ds(256 * j, 256 * g)], preferred_element_type=F32)
                for i in range(g):
                    a1, a3 = a[:, 256 * i:256 * i + LANES], a[:, 256 * i + LANES:256 * i + 256]
                    h[:, pl.ds(LANES * (j + i), LANES)] = (jax.nn.silu(a1) * a3).astype(BF16)

            @pl.when(step >= 1)
            def _():
                wait_kept(el)

            wide = min(512, d)
            for m in range(d // wide):
                cols = pl.ds(m * wide, wide)
                ys[el, :, cols] = jnp.dot(h[...], w2[el, :, cols], preferred_element_type=F32).astype(BF16)
            keep(p, k, el)

    for el in BOTH:
        wait_kept(el)


def _ffn_scratch(t, d, f, cap):
    cap2 = 2 * cap
    return [
        pltpu.VMEM((2, d, 2 * f), BF16),
        pltpu.VMEM((2, f, d), BF16),
        pltpu.VMEM((2, t, d), BF16),
        pltpu.VMEM((2, 2, 8, d), BF16),
        pltpu.VMEM((cap2, t), BF16),
        pltpu.VMEM((2, cap2, d), BF16),
        pltpu.VMEM((cap2, f), BF16),
        pltpu.VMEM((2, cap2, d), BF16),
    ]


FFN_SEMS = [SEM2] * 2 + [SEM4, SEM2]


def _split(a, b):
    return a + ((b - a) // 8 + 1) // 2 * 8


BOTH_NEAR, BOTH_FAR = ((0, -1), (1, 1)), ((0, 2), (1, 2))
STAGE = {0: 1, -1: 2, 1: 3, 2: 4}


class _Gather:
    def __init__(self, n, own, out, send_sem, recv_sem, pair_sem):
        self.side, self.me, self.x, self.y, self.c = _place(n)
        self.own, self.out = own, out
        self.send_sem, self.recv_sem, self.pair_sem = send_sem, recv_sem, pair_sem
        rows = own.shape[0]
        mid = _split(0, rows)
        self.rows = ((0, mid), (mid, rows))

    def device(self, axis, off, cc):
        side = self.side
        return ((self.y + axis * off) % side * side + (self.x + (1 - axis) * off) % side) * CORES + cc

    def place(self, color, j, s, part=None):
        side = self.side
        dx, dy = (j, s) if color == 0 else (s, j)
        chip = (self.y + dy + side) % side * side + (self.x + dx + side) % side
        a, b = self.rows[color]
        if part is not None:
            mid = _split(a, b)
            a, b = (a, mid) if part == 0 else (mid, b)
        return self.out.at[chip, self.c, pl.ds(a, b - a)]

    def copy(self, color, src, dst, axis, way, sem):
        dest = self.device(axis, 1 - 2 * way, self.c)
        pltpu.make_async_remote_copy(src, dst, self.send_sem, sem, device_id={'ep': dest}, device_id_type=MESH).start()

    def share(self, src, dst):
        other = self.device(0, 0, 1 - self.c)
        pltpu.make_async_remote_copy(src, dst, self.pair_sem.at[0], self.pair_sem.at[1], device_id={'ep': other}, device_id_type=MESH).start()

    def wait(self, ref, sem):
        pltpu.make_async_copy(ref, ref, sem).wait()

    def start(self):
        for color in BOTH:
            a, b = self.rows[color]
            src, dst = self.own.at[pl.ds(a, b - a)], self.place(color, 0, 0)
            for stage in BOTH:
                for way in BOTH:
                    self.copy(color, src, dst, color if stage == 0 else 1 - color, way, self.recv_sem.at[color, stage, way])
            self.share(src, dst)

    def along(self, j):
        items = []
        for color in BOTH:
            for way, off in (BOTH_FAR if j == 2 else BOTH_NEAR):
                if j == 2:
                    self.wait(self.place(color, off, 0, way), self.recv_sem.at[color, 0, 2 + way])
                else:
                    self.wait(self.place(color, off, 0), self.recv_sem.at[color, 0, way])
                    half = self.place(color, off, 0, way)
                    self.copy(color, half, half, color, way, self.recv_sem.at[color, 0, 2 + way])
                    items.append((color, off))
            if j == 2:
                items.append((color, j))
        for color, off in items:
            item = self.place(color, off, 0)
            for way in BOTH:
                self.copy(color, item, item, 1 - color, way, self.recv_sem.at[color, STAGE[off], way])
            self.share(item, item)

    def across(self, offs):
        for color in BOTH:
            for off in offs:
                at = STAGE[off]
                for way, s in BOTH_NEAR:
                    item = self.place(color, off, s)
                    self.wait(item, self.recv_sem.at[color, at, way])
                    half = self.place(color, off, s, way)
                    self.copy(color, half, half, 1 - color, way, self.recv_sem.at[color, at, 2 + way])
                    self.share(item, item)

    def last(self, offs):
        for color in BOTH:
            for off in offs:
                at = STAGE[off]
                for way in BOTH:
                    self.wait(self.place(color, off, 2, way), self.recv_sem.at[color, at, 2 + way])
                item = self.place(color, off, 2)
                self.share(item, item)

    def finish(self):
        got = self.out.at[:, 0]
        self.wait(got, self.pair_sem.at[1])

    def drain(self):
        chips = self.out.shape[0]
        self.wait(self.out.at[:, 0], self.pair_sem.at[0])
        self.wait(self.out.at[pl.ds(0, chips - 1), 0], self.send_sem)


def _k2(n, cap, keep, ug0, part1, ue1, ue3, ue2, rxf, ug1, ys, r, rl, rx2, mr, wsem, w2sem, usem, ysem,
        gsem, grsem, pairsem, osem, ssem, rsem, relsem, fsem, lsem, msem, bsem, r2sem, rfsem):
    side, me, x, y, c = _place(n)
    t, d = rxf.shape[1], rxf.shape[2]
    f = ue1.shape[2]
    kk, dh = r.shape[2], r.shape[3]
    tile = rx2.shape[3]
    experts = kk // cap
    far = side // 2
    units = 16
    th, cap2 = t // 2, 2 * cap
    gather = _Gather(n, part1, ug1, gsem, grsem, pairsem)

    def device(axis, off, cc):
        return ((y + axis * off) % side * side + (x + (1 - axis) * off) % side) * CORES + cc

    def remote(src, dst, send_sem, recv_sem, dest):
        return pltpu.make_async_remote_copy(src, dst, send_sem, recv_sem, device_id={'ep': dest}, device_id_type=MESH)

    def routing_rows(p, ug):
        axis = (c + p) % 2
        for off in range(side):
            pltpu.make_async_copy(ug.at[device(axis, off, 0) // CORES, :, pl.ds(th, 8)], mr.at[p, off], msem).start()

    kept = pltpu.make_async_copy(part1, ug1.at[me // CORES, c], osem)
    kept.start()
    routing_rows(0, ug0)

    barrier = pltpu.get_barrier_semaphore()
    peers = 0
    for off in range(side):
        for dc in range(CORES):
            for axis in BOTH:
                if off or (dc and not axis):
                    pl.semaphore_signal(barrier, inc=1, device_id={'ep': device(axis, off, (c + dc) % CORES)}, device_id_type=MESH)
                    peers += 1
    pl.semaphore_wait(barrier, peers)

    def send(p, k, want_far):
        for i in BOTH:
            dx, dy = _order(k, i)
            for half, off, other, mine, line in ((0, dy, dx, y, (x + dx) % side), (1, dx, dy, x, (y + dy) % side)):
                cc = (p + half) % 2
                src = ys.at[p, 2 * k + i, half]

                def near():
                    own = (off == 0) & (c == cc)
                    dst = r.at[p, line, pl.ds((mine * CORES + c) * cap2, cap2)]

                    @pl.when(own)
                    def _():
                        pltpu.make_async_copy(src, dst, rsem.at[p, line]).start()

                    @pl.when(jnp.logical_not(own) & (off != far))
                    def _():
                        remote(src, dst, ssem.at[p], rsem.at[p, line], device(1 - half, off, cc)).start()

                def relayed():
                    @pl.when(off == far)
                    def _():
                        for el in BOTH:
                            at = (p, half, el, other)
                            remote(src.at[pl.ds(el * cap, cap)], rl.at[at], ssem.at[p], relsem.at[at], device(1 - half, 1 - 2 * el, c)).start()

                if want_far != 0:
                    relayed()
                if want_far != 1:
                    near()

    def forward(p, other):
        for half, mine, line in ((0, y, (x + other) % side), (1, x, (y + other) % side)):
            for el in BOTH:
                at = (p, half, el, other)
                step = 1 - 2 * el
                pltpu.make_async_copy(rl.at[at], rl.at[at], relsem.at[at]).wait()
                origin = (mine - step + side) % side
                dst = r.at[p, line, pl.ds((origin * CORES + c) * cap2 + el * cap, cap)]
                remote(rl.at[at], dst, fsem.at[p], rsem.at[p, line], device(1 - half, step, (p + half) % 2)).start()

    gather.start()

    def before(step):
        def at(s):
            return pl.when(step == s)

        @at(1)
        def _():
            gather.along(1)

        @at(2)
        def _():
            gather.across((0,))

        @at(4)
        def _():
            gather.along(2)

        @at(5)
        def _():
            gather.across((-1, 1))

        @at(6)
        def _():
            gather.last((0,))

        @at(7)
        def _():
            gather.across((2,))

            @pl.loop(0, 6)
            def _(k):
                send(0, k, 1)

            @pl.loop(0, 6)
            def _(k):
                send(0, k, 0)

        @at(8)
        def _():
            gather.last((-1, 1, 2))
            kept.wait()
            gather.finish()
            routing_rows(1, ug1)

        @pl.when((step == 8) | (step == 9))
        def _():
            send(0, step - 2, 0)

        @at(10)
        def _():
            @pl.loop(0, side)
            def _(other):
                forward(0, other)

        @pl.when((step >= 10) & (step < 14))
        def _():
            send(1, step - 10, 2)

    def experts_phase(*refs):
        _ffn(n, cap, (ug0, ug1), ue1, ue3, ue2, ys, *refs, wsem, w2sem, usem, ysem, before=before)

    pl.run_scoped(experts_phase, *_ffn_scratch(t, d, f, cap))

    def role(w):
        p, q, b = w // 8, w % 8 // 2, w % 2
        first = 1 - (q + 3) // 4
        middle = (q + 1) // 2 % 2
        off = first * far + middle * (1 + (side - 2) * b)
        return p, (c + p) % 2, off, b + middle * (q % 2) * (1 - 2 * b)

    def combine_phase(rb, mt, pma, pmb, sb):
        def load(w):
            p, axis, off, _ = role(w)
            line = (x * (1 - axis) + y * axis + off) % side
            return r.at[p, line], rsem.at[p, line], pltpu.make_async_copy(r.at[p, line], rb.at[w % 2], lsem.at[w % 2])

        def start_load(w):
            rows, sem, copy = load(w)
            q, b = w % 8 // 2, w % 2

            @pl.when((q == 1) | ((b == 0) & (q != 2)))
            def _():
                pltpu.make_async_copy(rows, rows, sem).wait()

            copy.start()

        def prepare(w):
            p, axis, off, mh = role(w)
            af = axis.astype(F32)
            ex, sl, g = _routing(mr[p, off], t)
            cy = jnp.floor(ex * (1.0 / (2 * CORES * side)))
            cx = jnp.floor((ex - cy * (2 * CORES * side)) * (1.0 / (2 * CORES)))
            low = ex - cy * (2 * CORES * side) - cx * (2 * CORES)
            mine = x.astype(F32) * (1.0 - af) + y.astype(F32) * af
            across = cx * (1.0 - af) + cy * af
            along = cy * (1.0 - af) + cx * af
            e = jnp.where(across == mine, along * (2 * CORES) + low, -1.0)
            gap = jnp.zeros((2, t), F32)
            m = jnp.concatenate([e, gap, sl, gap, g, jnp.zeros((106, t), F32)], axis=0)
            for i in BOTH:
                @pl.when(mh == i)
                def _():
                    mt[w % 2] = m[:, i * 2 * tile:(i + 1) * 2 * tile].T

        def build(pm, w, i):
            rows = mt[w % 2, pl.ds(i * tile, tile)]
            lane = lax.broadcasted_iota(jnp.int32, (tile, LANES), 1).astype(F32)
            slot = jnp.zeros((tile, LANES), F32)
            gate = jnp.zeros((tile, LANES), F32)
            for j in range(6):
                hit = lane == rows[:, j:j + 1]
                slot = slot + jnp.where(hit, rows[:, 8 + j:9 + j] + 4096.0, 0.0)
                gate = gate + jnp.where(hit, rows[:, 16 + j:17 + j], 0.0)
            slot = slot - 4096.0
            for k0 in range(0, kk, LANES):
                v = jnp.zeros((tile, LANES), F32)
                for e in range(k0 // cap, min(experts - 1, (k0 + 127) // cap) + 1):
                    v = jnp.where(lane + float(k0 - e * cap) == slot[:, e:e + 1], gate[:, e:e + 1], v)
                for i_part, part in enumerate(_parts(v)):
                    pm[pl.ds(i_part * tile, tile), pl.ds(k0, LANES)] = part

        def send_sum(w, i):
            p, axis, off, mh = role(w)
            b = w % keep
            src = sb.at[b * 2 + i]
            rows = pl.ds((mh * 2 + i) * tile, tile)
            out = [rxf.at[j, rows, pl.ds(pl.multiple_of(axis * dh, dh), dh)] for j in range(3)]

            for way in BOTH:
                step = 1 - 2 * way

                @pl.when((off == far) & (mh == way))
                def _():
                    remote(src, rx2.at[p, way, i], bsem.at[b], r2sem.at[p, way, i], device(axis, step, c)).start()

                @pl.when(off == (side + step) % side)
                def _():
                    remote(src, out[way], bsem.at[b], rfsem.at[way], device(axis, step, p)).start()

            @pl.when((off == 0) & (axis == 0))
            def _():
                pltpu.make_async_copy(src, out[2], bsem.at[b]).start()

            @pl.when((off == 0) & (axis == 1))
            def _():
                remote(src, out[2], bsem.at[b], rfsem.at[2], device(axis, 0, p)).start()

        def wait_sent(b):
            sent = sb.at[pl.ds(b * 2, 2)]
            pltpu.make_async_copy(sent, sent, bsem.at[b]).wait()

        pltpu.make_async_copy(mr, mr, msem).wait()
        start_load(0)
        prepare(0)
        build(pma, 0, 0)

        @pl.loop(0, units)
        def _(w):
            p, axis, off, mh = role(w)
            after = w + 1 - (w + 1) // units
            load(w)[2].wait()

            @pl.when(w + 1 < units)
            def _():
                start_load(w + 1)
                prepare(w + 1)

            @pl.when(w == 2)
            def _():
                forward(1, far)

                @pl.loop(4, STEPS)
                def _(k):
                    send(1, k, 0)

            @pl.when(w == 4)
            def _():
                for other in range(side):
                    if other != far:
                        forward(1, other)

            @pl.when(w >= keep)
            def _():
                wait_sent(w % keep)

            for i, pm in ((0, pma), (1, pmb)):
                here = w % keep * 2 + i
                wide = min(512, dh)
                for j in range(dh // wide):
                    cols = pl.ds(j * wide, wide)
                    o = jnp.dot(pm[...], rb[w % 2, :, cols], preferred_element_type=F32)
                    sb[here, :, cols] = o[:tile] + o[tile:2 * tile] + o[2 * tile:]
                if i == 0:
                    build(pmb, w, 1)
                else:
                    build(pma, after, 0)

                for way in BOTH:
                    @pl.when((off == (side + 1 - 2 * way) % side) & (mh == way))
                    def _():
                        got = rx2.at[p, way, i]
                        pltpu.make_async_copy(got, got, r2sem.at[p, way, i]).wait()
                        sb[here] = sb[here] + rx2[p, way, i]

                send_sum(w, i)

        for w in range(units - keep, units):
            wait_sent(w % keep)

    pl.run_scoped(
        combine_phase,
        pltpu.VMEM((2, kk, dh), BF16),
        pltpu.VMEM((2, 2 * tile, LANES), F32),
        pltpu.VMEM((3 * tile, kk), BF16),
        pltpu.VMEM((3 * tile, kk), BF16),
        pltpu.VMEM((keep * 2, tile, dh), F32),
    )

    gather.drain()
    for p in BOTH:
        blocks = ys.at[p, pl.ds(0, 2 * STEPS - 2)]
        pltpu.make_async_copy(blocks, blocks, ssem.at[p]).wait()
        pltpu.make_async_copy(rl.at[p], rl.at[p], fsem.at[p]).wait()
    for j, got in enumerate((rxf.at[0], rxf.at[1], rxf.at[2, :, pl.ds(dh, dh)])):
        pltpu.make_async_copy(got, got, rfsem.at[j]).wait()


ANY = pl.BlockSpec(memory_space=pl.ANY)


def _rows(h0, idx, slot, ln, wr, n):
    t, d = h0.shape
    vmem = pl.BlockSpec(memory_space=pltpu.VMEM)
    return pl.pallas_call(
        functools.partial(_k0, n),
        out_shape=(jax.ShapeDtypeStruct((t // 2 + 8, d), BF16),) * CORES,
        in_specs=[ANY] + [vmem] * 4,
        out_specs=(ANY,) * CORES,
        scratch_shapes=[
            pltpu.VMEM((t, d), BF16),
            pltpu.VMEM((2, t // 2, d), BF16),
            pltpu.VMEM((2, 8, d), BF16),
            SEM4,
            SEM2,
            SEM2,
            SEM2,
        ],
        cost_estimate=pl.CostEstimate(flops=2 * t * d * 64, bytes_accessed=8 * t * d, transcendentals=0),
        compiler_params=pltpu.CompilerParams(collective_id=1, has_side_effects=True),
        name='rows',
    )(h0, idx, slot, ln, wr)


def _exchange(ug0, part1, ue1, ue3, ue2, n, cap, t):
    d, f = part1.shape[-1], ue1.shape[-1]
    dh = d // 2
    side = math.isqrt(n // CORES)
    tile = t // 4
    kk = CORES * side * 2 * cap
    keep = 4
    cap2 = 2 * cap
    flops = 2 * n * cap * (2 * t * d + 6 * d * f) + 2 * side * 3 * 2 * t * kk * dh
    return pl.pallas_call(
        functools.partial(_k2, n, cap, keep),
        out_shape=(
            jax.ShapeDtypeStruct((3, t, d), F32),
            jax.ShapeDtypeStruct(ug0.shape, BF16),
            jax.ShapeDtypeStruct((2, 2 * STEPS, 2, cap2, dh), BF16),
            jax.ShapeDtypeStruct((2, side, kk, dh), BF16),
            jax.ShapeDtypeStruct((2, 2, 2, side, cap, dh), BF16),
        ),
        in_specs=[ANY] * 5,
        out_specs=(ANY,) * 5,
        scratch_shapes=[
            pltpu.VMEM((2, 2, 2, tile, dh), F32),
            pltpu.VMEM((2, side, 2, 8, d), BF16),
        ] + FFN_SEMS + [
            SEM,
            pltpu.SemaphoreType.DMA((2, 5, 4)),
            SEM2,
            SEM,
            SEM2,
            pltpu.SemaphoreType.DMA((2, side)),
            pltpu.SemaphoreType.DMA((2, 2, 2, side)),
            SEM2,
            SEM2,
            SEM,
            pltpu.SemaphoreType.DMA((keep,)),
            pltpu.SemaphoreType.DMA((2, 2, 2)),
            pltpu.SemaphoreType.DMA((3,)),
        ],
        cost_estimate=pl.CostEstimate(flops=flops, bytes_accessed=4 * n * t * d, transcendentals=2 * n * cap * f),
        compiler_params=pltpu.CompilerParams(collective_id=0, has_side_effects=True, vmem_limit_bytes=67043328),
        name='exchange',
    )(ug0, part1, ue1, ue3, ue2)[0]


def solution(mesh):
    n = mesh.shape['ep']
    rows = P(('dp', 'ep'))
    rep = P()

    def local(h0, idx, slot, ln_attn, wq, wk, wv, wo, ln_ffn, ws1, ws3, ws2, ln_moe, wr, ue1, ue3, ue2):
        b, s, d = h0.shape
        top = idx.shape[-1]
        ne = ue1.shape[0] * n
        t = b * s
        cap = CAP_FACTOR * t * top // ne
        parts = _rows(h0.reshape(t, d), idx.reshape(t, top).T, slot.reshape(t, top).T, ln_moe.reshape(1, d), wr.T, n)
        ug0 = lax.all_gather(parts[0], 'ep').reshape(n // CORES, CORES, -1, d)
        a, fo = _dense(h0, ln_attn, wq, wk, wv, wo, ln_ffn, ws1, ws3, ws2)
        z = (a.astype(F32) + fo).reshape(t, d)
        ug0, z = lax.optimization_barrier((ug0, z))
        r = _exchange(ug0, parts[1], ue1, ue3, ue2, n, cap, t)
        return (z + (r[0] + r[1] + r[2])).astype(BF16).reshape(b, s, d)

    specs = (rows, rows, rows) + (rep,) * 11 + (P('ep'), P('ep'), P('ep'))
    return jax.shard_map(local, mesh=mesh, in_specs=specs, out_specs=rows, check_vma=False)
```

time: 909 us -> 890 us (0.979)
  Pallas kernels: 608 us -> 644 us
  other arithmetic: 48.6 us -> 25.6 us
  waiting for transfers between devices: 22.1 us -> 0.06 us
    pallas_call x1, Pallas kernels: 432 us -> 634 us  [_exchange(): pl.pallas_call(functools.partial(_k2, n, cap, keep), out_shape=(jax.Shape...]
    pallas_call x1, Pallas kernels: 176 us -> 10.1 us  [_rows(): pl.pallas_call(functools.partial(_k0, n), out_shape=(jax.ShapeDtypeStruct...]
    all_gather x2 -> x1, waiting for transfers between devices: 17.6 us -> 0.01 us  [local(): ug0 = lax.all_gather(parts[0], 'ep').reshape(n // CORES, CORES, -1, d)]
    concatenate x1 -> x0, other arithmetic: 14.5 us -> none  [local(): mine = jnp.concatenate([u, _encode(gi, sl, gate)], axis=0)]
    dot_general x8 -> x7, matrix products: 134 us -> 133 us  [_mm(): return jnp.einsum(form, a, b, preferred_element_type=jnp.float32)]
  transfers between devices with their start and end apart: 3 -> 1, of which waited for: 2 -> 0; matrix products, arithmetic and copies ran while one was open for 23% -> 24% of each run, Pallas kernels for 20% -> 0%
where the time goes in v4:
time: 890 us; the launch traced here: 886 us
  Pallas kernels  644 us (72%)
  matrix products  166 us (19%)
  local copies, waits for them, and re-layouts  35.7 us (4%)
  other arithmetic  25.6 us (3%)
  between operations  13.8 us (2%)
    pallas_call x1, Pallas kernels, _exchange(): pl.pallas_call(functools.partial(_k2, n, cap, keep), out_shape=(jax.Shape...  634 us
    dot_general x7, matrix products, _mm(): return jnp.einsum(form, a, b, preferred_element_type=jnp.float32)  133 us
    sub x1, matrix products, _dense(): jax.nn.softmax(jnp.where(causal, sc, -1e+30), axis=-1).astype(jnp.bfloat16)  33.6 us
    dot_general x2, local copies, waits for them, and re-layouts, _mm(): return jnp.einsum(form, a, b, preferred_element_type=jnp.float32)  24.6 us
  transfers between devices with their start and end apart: 1, of which 0 were waited for; matrix products, arithmetic and copies ran while one was open for 24% of the time, Pallas kernels for 0%

profile of v4, /device:TPU:97, one launch (start us, length us, event | category | flops | bytes accessed | tf_op | source)
XLA Modules:
  0.0 885.5 jit_solution(5261252278446581182)
XLA Ops:
  6.5 0.0 all-gather.3.cloned.1.call-start
  6.6 1.3 reshape.208.ln
  7.8 1.4 copy_bitcast_fusion
  9.2 10.1 %rows.1 = (bf16[520,2048]{1,0:T(8,128)(2,1)}, bf16[520,2048]{1,0:T(8,128)(2,1)}) custom-call(bf16[1024,2048]{1,0:T(8,128)(2,1)} %bitcast.75, s32[6,1024]{1,0:T(8,128)} %get-tuple-element.28.idx, s32[6,1024]{1,0:T(8,128)} %get-tuple-element.27.slot, bf16[1,2048]{1,0:T(2,128)(2,1)} %reshape.208.ln, bf16[64,2048]{1,0:T(8,128)(2,1)} %bitcast.81), custom_call_target="tpu_custom_call" | custom-call | flops 268435456 | bytes 16777216 | tf_op jit(solution)/shard_map/rows/pallas_call | solution.py:694
  19.3 0.1 all-gather.3.cloned.1.call-update
  19.4 0.7 convert_element_type.56
  20.1 1.3 convert_element_type.65
  21.4 3.1 fusion.6
  24.4 14.1 %fusion.25 = bf16[1024,2048]{1,0:T(8,128)(2,1)} fusion(bf16[2048,2048]{1,0:T(8,128)(2,1)} %param.23, bf16[1,1024,2048]{2,1,0:T(8,128)(2,1)} %param.17, f32[2048]{0:T(1024)S(1)} %convert_element_type.56, f32[1024]{0:T(1024)S(1)} %add_rsqrt_fusion.1), kind=kOutput, calls=%fused_computation.42 | convolution fusion | flops 8600420352 | bytes 16789504 | tf_op jit(solution)/shard_map/bsd,de->bse/dot_general | solution.py:25
  38.5 6.4 copy.27
  44.9 12.3 %copy.28 = bf16[2048,2048]{1,0:T(8,128)(2,1)} copy(bf16[2048,2048]{0,1:T(8,128)(2,1)} %bitcast.76) | data formatting | bytes 16777216 | tf_op jit(solution)/shard_map/bsd,de->bse/dot_general | solution.py:25
  57.3 12.3 %copy.29 = bf16[2048,2048]{1,0:T(8,128)(2,1)} copy(bf16[2048,2048]{0,1:T(8,128)(2,1)} %bitcast.77) | data formatting | bytes 16777216 | tf_op jit(solution)/shard_map/bsd,de->bse/dot_general | solution.py:25
  69.6 0.3 iota_compare_fusion
  69.9 1.0 fusion.45
  70.9 0.0 copy-start
  70.9 12.9 %fusion.28 = f32[1,1024,16,128]{1,3,2,0:T(8,128)S(1)} fusion(bf16[16,128,2048]{2,1,0:T(8,128)(2,1)} %bitcast.79, bf16[1,1024,2048]{2,1,0:T(8,128)(2,1)} %param.17, f32[2048]{0:T(1024)S(1)} %convert_element_type.56, f32[1024]{0:T(1024)S(1)} %add_rsqrt_fusion.1), kind=kOutput, calls=%fused_computation.43 | convolution fusion | flops 8598323200 | bytes 20983808 | tf_op jit(solution)/shard_map/bsd,de->bse/dot_general | solution.py:25
  83.8 0.0 copy-done
  83.8 11.5 %fusion.31 = f32[1,1024,16,128]{1,3,2,0:T(8,128)S(1)} fusion(bf16[16,128,2048]{2,1,0:T(8,128)(2,1)} %bitcast.78, bf16[1,1024,2048]{2,1,0:T(8,128)(2,1)S(1)} %copy-done, f32[2048]{0:T(1024)S(1)} %convert_element_type.56, f32[1024]{0:T(1024)S(1)} %add_rsqrt_fusion.1), kind=kOutput, calls=%fused_computation.44 | convolution fusion | flops 8598323200 | bytes 20983808 | tf_op jit(solution)/shard_map/bsd,de->bse/dot_general | solution.py:25
  95.3 4.9 fusion.36
  100.3 33.6 %fusion.56 = (f32[16,1024]{1,0:T(8,128)S(1)}, f32[16,1024,1024]{1,2,0:T(8,128)}) fusion(pred[1024,1024]{0,1:T(8,128)(4,1)S(1)} %iota_compare_fusion, bf16[1024,16,64]{0,2,1:T(8,128)(2,1)} %get-tuple-element.19, bf16[1024,16,64]{0,2,1:T(8,128)(2,1)} %get-tuple-element.20, bf16[1024,16,64]{0,2,1:T(8,128)(2,1)} %get-tuple-element.16, ...), kind=kOutput, calls=%fused_computation.65 | convolution fusion | flops 4378854400 | bytes 76611584 | tf_op jit(solution)/shard_map/sub | solution.py:53
  133.9 25.1 %fusion.35 = bf16[16,128,1024]{2,1,0:T(8,128)(2,1)} fusion(bf16[1024,16,128]{0,2,1:T(8,128)(2,1)} %bitcast.80, f32[16,1024,1024]{1,2,0:T(8,128)} %get-tuple-element.24, f32[16,1024]{1,0:T(8,128)S(1)} %get-tuple-element.23), kind=kOutput, calls=%fused_computation.46 | convolution fusion | flops 4330618880 | bytes 75563008 | tf_op jit(solution)/shard_map/bhqk,bkhe->bqhe/dot_general | solution.py:25
  159.1 0.0 copy-start.1
  159.1 14.5 %fusion.10 = (f32[1024]{0:T(1024)S(1)}, bf16[1,1024,2048]{2,1,0:T(8,128)(2,1)S(1)}) fusion(bf16[1024,2048]{0,1:T(8,128)(2,1)} %bitcast.82, bf16[2048,2048]{1,0:T(8,128)(2,1)} %param.24, bf16[1,1024,2048]{2,1,0:T(8,128)(2,1)} %param.17), kind=kOutput, calls=%fused_computation.20 | convolution fusion | flops 8602516480 | bytes 20975616 | tf_op jit(solution)/shard_map/bse,ed->bsd/dot_general | solution.py:25
  173.5 0.0 copy-start.2
  173.6 2.0 copy-done.2
  175.6 0.0 copy-done.1
  175.6 17.7 %fusion.42 = f32[1024,2816]{1,0:T(8,128)} fusion(bf16[2048,2816]{1,0:T(8,128)(2,1)} %param.26, bf16[1,1024,2048]{2,1,0:T(8,128)(2,1)S(1)} %get-tuple-element.26, f32[2048]{0:T(1024)S(1)} %copy-done.1, f32[1024]{0:T(1024)S(1)} %add_rsqrt_fusion), kind=kOutput, calls=%fused_computation.51 | convolution fusion | flops 11819548672 | bytes 27275264 | tf_op jit(solution)/shard_map/bsd,df->bsf/dot_general | solution.py:25
  193.2 37.0 %fusion.13 = f32[1024,2048]{1,0:T(8,128)} fusion(bf16[1,1024,2048]{2,1,0:T(8,128)(2,1)} %copy-done.2, bf16[2816,2048]{1,0:T(8,128)(2,1)} %param.28, f32[1024,2816]{1,0:T(8,128)} %fusion.42, bf16[2048,2816]{1,0:T(8,128)(2,1)} %param.27, f32[2048]{0:T(1024)S(1)} %copy-done.1, f32[1024]{0:T(1024)S(1)} %add_rsqrt_fusion), kind=kOutput, calls=%fused_computation.23 | convolution fusion | flops 23652204544 | bytes 47198208 | tf_op jit(solution)/shard_map/bsf,fd->bsd/dot_general | solution.py:25
  230.2 0.0 all-gather.3.cloned.1.call-done
  230.2 633.9 %exchange.1 = (f32[3,1024,2048]{2,1,0:T(8,128)}, bf16[16,2,520,2048]{3,2,1,0:T(8,128)(2,1)}, bf16[2,16,2,384,1024]{4,3,2,1,0:T(8,128)(2,1)}, bf16[2,4,3072,1024]...) custom-call(bf16[16,2,520,2048]{3,2,1,0:T(8,128)(2,1)} %bitcast.4.ug0, bf16[520,2048]{1,0:T(8,128)(2,1)} %get-tuple-element.13.part1, ...), custom_call_target="tpu_custom_call" | custom-call | flops 418759311360 | bytes 268435456 | tf_op jit(solution)/shard_map/exchange/pallas_call | solution.py:723
  864.1 14.3 %fusion.17 = bf16[1,1024,2048]{2,1,0:T(8,128)(2,1)} fusion(f32[1024,2048]{1,0:T(8,128)} %fusion.13, f32[3,1024,2048]{2,1,0:T(8,128)} %get-tuple-element.14), kind=kLoop, calls=%fused_computation.27 | loop fusion | flops 8388608 | bytes 37748736 | tf_op jit(solution)/shard_map/reshape | solution.py:775
  (3 shorter events, 0.0 us)
Async XLA Ops:
  6.5 223.7 %all-gather.3.cloned.1.call-start = ((), (), s32[]{:S(2)}) async-start(), calls=%async_computation | async-start | bytes 70287360 | tf_op jit(solution)/shard_map/all_gather | solution.py:770
  70.9 12.9 %copy-start = (bf16[1,1024,2048]{2,1,0:T(8,128)(2,1)S(1)}, bf16[1,1024,2048]{2,1,0:T(8,128)(2,1)}, u32[]{:S(2)}) copy-start(bf16[1,1024,2048]{2,1,0:T(8,128)(2,1)} %param.17) | copy-start | bytes 12582916
  159.1 16.5 %copy-start.1 = (f32[2048]{0:T(1024)S(1)}, f32[2048]{0:T(1024)}, u32[]{:S(2)}) copy-start(f32[2048]{0:T(1024)} %convert_element_type.65) | copy-start | bytes 24580
  173.5 2.0 copy-start.2
Sparse Core Ops, SparseCore 0:
  19.5 201.0 all-gather.2

commit v5 on v4

--- a/solution.py
+++ b/solution.py
@@ -17,45 +17,28 @@
 BF16 = jnp.bfloat16
 MESH = pl.DeviceIdType.MESH
 BOTH = (0, 1)
+PAIR = 2
+NT = (((1,), (1,)), ((), ()))
+STEP = (1, -1)
+loop = functools.partial(pl.loop, 0)
 SEM = pltpu.SemaphoreType.DMA
 SEM2, SEM4 = SEM((2,)), SEM((4,))
 
 
-def _mm(form, a, b):
-    return jnp.einsum(form, a, b, preferred_element_type=jnp.float32)
-
-
-def _rms(x, w):
-    xf = x.astype(jnp.float32)
-    r = lax.rsqrt(jnp.mean(xf * xf, axis=-1, keepdims=True) + EPS)
-    return (xf * r * w.astype(jnp.float32)).astype(jnp.bfloat16)
-
-
-def _rope(x):
-    s, half = x.shape[1], x.shape[-1] // 2
-    freq = 10000.0 ** (-jnp.arange(half, dtype=jnp.float32) / half)
-    ang = jnp.arange(s, dtype=jnp.float32)[:, None] * freq[None, :]
-    c = jnp.cos(ang)[None, :, None, :]
-    sn = jnp.sin(ang)[None, :, None, :]
-    x1, x2 = x[..., :half], x[..., half:]
-    return jnp.concatenate([x1 * c - x2 * sn, x2 * c + x1 * sn], axis=-1)
-
-
-def _dense(h0, ln_attn, wq, wk, wv, wo, ln_ffn, ws1, ws3, ws2):
-    b, s, _ = h0.shape
-    nh = wq.shape[1] // HEAD
-    x1 = _rms(h0, ln_attn)
-    q = _rope(_mm('bsd,de->bse', x1, wq).reshape(b, s, nh, HEAD)).astype(jnp.bfloat16)
-    k = _rope(_mm('bsd,de->bse', x1, wk).reshape(b, s, nh, HEAD)).astype(jnp.bfloat16)
-    v = _mm('bsd,de->bse', x1, wv).astype(jnp.bfloat16).reshape(b, s, nh, HEAD)
-    sc = _mm('bqhe,bkhe->bhqk', q, k) * HEAD ** -0.5
-    causal = jnp.arange(s)[:, None] >= jnp.arange(s)[None, :]
-    p = jax.nn.softmax(jnp.where(causal, sc, -1e30), axis=-1).astype(jnp.bfloat16)
-    o = _mm('bhqk,bkhe->bqhe', p, v).astype(jnp.bfloat16).reshape(b, s, nh * HEAD)
-    a = (h0.astype(jnp.float32) + _mm('bse,ed->bsd', o, wo)).astype(jnp.bfloat16)
-    x2 = _rms(a, ln_ffn)
-    hs = (jax.nn.silu(_mm('bsd,df->bsf', x2, ws1)) * _mm('bsd,df->bsf', x2, ws3)).astype(jnp.bfloat16)
-    return a, _mm('bsf,fd->bsd', hs, ws2)
+def _turns(t):
+    half = HEAD // 2
+    freq = 10000.0 ** (-jnp.arange(half, dtype=F32) / half)
+    ang = jnp.arange(t, dtype=F32)[:, None] * freq[None, :]
+    c, s = jnp.cos(ang), jnp.sin(ang)
+    return jnp.stack([jnp.concatenate([c, c], axis=1), jnp.concatenate([-s, s], axis=1)])
+
+
+def _norm(xf, w):
+    return (xf * lax.rsqrt(jnp.mean(xf * xf, axis=-1, keepdims=True) + EPS) * w).astype(BF16)
+
+
+def _dot(a, b):
+    return jnp.dot(a, b, preferred_element_type=F32)
 
 
 def _parts(c):
@@ -98,7 +81,7 @@
         return jnp.concatenate([e[i][:, q * half:(q + 1) * half] for i in BOTH], axis=1)
 
     b = [block(q) for q in range(4)]
-    lo = jnp.concatenate([b[0][6:], b[1][6:], b[2][6:]], axis=0)
+    lo = jnp.concatenate([b[0][6:], b[1][6:], b[2][6:]])
     return b[0][:6], b[1][:6], b[2][:6] + b[3][:6] + lo
 
 
@@ -118,7 +101,7 @@
 
     other = me + 1 - 2 * c
     barrier = pltpu.get_barrier_semaphore()
-    pl.semaphore_signal(barrier, inc=1, device_id={'ep': other}, device_id_type=MESH)
+    pl.semaphore_signal(barrier, device_id={'ep': other}, device_id_type=MESH)
     pl.semaphore_wait(barrier, 1)
 
     def gives(out):
@@ -139,9 +122,9 @@
         for i in BOTH:
             h_copy(o, i).wait()
             xf = hb[pl.ds((o * 2 + i) * tile, tile)].astype(F32)
-            u = (xf * lax.rsqrt(jnp.mean(xf * xf, axis=-1, keepdims=True) + EPS) * w).astype(BF16)
+            u = _norm(xf, w)
             ub[o, pl.ds(i * tile, tile)] = u
-            lg = lax.dot_general(wr[...], u, (((1,), (1,)), ((), ())), preferred_element_type=F32)
+            lg = lax.dot_general(wr[...], u, NT, preferred_element_type=F32)
             cols = pl.ds(pl.multiple_of((order[o] * 2 + i) * tile, tile), tile)
             ex, sl = idx[:, cols], slot[:, cols]
             pick = [jnp.sum(jnp.where(expert == ex[j:j + 1], lg, 0.0), axis=0, keepdims=True) for j in range(6)]
@@ -154,7 +137,7 @@
             zero = jnp.zeros((1, tile), F32)
             blocks = ([exf] + lo[:2], [slf] + lo[2:4], hi + lo[4:], mid + [zero, zero])
             for q, rows in enumerate(blocks):
-                eb[o, :, pl.ds(q * half + i * tile, tile)] = jnp.concatenate(rows, axis=0).astype(BF16)
+                eb[o, :, pl.ds(q * half + i * tile, tile)] = jnp.concatenate(rows).astype(BF16)
         for p, out in enumerate((out0, out1)):
             @pl.when(c == p)
             def _():
@@ -198,7 +181,7 @@
     for el in BOTH:
         weights(el)
 
-    @pl.loop(0, 2 * STEPS)
+    @loop(2 * STEPS)
     def _(step):
         p, k = step // STEPS, step % STEPS
         before(step)
@@ -207,7 +190,7 @@
         def _():
             load_u(ugs[1], 0)
 
-        @pl.loop(0, 2)
+        @loop(2)
         def _(i):
             pltpu.make_async_copy(u.at[i], u.at[i], usem.at[i]).wait()
             pltpu.make_async_copy(ur.at[i], ur.at[i], usem.at[2 + i]).wait()
@@ -232,7 +215,7 @@
         def _():
             load_u(ugs[1], k + 1)
 
-        @pl.loop(0, 2)
+        @loop(2)
         def _(el):
             @pl.when(step == 0)
             def _():
@@ -261,17 +244,196 @@
         wait_kept(el)
 
 
+def _dense(h0, cs, ln1, wq, wk, wv, wo, ln2, ws1, ws3, ws2, z, hb, xb, wa, wf, wg, qb, kb, vb, ob, hs, ct, zs, hsem, asem, fsem, gsem, zsem, hook):
+    t, d = hb.shape
+    wide, narrow = qb.shape[1], wf.shape[3]
+    groups, chunks = d // wide, ws1.shape[1] // narrow
+    tall, tile = t // 2, t // 4
+
+    def load_a(i):
+        b, cols = i % 2, pl.ds(pl.multiple_of(i % groups * wide, wide), wide)
+
+        @pl.when(i < groups)
+        def _():
+            for j, w in enumerate((wq, wk, wv)):
+                pltpu.make_async_copy(w.at[:, cols], wa.at[b, j], asem.at[b]).start()
+
+        @pl.when((i >= groups) & (i < 2 * groups))
+        def _():
+            pltpu.make_async_copy(wo.at[:, cols], wa.at[b, 0], asem.at[b]).start()
+
+    def load_f(j):
+        @pl.when(j < chunks)
+        def _():
+            for i, w in enumerate((ws1, ws3)):
+                cols = pl.ds(pl.multiple_of(j * narrow, narrow), narrow)
+                pltpu.make_async_copy(w.at[:, cols], wf.at[j % 2, i], fsem.at[j % 2]).start()
+
+    def load_g(j):
+        @pl.when(j < groups)
+        def _():
+            pltpu.make_async_copy(ws2.at[:, pl.ds(pl.multiple_of(j * wide, wide), wide)], wg.at[j % 2], gsem.at[j % 2]).start()
+
+    def wait(ref, sem):
+        pltpu.make_async_copy(ref, ref, sem).wait()
+
+    pltpu.make_async_copy(h0, hb, hsem).start()
+    pltpu.make_async_copy(cs, ct, hsem).start()
+    for load in (load_a, load_f, load_g):
+        for i in BOTH:
+            load(jnp.int32(i))
+    wait(hb, hsem)
+    wait(ct, hsem)
+
+    def norm(ln):
+        w = ln[...].astype(F32)
+
+        @loop(t // tile)
+        def _(i):
+            rows = pl.ds(pl.multiple_of(i * tile, tile), tile)
+            xb[rows] = _norm(hb[rows].astype(F32), w)
+
+    norm(ln1)
+
+    @loop(groups)
+    def _(g):
+        b = g % 2
+        hook('group', g)
+        wait(wa.at[b], asem.at[b])
+
+        @loop(t // tall)
+        def _(m):
+            rows = pl.ds(pl.multiple_of(m * tall, tall), tall)
+            c, s = ct[0, rows], ct[1, rows]
+            for j, out in enumerate((qb, kb)):
+                v = _dot(xb[rows], wa[b, j])
+                for i in range(wide // HEAD):
+                    head = v[:, i * HEAD:(i + 1) * HEAD]
+                    out[rows, pl.ds(i * HEAD, HEAD)] = (head * c + pltpu.roll(head, HEAD // 2, 1) * s).astype(BF16)
+            vb[rows] = _dot(xb[rows], wa[b, 2]).astype(BF16)
+
+        load_a(g + 2)
+
+        @loop(wide // HEAD)
+        def _(i):
+            cols = pl.ds(pl.multiple_of(i * HEAD, HEAD), HEAD)
+            causal = lax.broadcasted_iota(jnp.int32, (tile, tile), 0) >= lax.broadcasted_iota(jnp.int32, (tile, tile), 1)
+            for m in range(t // tile):
+                rows, past = pl.ds(m * tile, tile), pl.ds(0, m * tile)
+                q = qb[rows, cols]
+
+                def scores(keys):
+                    return lax.dot_general(q, kb[keys, cols], NT, preferred_element_type=F32) * HEAD ** -0.5
+
+                here = jnp.where(causal, scores(rows), -1e30)
+                top = jnp.max(here, axis=-1, keepdims=True)
+                if m:
+                    before = scores(past)
+                    top = jnp.maximum(top, jnp.max(before, axis=-1, keepdims=True))
+                    before = jnp.exp(before - top)
+                here = jnp.exp(here - top)
+                total = jnp.sum(here, axis=-1, keepdims=True)
+                if m:
+                    total = total + jnp.sum(before, axis=-1, keepdims=True)
+                share = 1.0 / total
+                o = _dot((here * share).astype(BF16), vb[rows, cols])
+                if m:
+                    o = o + _dot((before * share).astype(BF16), vb[past, cols])
+                ob[rows, pl.ds(pl.multiple_of(g * wide + i * HEAD, HEAD), HEAD)] = o.astype(BF16)
+
+    @loop(groups)
+    def _(g):
+        b = g % 2
+        cols = pl.ds(pl.multiple_of(g * wide, wide), wide)
+        wait(wa.at[b, 0], asem.at[b])
+
+        @loop(t // tall)
+        def _(m):
+            rows = pl.ds(pl.multiple_of(m * tall, tall), tall)
+            hb[rows, cols] = (hb[rows, cols].astype(F32) + _dot(ob[rows], wa[b, 0])).astype(BF16)
+
+        load_a(g + groups + 2)
+
+    norm(ln2)
+
+    @loop(chunks)
+    def _(j):
+        b = j % 2
+        hook('chunk', j)
+        wait(wf.at[b], fsem.at[b])
+
+        @loop(t // tall)
+        def _(m):
+            rows = pl.ds(pl.multiple_of(m * tall, tall), tall)
+            x = xb[rows]
+            a1, a3 = _dot(x, wf[b, 0]), _dot(x, wf[b, 1])
+            hs[rows, pl.ds(pl.multiple_of(j * narrow, narrow), narrow)] = (jax.nn.silu(a1) * a3).astype(BF16)
+
+        load_f(j + 2)
+
+    hook('down', None)
+
+    def z_copy(g, m):
+        cols = pl.ds(pl.multiple_of(g * wide, wide), wide)
+        return pltpu.make_async_copy(zs.at[m], z.at[pl.ds(pl.multiple_of(m * tall, tall), tall), cols], zsem.at[m])
+
+    @loop(groups)
+    def _(g):
+        b = g % 2
+        cols = pl.ds(pl.multiple_of(g * wide, wide), wide)
+        wait(wg.at[b], gsem.at[b])
+
+        @loop(t // tall)
+        def _(m):
+            rows = pl.ds(pl.multiple_of(m * tall, tall), tall)
+
+            @pl.when(g >= 1)
+            def _():
+                z_copy(g, m).wait()
+
+            zs[m] = hb[rows, cols].astype(F32) + _dot(hs[rows], wg[b])
+            z_copy(g, m).start()
+
+        load_g(g + 2)
+
+    for m in BOTH:
+        wait(zs.at[m], zsem.at[m])
+
+
+def _dense_scratch(t, d, fs):
+    wide, narrow = 4 * HEAD, 2 * HEAD
+    head = pltpu.VMEM((t, wide), BF16)
+    full = pltpu.VMEM((t, d), BF16)
+    return [
+        full,
+        full,
+        pltpu.VMEM((PAIR, 3, d, wide), BF16),
+        pltpu.VMEM((PAIR, PAIR, d, narrow), BF16),
+        pltpu.VMEM((PAIR, fs, wide), BF16),
+        head,
+        head,
+        head,
+        full,
+        pltpu.VMEM((t, fs), BF16),
+        pltpu.VMEM((PAIR, t, HEAD), F32),
+        pltpu.VMEM((PAIR, t // 2, wide), F32),
+    ]
+
+
+DENSE_SEMS = [SEM, SEM2, SEM2, SEM2, SEM2]
+
+
 def _ffn_scratch(t, d, f, cap):
     cap2 = 2 * cap
     return [
-        pltpu.VMEM((2, d, 2 * f), BF16),
-        pltpu.VMEM((2, f, d), BF16),
-        pltpu.VMEM((2, t, d), BF16),
-        pltpu.VMEM((2, 2, 8, d), BF16),
+        pltpu.VMEM((PAIR, d, 2 * f), BF16),
+        pltpu.VMEM((PAIR, f, d), BF16),
+        pltpu.VMEM((PAIR, t, d), BF16),
+        pltpu.VMEM((PAIR, PAIR, 8, d), BF16),
         pltpu.VMEM((cap2, t), BF16),
-        pltpu.VMEM((2, cap2, d), BF16),
+        pltpu.VMEM((PAIR, cap2, d), BF16),
         pltpu.VMEM((cap2, f), BF16),
-        pltpu.VMEM((2, cap2, d), BF16),
+        pltpu.VMEM((PAIR, cap2, d), BF16),
     ]
 
 
@@ -310,7 +472,7 @@
         return self.out.at[chip, self.c, pl.ds(a, b - a)]
 
     def copy(self, color, src, dst, axis, way, sem):
-        dest = self.device(axis, 1 - 2 * way, self.c)
+        dest = self.device(axis, STEP[way], self.c)
         pltpu.make_async_remote_copy(src, dst, self.send_sem, sem, device_id={'ep': dest}, device_id_type=MESH).start()
 
     def share(self, src, dst):
@@ -378,8 +540,11 @@
         self.wait(self.out.at[pl.ds(0, chips - 1), 0], self.send_sem)
 
 
-def _k2(n, cap, keep, ug0, part1, ue1, ue3, ue2, rxf, ug1, ys, r, rl, rx2, mr, wsem, w2sem, usem, ysem,
-        gsem, grsem, pairsem, osem, ssem, rsem, relsem, fsem, lsem, msem, bsem, r2sem, rfsem):
+def _k2(n, cap, keep, part0, part1, ue1, ue3, ue2, *refs):
+    dense_in, refs = refs[:11], refs[11:]
+    rxf, z, ug0, ug1, ys, r, rl, rx2, mr, *refs = refs
+    dense_sems, refs = refs[:5], refs[5:]
+    wsem, w2sem, usem, ysem, gsem, grsem, pairsem, osem, ssem, rsem, relsem, fsem, lsem, msem, bsem, r2sem, rfsem = refs
     side, me, x, y, c = _place(n)
     t, d = rxf.shape[1], rxf.shape[2]
     f = ue1.shape[2]
@@ -389,7 +554,7 @@
     far = side // 2
     units = 16
     th, cap2 = t // 2, 2 * cap
-    gather = _Gather(n, part1, ug1, gsem, grsem, pairsem)
+    gathers = [_Gather(n, part, ug, gsem.at[p], grsem.at[p], pairsem.at[p]) for p, (part, ug) in enumerate(((part0, ug0), (part1, ug1)))]
 
     def device(axis, off, cc):
         return ((y + axis * off) % side * side + (x + (1 - axis) * off) % side) * CORES + cc
@@ -402,9 +567,9 @@
         for off in range(side):
             pltpu.make_async_copy(ug.at[device(axis, off, 0) // CORES, :, pl.ds(th, 8)], mr.at[p, off], msem).start()
 
-    kept = pltpu.make_async_copy(part1, ug1.at[me // CORES, c], osem)
-    kept.start()
-    routing_rows(0, ug0)
+    kept = [pltpu.make_async_copy(part, ug.at[me // CORES, c], osem.at[p]) for p, (part, ug) in enumerate(((part0, ug0), (part1, ug1)))]
+    for cp in kept:
+        cp.start()
 
     barrier = pltpu.get_barrier_semaphore()
     peers = 0
@@ -412,7 +577,7 @@
         for dc in range(CORES):
             for axis in BOTH:
                 if off or (dc and not axis):
-                    pl.semaphore_signal(barrier, inc=1, device_id={'ep': device(axis, off, (c + dc) % CORES)}, device_id_type=MESH)
+                    pl.semaphore_signal(barrier, device_id={'ep': device(axis, off, (c + dc) % CORES)}, device_id_type=MESH)
                     peers += 1
     pl.semaphore_wait(barrier, peers)
 
@@ -440,7 +605,7 @@
                     def _():
                         for el in BOTH:
                             at = (p, half, el, other)
-                            remote(src.at[pl.ds(el * cap, cap)], rl.at[at], ssem.at[p], relsem.at[at], device(1 - half, 1 - 2 * el, c)).start()
+                            remote(src.at[pl.ds(el * cap, cap)], rl.at[at], ssem.at[p], relsem.at[at], device(1 - half, STEP[el], c)).start()
 
                 if want_far != 0:
                     relayed()
@@ -451,13 +616,42 @@
         for half, mine, line in ((0, y, (x + other) % side), (1, x, (y + other) % side)):
             for el in BOTH:
                 at = (p, half, el, other)
-                step = 1 - 2 * el
+                step = STEP[el]
                 pltpu.make_async_copy(rl.at[at], rl.at[at], relsem.at[at]).wait()
                 origin = (mine - step + side) % side
                 dst = r.at[p, line, pl.ds((origin * CORES + c) * cap2 + el * cap, cap)]
                 remote(rl.at[at], dst, fsem.at[p], rsem.at[p, line], device(1 - half, step, (p + half) % 2)).start()
 
-    gather.start()
+    first, second = gathers
+    first.start()
+
+    def hook(name, i):
+        if name == 'group':
+            @pl.when(i == 2)
+            def _():
+                first.along(1)
+
+            @pl.when(i == 3)
+            def _():
+                first.across((0,))
+        elif name == 'chunk':
+            @pl.when(i == 4)
+            def _():
+                first.along(2)
+        else:
+            first.across((-1, 1))
+
+    def dense_phase(*refs):
+        _dense(*dense_in, z, *refs, *dense_sems, hook=hook)
+
+    pl.run_scoped(dense_phase, *_dense_scratch(t, d, dense_in[8].shape[1]))
+    first.last((0,))
+    first.across((2,))
+    second.start()
+    first.last((-1, 1, 2))
+    kept[0].wait()
+    first.finish()
+    routing_rows(0, ug0)
 
     def before(step):
         def at(s):
@@ -465,54 +659,51 @@
 
         @at(1)
         def _():
-            gather.along(1)
+            second.along(1)
 
         @at(2)
         def _():
-            gather.across((0,))
+            second.across((0,))
+
+        @at(3)
+        def _():
+            second.along(2)
 
         @at(4)
         def _():
-            gather.along(2)
+            second.across((-1, 1))
 
         @at(5)
         def _():
-            gather.across((-1, 1))
+            second.last((0,))
 
         @at(6)
         def _():
-            gather.last((0,))
-
-        @at(7)
-        def _():
-            gather.across((2,))
-
-            @pl.loop(0, 6)
-            def _(k):
-                send(0, k, 1)
-
-            @pl.loop(0, 6)
-            def _(k):
-                send(0, k, 0)
+            second.across((2,))
+
+            for want in (1, 0):
+                @loop(5)
+                def _(k):
+                    send(0, k, want)
 
         @at(8)
         def _():
-            gather.last((-1, 1, 2))
-            kept.wait()
-            gather.finish()
+            second.last((-1, 1, 2))
+            kept[1].wait()
+            second.finish()
             routing_rows(1, ug1)
 
-        @pl.when((step == 8) | (step == 9))
+        @pl.when((step >= 7) & (step < 10))
         def _():
             send(0, step - 2, 0)
 
         @at(10)
         def _():
-            @pl.loop(0, side)
+            @loop(side)
             def _(other):
                 forward(0, other)
 
-        @pl.when((step >= 10) & (step < 14))
+        @pl.when(step >= 10)
         def _():
             send(1, step - 10, 2)
 
@@ -520,6 +711,8 @@
         _ffn(n, cap, (ug0, ug1), ue1, ue3, ue2, ys, *refs, wsem, w2sem, usem, ysem, before=before)
 
     pl.run_scoped(experts_phase, *_ffn_scratch(t, d, f, cap))
+    for k in (6, 7):
+        send(1, k, 0)
 
     def role(w):
         p, q, b = w // 8, w % 8 // 2, w % 2
@@ -556,7 +749,7 @@
             along = cy * (1.0 - af) + cx * af
             e = jnp.where(across == mine, along * (2 * CORES) + low, -1.0)
             gap = jnp.zeros((2, t), F32)
-            m = jnp.concatenate([e, gap, sl, gap, g, jnp.zeros((106, t), F32)], axis=0)
+            m = jnp.concatenate([e, gap, sl, gap, g, jnp.zeros((106, t), F32)])
             for i in BOTH:
                 @pl.when(mh == i)
                 def _():
@@ -587,7 +780,7 @@
             out = [rxf.at[j, rows, pl.ds(pl.multiple_of(axis * dh, dh), dh)] for j in range(3)]
 
             for way in BOTH:
-                step = 1 - 2 * way
+                step = STEP[way]
 
                 @pl.when((off == far) & (mh == way))
                 def _():
@@ -614,7 +807,7 @@
         prepare(0)
         build(pma, 0, 0)
 
-        @pl.loop(0, units)
+        @loop(units)
         def _(w):
             p, axis, off, mh = role(w)
             after = w + 1 - (w + 1) // units
@@ -629,11 +822,7 @@
             def _():
                 forward(1, far)
 
-                @pl.loop(4, STEPS)
-                def _(k):
-                    send(1, k, 0)
-
-            @pl.when(w == 4)
+            @pl.when(w == 3)
             def _():
                 for other in range(side):
                     if other != far:
@@ -656,7 +845,7 @@
                     build(pma, after, 0)
 
                 for way in BOTH:
-                    @pl.when((off == (side + 1 - 2 * way) % side) & (mh == way))
+                    @pl.when((off == (side + STEP[way]) % side) & (mh == way))
                     def _():
                         got = rx2.at[p, way, i]
                         pltpu.make_async_copy(got, got, r2sem.at[p, way, i]).wait()
@@ -669,14 +858,15 @@
 
     pl.run_scoped(
         combine_phase,
-        pltpu.VMEM((2, kk, dh), BF16),
-        pltpu.VMEM((2, 2 * tile, LANES), F32),
+        pltpu.VMEM((PAIR, kk, dh), BF16),
+        pltpu.VMEM((PAIR, 2 * tile, LANES), F32),
         pltpu.VMEM((3 * tile, kk), BF16),
         pltpu.VMEM((3 * tile, kk), BF16),
         pltpu.VMEM((keep * 2, tile, dh), F32),
     )
 
-    gather.drain()
+    for gather in gathers:
+        gather.drain()
     for p in BOTH:
         blocks = ys.at[p, pl.ds(0, 2 * STEPS - 2)]
         pltpu.make_async_copy(blocks, blocks, ssem.at[p]).wait()
@@ -698,8 +888,8 @@
         out_specs=(ANY,) * CORES,
         scratch_shapes=[
             pltpu.VMEM((t, d), BF16),
-            pltpu.VMEM((2, t // 2, d), BF16),
-            pltpu.VMEM((2, 8, d), BF16),
+            pltpu.VMEM((PAIR, t // 2, d), BF16),
+            pltpu.VMEM((PAIR, 8, d), BF16),
             SEM4,
             SEM2,
             SEM2,
@@ -711,48 +901,50 @@
     )(h0, idx, slot, ln, wr)
 
 
-def _exchange(ug0, part1, ue1, ue3, ue2, n, cap, t):
-    d, f = part1.shape[-1], ue1.shape[-1]
+def _layer(parts, experts, dense, n, cap, t):
+    d, f, fs = parts[0].shape[-1], experts[0].shape[-1], dense[8].shape[-1]
     dh = d // 2
     side = math.isqrt(n // CORES)
     tile = t // 4
     kk = CORES * side * 2 * cap
     keep = 4
     cap2 = 2 * cap
-    flops = 2 * n * cap * (2 * t * d + 6 * d * f) + 2 * side * 3 * 2 * t * kk * dh
+    vmem = pl.BlockSpec(memory_space=pltpu.VMEM)
+    gathered = jax.ShapeDtypeStruct((n // CORES, CORES) + parts[0].shape, BF16)
     return pl.pallas_call(
         functools.partial(_k2, n, cap, keep),
         out_shape=(
             jax.ShapeDtypeStruct((3, t, d), F32),
-            jax.ShapeDtypeStruct(ug0.shape, BF16),
-            jax.ShapeDtypeStruct((2, 2 * STEPS, 2, cap2, dh), BF16),
-            jax.ShapeDtypeStruct((2, side, kk, dh), BF16),
-            jax.ShapeDtypeStruct((2, 2, 2, side, cap, dh), BF16),
+            jax.ShapeDtypeStruct((t, d), F32),
+            gathered,
+            gathered,
+            jax.ShapeDtypeStruct((PAIR, PAIR * STEPS, PAIR, cap2, dh), BF16),
+            jax.ShapeDtypeStruct((PAIR, side, kk, dh), BF16),
+            jax.ShapeDtypeStruct((PAIR, PAIR, PAIR, side, cap, dh), BF16),
         ),
-        in_specs=[ANY] * 5,
-        out_specs=(ANY,) * 5,
+        in_specs=[ANY] * 7 + [vmem, ANY, ANY, ANY, ANY, vmem, ANY, ANY, ANY],
+        out_specs=(ANY,) * 7,
         scratch_shapes=[
-            pltpu.VMEM((2, 2, 2, tile, dh), F32),
-            pltpu.VMEM((2, side, 2, 8, d), BF16),
-        ] + FFN_SEMS + [
-            SEM,
-            pltpu.SemaphoreType.DMA((2, 5, 4)),
+            pltpu.VMEM((PAIR, PAIR, PAIR, tile, dh), F32),
+            pltpu.VMEM((PAIR, side, 2, 8, d), BF16),
+        ] + DENSE_SEMS + FFN_SEMS + [
             SEM2,
-            SEM,
+            SEM((PAIR, PAIR, 5, 4)),
+            SEM((PAIR, PAIR)),
             SEM2,
-            pltpu.SemaphoreType.DMA((2, side)),
-            pltpu.SemaphoreType.DMA((2, 2, 2, side)),
+            SEM2,
+            SEM((PAIR, side)),
+            SEM((PAIR, PAIR, PAIR, side)),
             SEM2,
             SEM2,
             SEM,
-            pltpu.SemaphoreType.DMA((keep,)),
-            pltpu.SemaphoreType.DMA((2, 2, 2)),
-            pltpu.SemaphoreType.DMA((3,)),
+            SEM((keep,)),
+            SEM((PAIR, PAIR, PAIR)),
+            SEM((3,)),
         ],
-        cost_estimate=pl.CostEstimate(flops=flops, bytes_accessed=4 * n * t * d, transcendentals=2 * n * cap * f),
         compiler_params=pltpu.CompilerParams(collective_id=0, has_side_effects=True, vmem_limit_bytes=67043328),
-        name='exchange',
-    )(ug0, part1, ue1, ue3, ue2)[0]
+        name='layer',
+    )(*parts, *experts, *dense)[:2]
 
 
 def solution(mesh):
@@ -767,11 +959,9 @@
         t = b * s
         cap = CAP_FACTOR * t * top // ne
         parts = _rows(h0.reshape(t, d), idx.reshape(t, top).T, slot.reshape(t, top).T, ln_moe.reshape(1, d), wr.T, n)
-        ug0 = lax.all_gather(parts[0], 'ep').reshape(n // CORES, CORES, -1, d)
-        a, fo = _dense(h0, ln_attn, wq, wk, wv, wo, ln_ffn, ws1, ws3, ws2)
-        z = (a.astype(F32) + fo).reshape(t, d)
-        ug0, z = lax.optimization_barrier((ug0, z))
-        r = _exchange(ug0, parts[1], ue1, ue3, ue2, n, cap, t)
+        flat = h0.reshape(t, d)
+        dense = (flat, _turns(t), ln_attn.reshape(1, d), wq, wk, wv, wo, ln_ffn.reshape(1, d), ws1, ws3, ws2)
+        r, z = _layer(parts, (ue1, ue3, ue2), dense, n, cap, t)
         return (z + (r[0] + r[1] + r[2])).astype(BF16).reshape(b, s, d)
 
     specs = (rows, rows, rows) + (rep,) * 11 + (P('ep'), P('ep'), P('ep'))

time: 890 us -> 825 us (0.927)
  matrix products: 166 us -> 0 us
  Pallas kernels: 644 us -> 802 us
  local copies, waits for them, and re-layouts: 35.7 us -> 5.24 us
  between operations: 13.8 us -> 0.03 us
    pallas_call x1, Pallas kernels: 634 us -> 792 us  [_layer(): pl.pallas_call(functools.partial(_k2, n, cap, keep), out_shape=(jax.Shape...]
    dot_general x7 -> x0, matrix products: 133 us -> none  [_mm(): return jnp.einsum(form, a, b, preferred_element_type=jnp.float32)]
    sub x1 -> x0, matrix products: 33.6 us -> none  [_dense(): jax.nn.softmax(jnp.where(causal, sc, -1e+30), axis=-1).astype(jnp.bfloat16)]
    dot_general x2 -> x0, local copies, waits for them, and re-layouts: 24.6 us -> none  [_mm(): return jnp.einsum(form, a, b, preferred_element_type=jnp.float32)]
  transfers between devices with their start and end apart: 1 -> 0, of which waited for: 0 -> 0; matrix products, arithmetic and copies ran while one was open for 24% -> 0% of each run, Pallas kernels for 0% -> 0%
where the time goes in v5:
time: 825 us
  Pallas kernels  802 us (97%)
  other arithmetic  17.6 us (2%)
    pallas_call x1, Pallas kernels, _layer(): pl.pallas_call(functools.partial(_k2, n, cap, keep), out_shape=(jax.Shape...  792 us

profile of v5, /device:TPU:97, one launch (start us, length us, event | category | flops | bytes accessed | tf_op | source)
XLA Modules:
  0.0 825.1 jit_solution(361830986523846868)
XLA Ops:
  0.0 1.3 reshape.34.refs_2_
  1.3 1.3 reshape.35.refs_7_
  2.6 1.3 reshape.33.ln
  3.9 1.4 copy_bitcast_fusion
  5.3 2.0 fusion.3
  7.2 0.3 maximum_bitcast_fusion
  7.6 1.0 pad_maximum_fusion.refs_1_
  8.6 10.1 %rows.1 = (bf16[520,2048]{1,0:T(8,128)(2,1)}, bf16[520,2048]{1,0:T(8,128)(2,1)}) custom-call(bf16[1024,2048]{1,0:T(8,128)(2,1)} %bitcast.22, s32[6,1024]{1,0:T(8,128)} %get-tuple-element.17.idx, s32[6,1024]{1,0:T(8,128)} %get-tuple-element.16.slot, bf16[1,2048]{1,0:T(2,128)(2,1)} %reshape.33.ln, bf16[64,2048]{1,0:T(8,128)(2,1)} %bitcast.24), custom_call_target="tpu_custom_call" | custom-call | flops 268435456 | bytes 16777216 | tf_op jit(solution)/shard_map/rows/pallas_call | solution.py:884
  18.7 792.1 %layer.1 = (f32[3,1024,2048]{2,1,0:T(8,128)}, f32[1024,2048]{1,0:T(8,128)}, bf16[16,2,520,2048]{3,2,1,0:T(8,128)(2,1)}, bf16[16,2,520,2048]{3,2,1,0:T(8,128)(2,1...) custom-call(bf16[520,2048]{1,0:T(8,128)(2,1)} %get-tuple-element.9.p, ...), custom_call_target="tpu_custom_call" | custom-call | tf_op jit(solution)/shard_map/layer/pallas_call | solution.py:914
  810.8 14.3 %fusion.1 = bf16[1,1024,2048]{2,1,0:T(8,128)(2,1)} fusion(f32[1024,2048]{1,0:T(8,128)} %get-tuple-element.11, f32[3,1024,2048]{2,1,0:T(8,128)} %get-tuple-element.12), kind=kLoop, calls=%fused_computation.2 | loop fusion | flops 8388608 | bytes 37748736 | tf_op jit(solution)/shard_map/reshape | solution.py:965
  (1 shorter events, 0.0 us)

commit v6 on v5

--- a/solution.py
+++ b/solution.py
@@ -29,12 +29,16 @@
     half = HEAD // 2
     freq = 10000.0 ** (-jnp.arange(half, dtype=F32) / half)
     ang = jnp.arange(t, dtype=F32)[:, None] * freq[None, :]
-    c, s = jnp.cos(ang), jnp.sin(ang)
-    return jnp.stack([jnp.concatenate([c, c], axis=1), jnp.concatenate([-s, s], axis=1)])
+    return jnp.cos(ang), jnp.sin(ang)
 
 
 def _norm(xf, w):
     return (xf * lax.rsqrt(jnp.mean(xf * xf, axis=-1, keepdims=True) + EPS) * w).astype(BF16)
+
+
+def _weight(ln):
+    w = ln[...].astype(F32)
+    return jnp.concatenate([w[i:i + 1] for i in range(w.shape[0])], axis=1)
 
 
 def _dot(a, b):
@@ -85,7 +89,7 @@
     return b[0][:6], b[1][:6], b[2][:6] + b[3][:6] + lo
 
 
-def _k0(n, h0, idx, slot, ln, wr, out0, out1, hb, ub, eb, hsem, lsem, ssem, rsem):
+def _own_rows(n, h0, idx, slot, ln, wr, out0, out1, hb, ub, eb, hsem, lsem, ssem, rsem, barrier):
     side, me, x, y, c = _place(n)
     t = hb.shape[0]
     half, tile, ne = t // 2, t // 4, wr.shape[0]
@@ -100,9 +104,7 @@
             h_copy(o, i).start()
 
     other = me + 1 - 2 * c
-    barrier = pltpu.get_barrier_semaphore()
-    pl.semaphore_signal(barrier, device_id={'ep': other}, device_id_type=MESH)
-    pl.semaphore_wait(barrier, 1)
+    barrier()
 
     def gives(out):
         return [
@@ -116,7 +118,7 @@
             for j, (src, rows) in enumerate(((ub.at[1], pl.ds(0, half)), (eb.at[1], pl.ds(half, 8))))
         ]
 
-    w = ln[...].astype(F32)
+    w = _weight(ln)
     expert = lax.broadcasted_iota(jnp.int32, (ne, tile), 0)
     for o in BOTH:
         for i in BOTH:
@@ -244,7 +246,7 @@
         wait_kept(el)
 
 
-def _dense(h0, cs, ln1, wq, wk, wv, wo, ln2, ws1, ws3, ws2, z, hb, xb, wa, wf, wg, qb, kb, vb, ob, hs, ct, zs, hsem, asem, fsem, gsem, zsem, hook):
+def _dense(h0, cos, sin, wq, wk, wv, wo, ws1, ws3, ws2, lns, z, hb, xb, wa, wf, wg, qb, kb, vb, ob, hs, ct, zs, hsem, asem, fsem, gsem, zsem, hook):
     t, d = hb.shape
     wide, narrow = qb.shape[1], wf.shape[3]
     groups, chunks = d // wide, ws1.shape[1] // narrow
@@ -278,7 +280,8 @@
         pltpu.make_async_copy(ref, ref, sem).wait()
 
     pltpu.make_async_copy(h0, hb, hsem).start()
-    pltpu.make_async_copy(cs, ct, hsem).start()
+    for i, v in enumerate((cos, sin)):
+        pltpu.make_async_copy(v, ct.at[i], hsem).start()
     for load in (load_a, load_f, load_g):
         for i in BOTH:
             load(jnp.int32(i))
@@ -286,14 +289,14 @@
     wait(ct, hsem)
 
     def norm(ln):
-        w = ln[...].astype(F32)
+        w = _weight(ln)
 
         @loop(t // tile)
         def _(i):
             rows = pl.ds(pl.multiple_of(i * tile, tile), tile)
             xb[rows] = _norm(hb[rows].astype(F32), w)
 
-    norm(ln1)
+    norm(lns[0])
 
     @loop(groups)
     def _(g):
@@ -305,6 +308,7 @@
         def _(m):
             rows = pl.ds(pl.multiple_of(m * tall, tall), tall)
             c, s = ct[0, rows], ct[1, rows]
+            c, s = jnp.concatenate([c, c], axis=1), jnp.concatenate([-s, s], axis=1)
             for j, out in enumerate((qb, kb)):
                 v = _dot(xb[rows], wa[b, j])
                 for i in range(wide // HEAD):
@@ -354,7 +358,7 @@
 
         load_a(g + groups + 2)
 
-    norm(ln2)
+    norm(lns[1])
 
     @loop(chunks)
     def _(j):
@@ -415,7 +419,7 @@
         head,
         full,
         pltpu.VMEM((t, fs), BF16),
-        pltpu.VMEM((PAIR, t, HEAD), F32),
+        pltpu.VMEM((PAIR, t, HEAD // 2), F32),
         pltpu.VMEM((PAIR, t // 2, wide), F32),
     ]
 
@@ -540,11 +544,11 @@
         self.wait(self.out.at[pl.ds(0, chips - 1), 0], self.send_sem)
 
 
-def _k2(n, cap, keep, part0, part1, ue1, ue3, ue2, *refs):
-    dense_in, refs = refs[:11], refs[11:]
-    rxf, z, ug0, ug1, ys, r, rl, rx2, mr, *refs = refs
-    dense_sems, refs = refs[:5], refs[5:]
-    wsem, w2sem, usem, ysem, gsem, grsem, pairsem, osem, ssem, rsem, relsem, fsem, lsem, msem, bsem, r2sem, rfsem = refs
+def _k2(n, cap, keep, idx, slot, ln_moe, ln_attn, ln_ffn, wr, ue1, ue3, ue2, *refs):
+    dense_in, refs = refs[:10], refs[10:]
+    rxf, z, zx, part0, part1, ug0, ug1, ys, r, rl, rx2, mr, *refs = refs
+    row_sems, dense_sems, refs = refs[:4], refs[4:9], refs[9:]
+    wsem, w2sem, usem, ysem, gsem, grsem, pairsem, osem, ssem, rsem, relsem, fsem, lsem, msem, bsem, r2sem, rfsem, zsem, zbsem = refs
     side, me, x, y, c = _place(n)
     t, d = rxf.shape[1], rxf.shape[2]
     f = ue1.shape[2]
@@ -567,19 +571,22 @@
         for off in range(side):
             pltpu.make_async_copy(ug.at[device(axis, off, 0) // CORES, :, pl.ds(th, 8)], mr.at[p, off], msem).start()
 
+    def barrier():
+        here = pltpu.get_barrier_semaphore()
+        peers = 0
+        for off in range(side):
+            for dc in range(CORES):
+                for axis in BOTH:
+                    if off or (dc and not axis):
+                        pl.semaphore_signal(here, device_id={'ep': device(axis, off, (c + dc) % CORES)}, device_id_type=MESH)
+                        peers += 1
+        pl.semaphore_wait(here, peers)
+
+    def rows_phase(*refs):
+        _own_rows(n, dense_in[0], idx, slot, ln_moe, wr, part0, part1, *refs, *row_sems, barrier)
+
+    pl.run_scoped(rows_phase, pltpu.VMEM((t, d), BF16), pltpu.VMEM((PAIR, th, d), BF16), pltpu.VMEM((PAIR, 8, d), BF16))
     kept = [pltpu.make_async_copy(part, ug.at[me // CORES, c], osem.at[p]) for p, (part, ug) in enumerate(((part0, ug0), (part1, ug1)))]
-    for cp in kept:
-        cp.start()
-
-    barrier = pltpu.get_barrier_semaphore()
-    peers = 0
-    for off in range(side):
-        for dc in range(CORES):
-            for axis in BOTH:
-                if off or (dc and not axis):
-                    pl.semaphore_signal(barrier, device_id={'ep': device(axis, off, (c + dc) % CORES)}, device_id_type=MESH)
-                    peers += 1
-    pl.semaphore_wait(barrier, peers)
 
     def send(p, k, want_far):
         for i in BOTH:
@@ -624,6 +631,8 @@
 
     first, second = gathers
     first.start()
+    for cp in kept:
+        cp.start()
 
     def hook(name, i):
         if name == 'group':
@@ -642,9 +651,11 @@
             first.across((-1, 1))
 
     def dense_phase(*refs):
-        _dense(*dense_in, z, *refs, *dense_sems, hook=hook)
-
-    pl.run_scoped(dense_phase, *_dense_scratch(t, d, dense_in[8].shape[1]))
+        _dense(*dense_in, (ln_attn, ln_ffn), z, *refs, *dense_sems, hook=hook)
+
+    pl.run_scoped(dense_phase, *_dense_scratch(t, d, dense_in[7].shape[1]))
+    z_given = remote(z.at[:, pl.ds(dh, dh)], zx, zsem.at[0], zsem.at[1], device(0, 0, 1 - c))
+    z_given.start()
     first.last((0,))
     first.across((2,))
     second.start()
@@ -721,7 +732,14 @@
         off = first * far + middle * (1 + (side - 2) * b)
         return p, (c + p) % 2, off, b + middle * (q % 2) * (1 - 2 * b)
 
-    def combine_phase(rb, mt, pma, pmb, sb):
+    def combine_phase(rb, mt, pma, pmb, sb, zb):
+        def load_z(axis, m, i):
+            rows = pl.ds(pl.multiple_of(m * tile, tile), tile)
+            for j, src in enumerate((z.at[rows, pl.ds(0, dh)], zx.at[rows])):
+                @pl.when(axis == j)
+                def _():
+                    pltpu.make_async_copy(src, zb.at[i], zbsem.at[i]).start()
+
         def load(w):
             p, axis, off, _ = role(w)
             line = (x * (1 - axis) + y * axis + off) % side
@@ -832,6 +850,11 @@
             def _():
                 wait_sent(w % keep)
 
+            @pl.when(off == 0)
+            def _():
+                for i in BOTH:
+                    load_z(axis, mh * 2 + i, i)
+
             for i, pm in ((0, pma), (1, pmb)):
                 here = w % keep * 2 + i
                 wide = min(512, dh)
@@ -851,11 +874,17 @@
                         pltpu.make_async_copy(got, got, r2sem.at[p, way, i]).wait()
                         sb[here] = sb[here] + rx2[p, way, i]
 
+                @pl.when(off == 0)
+                def _():
+                    pltpu.make_async_copy(zb.at[i], zb.at[i], zbsem.at[i]).wait()
+                    sb[here] = sb[here] + zb[i]
+
                 send_sum(w, i)
 
         for w in range(units - keep, units):
             wait_sent(w % keep)
 
+    z_given.wait()
     pl.run_scoped(
         combine_phase,
         pltpu.VMEM((PAIR, kk, dh), BF16),
@@ -863,6 +892,7 @@
         pltpu.VMEM((3 * tile, kk), BF16),
         pltpu.VMEM((3 * tile, kk), BF16),
         pltpu.VMEM((keep * 2, tile, dh), F32),
+        pltpu.VMEM((PAIR, tile, dh), F32),
     )
 
     for gather in gathers:
@@ -878,31 +908,8 @@
 ANY = pl.BlockSpec(memory_space=pl.ANY)
 
 
-def _rows(h0, idx, slot, ln, wr, n):
-    t, d = h0.shape
-    vmem = pl.BlockSpec(memory_space=pltpu.VMEM)
-    return pl.pallas_call(
-        functools.partial(_k0, n),
-        out_shape=(jax.ShapeDtypeStruct((t // 2 + 8, d), BF16),) * CORES,
-        in_specs=[ANY] + [vmem] * 4,
-        out_specs=(ANY,) * CORES,
-        scratch_shapes=[
-            pltpu.VMEM((t, d), BF16),
-            pltpu.VMEM((PAIR, t // 2, d), BF16),
-            pltpu.VMEM((PAIR, 8, d), BF16),
-            SEM4,
-            SEM2,
-            SEM2,
-            SEM2,
-        ],
-        cost_estimate=pl.CostEstimate(flops=2 * t * d * 64, bytes_accessed=8 * t * d, transcendentals=0),
-        compiler_params=pltpu.CompilerParams(collective_id=1, has_side_effects=True),
-        name='rows',
-    )(h0, idx, slot, ln, wr)
-
-
-def _layer(parts, experts, dense, n, cap, t):
-    d, f, fs = parts[0].shape[-1], experts[0].shape[-1], dense[8].shape[-1]
+def _layer(routing, experts, dense, n, cap):
+    (t, d), f, fs = dense[0].shape, experts[0].shape[-1], dense[7].shape[-1]
     dh = d // 2
     side = math.isqrt(n // CORES)
     tile = t // 4
@@ -910,23 +917,32 @@
     keep = 4
     cap2 = 2 * cap
     vmem = pl.BlockSpec(memory_space=pltpu.VMEM)
-    gathered = jax.ShapeDtypeStruct((n // CORES, CORES) + parts[0].shape, BF16)
+    part = jax.ShapeDtypeStruct((t // 2 + 8, d), BF16)
+    gathered = jax.ShapeDtypeStruct((n // CORES, CORES) + part.shape, BF16)
+    outs = (
+        jax.ShapeDtypeStruct((3, t, d), F32),
+        jax.ShapeDtypeStruct((t, d), F32),
+        jax.ShapeDtypeStruct((t, dh), F32),
+        part,
+        part,
+        gathered,
+        gathered,
+        jax.ShapeDtypeStruct((PAIR, PAIR * STEPS, PAIR, cap2, dh), BF16),
+        jax.ShapeDtypeStruct((PAIR, side, kk, dh), BF16),
+        jax.ShapeDtypeStruct((PAIR, PAIR, PAIR, side, cap, dh), BF16),
+    )
     return pl.pallas_call(
         functools.partial(_k2, n, cap, keep),
-        out_shape=(
-            jax.ShapeDtypeStruct((3, t, d), F32),
-            jax.ShapeDtypeStruct((t, d), F32),
-            gathered,
-            gathered,
-            jax.ShapeDtypeStruct((PAIR, PAIR * STEPS, PAIR, cap2, dh), BF16),
-            jax.ShapeDtypeStruct((PAIR, side, kk, dh), BF16),
-            jax.ShapeDtypeStruct((PAIR, PAIR, PAIR, side, cap, dh), BF16),
-        ),
-        in_specs=[ANY] * 7 + [vmem, ANY, ANY, ANY, ANY, vmem, ANY, ANY, ANY],
-        out_specs=(ANY,) * 7,
+        out_shape=outs,
+        in_specs=[vmem] * len(routing) + [ANY] * (len(experts) + len(dense)),
+        out_specs=(ANY,) * len(outs),
         scratch_shapes=[
             pltpu.VMEM((PAIR, PAIR, PAIR, tile, dh), F32),
-            pltpu.VMEM((PAIR, side, 2, 8, d), BF16),
+            pltpu.VMEM((PAIR, side, PAIR, 8, d), BF16),
+            SEM4,
+            SEM2,
+            SEM2,
+            SEM2,
         ] + DENSE_SEMS + FFN_SEMS + [
             SEM2,
             SEM((PAIR, PAIR, 5, 4)),
@@ -941,10 +957,29 @@
             SEM((keep,)),
             SEM((PAIR, PAIR, PAIR)),
             SEM((3,)),
+            SEM2,
+            SEM2,
         ],
         compiler_params=pltpu.CompilerParams(collective_id=0, has_side_effects=True, vmem_limit_bytes=67043328),
         name='layer',
-    )(*parts, *experts, *dense)[:2]
+    )(*routing, *experts, *dense)[0]
+
+
+def _add(r, out):
+    out[...] = (r[0] + r[1] + r[2]).astype(BF16)
+
+
+def _total(r):
+    ways, t, d = r.shape
+    tile = t // 8
+    return pl.pallas_call(
+        _add,
+        grid=(t // tile,),
+        out_shape=jax.ShapeDtypeStruct((t, d), BF16),
+        in_specs=[pl.BlockSpec((ways, tile, d), lambda i: (0, i, 0))],
+        out_specs=pl.BlockSpec((tile, d), lambda i: (i, 0)),
+        name='total',
+    )(r)
 
 
 def solution(mesh):
@@ -958,11 +993,9 @@
         ne = ue1.shape[0] * n
         t = b * s
         cap = CAP_FACTOR * t * top // ne
-        parts = _rows(h0.reshape(t, d), idx.reshape(t, top).T, slot.reshape(t, top).T, ln_moe.reshape(1, d), wr.T, n)
-        flat = h0.reshape(t, d)
-        dense = (flat, _turns(t), ln_attn.reshape(1, d), wq, wk, wv, wo, ln_ffn.reshape(1, d), ws1, ws3, ws2)
-        r, z = _layer(parts, (ue1, ue3, ue2), dense, n, cap, t)
-        return (z + (r[0] + r[1] + r[2])).astype(BF16).reshape(b, s, d)
+        routing = (idx.reshape(t, top).T, slot.reshape(t, top).T, *(v.reshape(d // LANES, LANES) for v in (ln_moe, ln_attn, ln_ffn)), wr.T)
+        dense = (h0.reshape(t, d), *_turns(t), wq, wk, wv, wo, ws1, ws3, ws2)
+        return _total(_layer(routing, (ue1, ue3, ue2), dense, n, cap)).reshape(b, s, d)
 
     specs = (rows, rows, rows) + (rep,) * 11 + (P('ep'), P('ep'), P('ep'))
     return jax.shard_map(local, mesh=mesh, in_specs=specs, out_specs=rows, check_vma=False)

time: 825 us -> 818 us (level)
  other arithmetic: 17.6 us -> 2.81 us
  Pallas kernels: 802 us -> 813 us
    reshape x1 -> x0, other arithmetic: 14.3 us -> none  [local(): return (z + (r[0] + r[1] + r[2])).astype(BF16).reshape(b, s, d)]
    pallas_call x2, Pallas kernels: 802 us -> 813 us  [the longest x1 802 us: _layer(): pl.pallas_call(functools.partial(_k2, n, cap, keep), out_shape=outs, in_s...]
where the time goes in v6:
time: 818 us; the launch traced here: 817 us
  Pallas kernels  813 us (99%)
    pallas_call x1, Pallas kernels, _layer(): pl.pallas_call(functools.partial(_k2, n, cap, keep), out_shape=outs, in_s...  802 us

profile of v6, /device:TPU:97, one launch (start us, length us, event | category | flops | bytes accessed | tf_op | source)
XLA Modules:
  0.0 817.5 jit_solution(10939911749838552008)
XLA Ops:
  0.0 1.4 copy_bitcast_fusion
  1.4 2.8 fusion
  4.2 801.9 %layer.1 = (f32[3,1024,2048]{2,1,0:T(8,128)}, f32[1024,2048]{1,0:T(8,128)}, f32[1024,1024]{1,0:T(8,128)}, bf16[520,2048]{1,0:T(8,128)(2,1)}, bf16[520,2048]{1,0:...) custom-call(s32[6,1024]{1,0:T(8,128)} %get-tuple-element.10.idx, ...), custom_call_target="tpu_custom_call" | custom-call | tf_op jit(solution)/shard_map/layer/pallas_call | solution.py:934
  806.1 11.4 %total.1 = bf16[1024,2048]{1,0:T(8,128)(2,1)} custom-call(f32[3,1024,2048]{2,1,0:T(8,128)} %get-tuple-element.6.r), custom_call_target="tpu_custom_call" | custom-call | tf_op jit(solution)/shard_map/total/pallas_call | solution.py:975
  (1 shorter events, 0.0 us)

commit v7 on v6

--- a/solution.py
+++ b/solution.py
@@ -25,11 +25,15 @@
 SEM2, SEM4 = SEM((2,)), SEM((4,))
 
 
+FINE = 32
+
+
 def _turns(t):
     half = HEAD // 2
     freq = 10000.0 ** (-jnp.arange(half, dtype=F32) / half)
-    ang = jnp.arange(t, dtype=F32)[:, None] * freq[None, :]
-    return jnp.cos(ang), jnp.sin(ang)
+    pos = jnp.concatenate([FINE * jnp.arange(t // FINE, dtype=F32), jnp.arange(FINE, dtype=F32)])
+    ang = pos[:, None] * freq[None, :]
+    return jnp.stack([jnp.cos(ang), jnp.sin(ang)])
 
 
 def _norm(xf, w):
@@ -104,7 +108,7 @@
             h_copy(o, i).start()
 
     other = me + 1 - 2 * c
-    barrier()
+    ready = barrier()
 
     def gives(out):
         return [
@@ -128,18 +132,20 @@
             ub[o, pl.ds(i * tile, tile)] = u
             lg = lax.dot_general(wr[...], u, NT, preferred_element_type=F32)
             cols = pl.ds(pl.multiple_of((order[o] * 2 + i) * tile, tile), tile)
-            ex, sl = idx[:, cols], slot[:, cols]
-            pick = [jnp.sum(jnp.where(expert == ex[j:j + 1], lg, 0.0), axis=0, keepdims=True) for j in range(6)]
+            ex, sl = ([v[j, :, cols] for j in range(v.shape[0])] for v in (idx, slot))
+            pick = [jnp.sum(jnp.where(expert == v, lg, 0.0), axis=0, keepdims=True) for v in ex]
             top = functools.reduce(jnp.maximum, pick)
             e = [jnp.exp(v - top) for v in pick]
             total = functools.reduce(jnp.add, e)
             parts = [_parts(v / total) for v in e]
             hi, mid, lo = ([p[q].astype(F32) for p in parts] for q in range(3))
-            exf, slf = ex.astype(F32), sl.astype(F32)
+            exf, slf = ([v.astype(F32) for v in rows] for rows in (ex, sl))
             zero = jnp.zeros((1, tile), F32)
-            blocks = ([exf] + lo[:2], [slf] + lo[2:4], hi + lo[4:], mid + [zero, zero])
+            blocks = (exf + lo[:2], slf + lo[2:4], hi + lo[4:], mid + [zero, zero])
             for q, rows in enumerate(blocks):
                 eb[o, :, pl.ds(q * half + i * tile, tile)] = jnp.concatenate(rows).astype(BF16)
+        if o == 0:
+            ready()
         for p, out in enumerate((out0, out1)):
             @pl.when(c == p)
             def _():
@@ -246,7 +252,7 @@
         wait_kept(el)
 
 
-def _dense(h0, cos, sin, wq, wk, wv, wo, ws1, ws3, ws2, lns, z, hb, xb, wa, wf, wg, qb, kb, vb, ob, hs, ct, zs, hsem, asem, fsem, gsem, zsem, hook):
+def _dense(h0, wq, wk, wv, wo, ws1, ws3, ws2, lns, turns, z, hb, xb, wa, wf, wg, qb, kb, vb, ob, hs, ct, zs, hsem, asem, fsem, gsem, zsem, hook):
     t, d = hb.shape
     wide, narrow = qb.shape[1], wf.shape[3]
     groups, chunks = d // wide, ws1.shape[1] // narrow
@@ -280,13 +286,20 @@
         pltpu.make_async_copy(ref, ref, sem).wait()
 
     pltpu.make_async_copy(h0, hb, hsem).start()
-    for i, v in enumerate((cos, sin)):
-        pltpu.make_async_copy(v, ct.at[i], hsem).start()
     for load in (load_a, load_f, load_g):
         for i in BOTH:
             load(jnp.int32(i))
+    coarse = t // FINE
+
+    @loop(coarse)
+    def _(i):
+        c1, s1 = (turns[j, pl.ds(i, 1)] for j in BOTH)
+        c2, s2 = (turns[j, pl.ds(coarse, FINE)] for j in BOTH)
+        rows = pl.ds(pl.multiple_of(i * FINE, FINE), FINE)
+        ct[0, rows] = c1 * c2 - s1 * s2
+        ct[1, rows] = s1 * c2 + c1 * s2
+
     wait(hb, hsem)
-    wait(ct, hsem)
 
     def norm(ln):
         w = _weight(ln)
@@ -544,8 +557,8 @@
         self.wait(self.out.at[pl.ds(0, chips - 1), 0], self.send_sem)
 
 
-def _k2(n, cap, keep, idx, slot, ln_moe, ln_attn, ln_ffn, wr, ue1, ue3, ue2, *refs):
-    dense_in, refs = refs[:10], refs[10:]
+def _k2(n, cap, keep, idx, slot, ln_moe, ln_attn, ln_ffn, turns, wr, ue1, ue3, ue2, *refs):
+    dense_in, refs = refs[:8], refs[8:]
     rxf, z, zx, part0, part1, ug0, ug1, ys, r, rl, rx2, mr, *refs = refs
     row_sems, dense_sems, refs = refs[:4], refs[4:9], refs[9:]
     wsem, w2sem, usem, ysem, gsem, grsem, pairsem, osem, ssem, rsem, relsem, fsem, lsem, msem, bsem, r2sem, rfsem, zsem, zbsem = refs
@@ -580,7 +593,7 @@
                     if off or (dc and not axis):
                         pl.semaphore_signal(here, device_id={'ep': device(axis, off, (c + dc) % CORES)}, device_id_type=MESH)
                         peers += 1
-        pl.semaphore_wait(here, peers)
+        return functools.partial(pl.semaphore_wait, here, peers)
 
     def rows_phase(*refs):
         _own_rows(n, dense_in[0], idx, slot, ln_moe, wr, part0, part1, *refs, *row_sems, barrier)
@@ -651,9 +664,9 @@
             first.across((-1, 1))
 
     def dense_phase(*refs):
-        _dense(*dense_in, (ln_attn, ln_ffn), z, *refs, *dense_sems, hook=hook)
-
-    pl.run_scoped(dense_phase, *_dense_scratch(t, d, dense_in[7].shape[1]))
+        _dense(*dense_in, (ln_attn, ln_ffn), turns, z, *refs, *dense_sems, hook=hook)
+
+    pl.run_scoped(dense_phase, *_dense_scratch(t, d, dense_in[5].shape[1]))
     z_given = remote(z.at[:, pl.ds(dh, dh)], zx, zsem.at[0], zsem.at[1], device(0, 0, 1 - c))
     z_given.start()
     first.last((0,))
@@ -909,7 +922,7 @@
 
 
 def _layer(routing, experts, dense, n, cap):
-    (t, d), f, fs = dense[0].shape, experts[0].shape[-1], dense[7].shape[-1]
+    (t, d), f, fs = dense[0].shape, experts[0].shape[-1], dense[5].shape[-1]
     dh = d // 2
     side = math.isqrt(n // CORES)
     tile = t // 4
@@ -971,7 +984,7 @@
 
 def _total(r):
     ways, t, d = r.shape
-    tile = t // 8
+    tile = t // 16
     return pl.pallas_call(
         _add,
         grid=(t // tile,),
@@ -993,8 +1006,8 @@
         ne = ue1.shape[0] * n
         t = b * s
         cap = CAP_FACTOR * t * top // ne
-        routing = (idx.reshape(t, top).T, slot.reshape(t, top).T, *(v.reshape(d // LANES, LANES) for v in (ln_moe, ln_attn, ln_ffn)), wr.T)
-        dense = (h0.reshape(t, d), *_turns(t), wq, wk, wv, wo, ws1, ws3, ws2)
+        routing = (*(jnp.moveaxis(v, -1, 0) for v in (idx, slot)), *(v.reshape(d // LANES, LANES) for v in (ln_moe, ln_attn, ln_ffn)), _turns(t), wr.T)
+        dense = (h0.reshape(t, d), wq, wk, wv, wo, ws1, ws3, ws2)
         return _total(_layer(routing, (ue1, ue3, ue2), dense, n, cap)).reshape(b, s, d)
 
     specs = (rows, rows, rows) + (rep,) * 11 + (P('ep'), P('ep'), P('ep'))

time: 818 us -> 816 us (level)
  no operation moved by 1% of the time
where the time goes in v7:
time: 816 us
  Pallas kernels  815 us (100%)
    pallas_call x1, Pallas kernels, _layer(): pl.pallas_call(functools.partial(_k2, n, cap, keep), out_shape=outs, in_s...  800 us

profile of v7, /device:TPU:97, one launch (start us, length us, event | category | flops | bytes accessed | tf_op | source)
XLA Modules:
  0.0 815.9 jit_solution(11777245137842010894)
XLA Ops:
  0.0 0.1 pad_maximum_fusion.1
  0.1 0.2 multiply_cosine_fusion
  0.3 0.6 pad_maximum_fusion.turns
  0.9 799.8 %layer.1 = (f32[3,1024,2048]{2,1,0:T(8,128)}, f32[1024,2048]{1,0:T(8,128)}, f32[1024,1024]{1,0:T(8,128)}, bf16[520,2048]{1,0:T(8,128)(2,1)}, bf16[520,2048]{1,0:...) custom-call(s32[6,1,1024]{2,1,0:T(1,128)} %bitcast.10, ...), custom_call_target="tpu_custom_call" | custom-call | tf_op jit(solution)/shard_map/layer/pallas_call | solution.py:947
  800.7 15.2 %total.1 = bf16[1024,2048]{1,0:T(8,128)(2,1)} custom-call(f32[3,1024,2048]{2,1,0:T(8,128)} %get-tuple-element.6.r), custom_call_target="tpu_custom_call" | custom-call | tf_op jit(solution)/shard_map/total/pallas_call | solution.py:988
  (2 shorter events, 0.0 us)
